TPU v7x, 128 devices: a whole 4x4x4 slice. The times are simulated.
128 devices in a mesh: vocab: 64 (over y, z, x), dp: 2 (over core).
Axes of the slice: x: 4, y: 4, z: 4, core: 2. Of those that a mesh axis runs over, the one named last changes fastest.
Arguments:
- hidden: bfloat16 [2048, 4096], P('dp', 'vocab'), may hold values from -64 to 64
- head_weight: bfloat16 [65536, 4096], P('vocab'), may hold values from -0.28125 to 0.28125
- targets: int32 [2048], P('dp'), may hold values from 0 to 65535
- loss_cot: float32 [2048], P('dp'), may hold values from -40 to 40
Outputs:
- tok_loss: float32 [2048], P('dp')
- hidden_grad: bfloat16 [2048, 4096], P('dp', 'vocab')
- g_factor: float32 [65536, 1024], P(('vocab', 'dp'))
- a_factor: float32 [4096, 4096], P('vocab')
All inputs are finite; a program needn't handle non-finite values.
Results may differ from a plain program's by a relative error of at most 0.0049.
Values may be sent and summed in bfloat16 or wider, within the bound.
No kernel may reach another device: no remote copies, remote signals or barrier semaphores. Data moves between devices by JAX's collectives and lax.ppermute only.
A program may use at most 128 MiB of HBM per device.

v0:
```python
import jax
import jax.numpy as jnp
import numpy as np
from jax import lax
from jax.experimental import pallas as pl
from jax.experimental.pallas import tpu as pltpu
from jax.sharding import Mesh
from jax.sharding import PartitionSpec as P

TOK_DEV = 1024
VOCAB = ("vocab_0", "vocab_1", "vocab_2")
ALL = ("vocab_0", "vocab_1", "vocab_2", "dp")

SMALL = (((0, 1), (2, 3)), ((0, 3), (1, 2)))
LARGE = (((1, 2), (0, 3)), ((0, 1), (3, 2)))
SWAP = [(0, 1), (1, 0)]
F32 = jnp.float32
BF16 = jnp.bfloat16

GROUPS = (
    ((0, 64, 0), (1, 64, 0), (2, 48, 0)),
    ((2, 16, 48), (3, 64, 0), (4, 64, 0), (5, 32, 0)),
    ((5, 32, 32), (6, 64, 0), (7, 64, 0)),
)
SIZES = [sum(rows for _, rows, _ in group) for group in GROUPS]
STARTS = [0, SIZES[0], SIZES[0] + SIZES[1]]


def device(y, z, x, core):
    return ((y * 4 + z) * 4 + x) * 2 + core


def small_cubes():
    return [
        [device(y, z, x, core) for y in a for z in b for x in c]
        for core in (0, 1) for a in SMALL[core] for b in SMALL[core] for c in SMALL[core]
    ]


def partner(core, c):
    return next(p[1 - p.index(c)] for p in LARGE[core] if c in p)


def spots():
    return [(y, z, x, core) for y in range(4) for z in range(4) for x in range(4) for core in (0, 1)]


def large_pairs(axis):
    out = []
    for at in spots():
        to = list(at)
        to[axis] = partner(at[3], at[axis])
        out.append((device(*at), device(*to)))
    return out


def chip_table():
    table = np.zeros((128, 3, 8, 8), np.int32)
    for at in spots():
        core = at[3]
        for group in range(3):
            for l in range(8):
                for s in range(8):
                    chip = 0
                    for axis in range(3):
                        c = at[axis]
                        if l >> ((axis - group) % 3) & 1:
                            c = partner(core, c)
                        pair = next(p for p in SMALL[core] if c in p)
                        chip = chip * 4 + pair[s >> (2 - axis) & 1]
                    table[device(*at), group, l, s] = chip
    return table.reshape(128, 192)


SMALL_CUBES = small_cubes()
LARGE_PAIRS = [large_pairs(axis) for axis in range(3)]
CHIPS = chip_table()


def small_stage(x):
    return lax.all_to_all(x, ALL, 0, 0, axis_index_groups=SMALL_CUBES, tiled=True)


def gathered_groups(some):
    held = [some[start : start + size] for start, size in zip(STARTS, SIZES)]
    got = [lax.ppermute(held[g], ALL, LARGE_PAIRS[g]) for g in range(3)]
    first = [jnp.concatenate([h, r]) for h, r in zip(held, got)]
    second = [lax.ppermute(first[g], ALL, LARGE_PAIRS[(g + 1) % 3]) for g in range(3)]
    third = [
        [lax.ppermute(part, ALL, LARGE_PAIRS[(g + 2) % 3]) for part in (first[g], second[g])]
        for g in range(3)
    ]
    return [[first[g], second[g], *third[g]] for g in range(3)]


def add_up(*terms):
    total = terms[0].astype(F32)
    for term in terms[1:]:
        total = total + term.astype(F32)
    return total.astype(BF16)


def summed_groups(sends, keeps):
    trade = lambda x, g, step: lax.ppermute(x, ALL, LARGE_PAIRS[(g + step) % 3])
    far = [trade(sends[g], g, 2) for g in range(3)]
    mid = [trade(add_up(keeps[g][2:], far[g][2:]), g, 1) for g in range(3)]
    near = [trade(add_up(keeps[g][1], far[g][1], mid[g][1]), g, 0) for g in range(3)]
    return jnp.concatenate(
        [add_up(keeps[g][0], far[g][0], mid[g][0], near[g]) for g in range(3)]
    )


def gather_copies(chips, got, h):
    quarters = []
    for large in (0, 1):
        for small in (0, 1):
            copies = []
            for g, group in enumerate(GROUPS):
                for l in range(8):
                    if l >> (-g % 3) & 1 != large:
                        continue
                    src, at = got[4 * g + l // 2], (l % 2) * SIZES[g]
                    for s, count, first in group:
                        if s >> 2 == small:
                            dst = pl.multiple_of(chips[64 * g + 8 * l + s] * 64 + first, 16)
                            copies.append((src.at[pl.ds(at, count)], h.at[pl.ds(dst, count)]))
                        at += count
            quarters.append((chips[8 * large + 4 * small] // 16, copies))
    return quarters


def a_kernel(chips, *refs):
    got, (own, out, h, sem) = refs[:12], refs[12:]
    for _, copies in gather_copies(chips, got, h):
        for src, dst in copies:
            pltpu.make_async_copy(src, dst, sem).start()
    pltpu.make_async_copy(h, h, sem).wait()
    out[...] = lax.dot_general(
        own[...], h[...], (((1,), (1,)), ((), ())), preferred_element_type=F32
    )


def a_part_of(chips, got, own):
    feats, tokens = own.shape
    width = 64 * feats
    return pl.pallas_call(
        a_kernel,
        grid_spec=pltpu.PrefetchScalarGridSpec(
            num_scalar_prefetch=1,
            grid=(),
            in_specs=[pl.BlockSpec(memory_space=pl.ANY)] * len(got)
            + [pl.BlockSpec(memory_space=pltpu.VMEM)],
            out_specs=pl.BlockSpec(memory_space=pltpu.VMEM),
            scratch_shapes=[pltpu.VMEM((width, tokens), BF16), pltpu.SemaphoreType.DMA],
        ),
        out_shape=jax.ShapeDtypeStruct((feats, width), F32),
        compiler_params=pltpu.CompilerParams(vmem_limit_bytes=32 << 20),
        cost_estimate=pl.CostEstimate(
            flops=2 * feats * width * tokens, bytes_accessed=2 * width * tokens, transcendentals=0
        ),
    )(chips, *got, own)


def turn_kernel(chips, w, wide, tall, turned):
    step = pl.program_id(0)
    size = w.shape[1]

    @pl.when(step < 8)
    def _():
        turned[pl.ds(pl.multiple_of(step * size, size), size)] = w[...].T

    @pl.when(step >= 8)
    def _():
        pieces = []
        for g, group in enumerate(GROUPS):
            for s, count, first in group:
                at = pl.multiple_of(chips[64 * g + 8 * (step - 8) + s] * 64 + first, 16)
                pieces.append(turned[pl.ds(at, count)])
        rows = jnp.concatenate(pieces, axis=0)
        tall[...] = rows
        wide[...] = rows.T


def turned_weights(chips, w):
    vocab_rows, width = w.shape
    size = width // 8
    late = lambda i: jnp.maximum(i - 8, 0)
    return pl.pallas_call(
        turn_kernel,
        grid_spec=pltpu.PrefetchScalarGridSpec(
            num_scalar_prefetch=1,
            grid=(16,),
            in_specs=[pl.BlockSpec((vocab_rows, size), lambda i, t: (0, jnp.minimum(i, 7)))],
            out_specs=[
                pl.BlockSpec((vocab_rows, size), lambda i, t: (0, late(i))),
                pl.BlockSpec((size, vocab_rows), lambda i, t: (late(i), 0)),
            ],
            scratch_shapes=[pltpu.VMEM((width, vocab_rows), BF16)],
        ),
        out_shape=[pltpu.HBM((vocab_rows, width), BF16), pltpu.HBM((width, vocab_rows), BF16)],
        compiler_params=pltpu.CompilerParams(
            dimension_semantics=("arbitrary",), vmem_limit_bytes=32 << 20
        ),
        cost_estimate=pl.CostEstimate(
            flops=2048 * vocab_rows * width, bytes_accessed=6 * vocab_rows * width, transcendentals=0
        ),
    )(chips, w)


def half_copies(got, h):
    size = sum(SIZES)
    for g in range(3):
        for l in range(4):
            src = got[2 * g + l // 2].at[pl.ds((l % 2) * SIZES[g], SIZES[g])]
            yield src, h.at[pl.ds(l * size + STARTS[g], SIZES[g])]


def early_kernel(*refs):
    got, (w, part, h, sem) = refs[:6], refs[6:]

    @pl.when(pl.program_id(0) == 0)
    def _():
        for src, dst in half_copies(got, h):
            pltpu.make_async_copy(src, dst, sem).start()
        pltpu.make_async_copy(h, h, sem).wait()

    part[...] = jnp.dot(w[...], h[...], preferred_element_type=F32)


def late_kernel(*refs):
    got, (w, part, tgt, logits, stats, h, top, total, hit, sem) = refs[:6], refs[6:]
    step = pl.program_id(0)
    rows, tokens = logits.shape

    @pl.when(step == 0)
    def _():
        for src, dst in half_copies(got, h):
            pltpu.make_async_copy(src, dst, sem).start()
        top[...] = jnp.full(top.shape, -jnp.inf, F32)
        total[...] = jnp.zeros(total.shape, F32)
        hit[...] = jnp.zeros(hit.shape, F32)
        pltpu.make_async_copy(h, h, sem).wait()

    block = part[...] + jnp.dot(w[...], h[...], preferred_element_type=F32)
    logits[...] = block
    at = lax.broadcasted_iota(jnp.int32, block.shape, 0) + step * rows
    hit[...] += jnp.sum(jnp.where(at == tgt[...], block, F32(0.0)), axis=0, keepdims=True)
    now = jnp.maximum(top[...], jnp.max(block, axis=0, keepdims=True))
    added = jnp.sum(jnp.exp(block - now), axis=0, keepdims=True)
    total[...] = total[...] * jnp.exp(top[...] - now) + added
    top[...] = now

    @pl.when(step == pl.num_programs(0) - 1)
    def _():
        lse = top[...] + jnp.log(total[...])
        both = [r[:, k : k + 128] for r in (lse, hit[...]) for k in range(0, tokens, 128)]
        stats[...] = jnp.broadcast_to(jnp.concatenate(both, axis=0)[None], stats.shape)


LOGIT_ROWS = 256


def half_logits(half, got, wide, part=None, tgt=None):
    vocab_rows, width = wide.shape
    tokens = got[0].shape[1]
    rows, lines = LOGIT_ROWS, 2 * tokens // 128
    block = pl.BlockSpec((rows, tokens), lambda i: (i, 0))
    row = pl.BlockSpec((1, tokens), lambda i: (0, 0))
    late = part is not None
    return pl.pallas_call(
        late_kernel if late else early_kernel,
        grid=(vocab_rows // rows,),
        in_specs=[pl.BlockSpec(memory_space=pl.ANY)] * len(got)
        + [pl.BlockSpec((rows, width // 2), lambda i: (i, half))]
        + ([block, row] if late else []),
        out_specs=[block, pl.BlockSpec((64, lines, 128), lambda i: (0, 0, 0))] if late else block,
        out_shape=[
            pltpu.HBM((vocab_rows, tokens), F32), jax.ShapeDtypeStruct((64, lines, 128), F32),
        ] if late else pltpu.HBM((vocab_rows, tokens), F32),
        scratch_shapes=[pltpu.VMEM((width // 2, tokens), BF16)]
        + [pltpu.VMEM((1, tokens), F32)] * (3 if late else 0)
        + [pltpu.SemaphoreType.DMA],
        compiler_params=pltpu.CompilerParams(
            dimension_semantics=("arbitrary",), vmem_limit_bytes=32 << 20
        ),
        cost_estimate=pl.CostEstimate(
            flops=vocab_rows * width * tokens,
            bytes_accessed=width * (vocab_rows + tokens) + 4 * vocab_rows * tokens,
            transcendentals=vocab_rows * tokens,
        ),
    )(*got, wide, *([part, tgt] if late else []))


def signal_kernel(stats, logits, cot, tgt, grad, loss, row):
    step = pl.program_id(0)
    rows, tokens = logits.shape
    lines = tokens // 128

    @pl.when(step == 0)
    def _():
        lse = stats[:, :lines]
        top = jnp.max(lse, axis=0)
        full = top + jnp.log(jnp.sum(jnp.exp(lse - top[None]), axis=0))
        tok = full - jnp.sum(stats[:, lines:], axis=0)
        row[...] = jnp.concatenate([full[k : k + 1] for k in range(lines)], axis=1)
        loss[...] = jnp.concatenate([tok[k : k + 1] for k in range(lines)], axis=1)

    block = logits[...]
    at = lax.broadcasted_iota(jnp.int32, block.shape, 0) + step * rows
    one = jnp.where(at == tgt[...], F32(1.0), F32(0.0))
    grad[...] = (cot[...] * (jnp.exp(block - row[...]) - one)).astype(BF16)


def signal_of(stats, logits, cot, tgt):
    vocab_rows, tokens = logits.shape
    rows = 128
    whole = lambda *shape: pl.BlockSpec(shape, lambda i: (0,) * len(shape))
    return pl.pallas_call(
        signal_kernel,
        grid=(vocab_rows // rows,),
        in_specs=[
            whole(*stats.shape),
            pl.BlockSpec((rows, tokens), lambda i: (i, 0)),
            whole(1, tokens),
            whole(1, tokens),
        ],
        out_specs=[pl.BlockSpec((rows, tokens), lambda i: (i, 0)), whole(1, tokens)],
        out_shape=[
            jax.ShapeDtypeStruct((vocab_rows, tokens), BF16),
            jax.ShapeDtypeStruct((1, tokens), F32),
        ],
        scratch_shapes=[pltpu.VMEM((1, tokens), F32)],
        compiler_params=pltpu.CompilerParams(
            dimension_semantics=("arbitrary",), vmem_limit_bytes=16 << 20
        ),
        cost_estimate=pl.CostEstimate(
            flops=8 * vocab_rows * tokens, bytes_accessed=6 * vocab_rows * tokens,
            transcendentals=vocab_rows * tokens,
        ),
    )(stats, logits, cot, tgt)


def grad_kernel(tall, grad, *outs):
    block = jnp.dot(tall[...], grad[...], preferred_element_type=F32).astype(BF16)
    for start, size, out in zip(STARTS, SIZES, outs):
        out[...] = block[start : start + size]


def half_grads(half, tall, grad):
    vocab_rows, tokens = grad.shape
    width = tall.shape[0]
    return pl.pallas_call(
        grad_kernel,
        grid=(4,),
        in_specs=[
            pl.BlockSpec((width // 8, vocab_rows), lambda i: (4 * half + i, 0)),
            pl.BlockSpec((vocab_rows, tokens), lambda i: (0, 0)),
        ],
        out_specs=[pl.BlockSpec((None, size, tokens), lambda i: (i, 0, 0)) for size in SIZES],
        out_shape=[pltpu.HBM((4, size, tokens), BF16) for size in SIZES],
        compiler_params=pltpu.CompilerParams(
            dimension_semantics=("arbitrary",), vmem_limit_bytes=32 << 20
        ),
        cost_estimate=pl.CostEstimate(
            flops=vocab_rows * width * tokens, bytes_accessed=width * (vocab_rows + tokens),
            transcendentals=0,
        ),
    )(tall, grad)


def body(hidden, head_weight, targets, loss_cot):
    vocab_rows, _ = head_weight.shape
    own = hidden.T
    feats, tokens = own.shape
    core = lax.axis_index("dp")
    chips = lax.dynamic_index_in_dim(jnp.asarray(CHIPS), lax.axis_index(ALL), 0, keepdims=False)
    tgt = (targets - lax.axis_index(VOCAB) * vocab_rows)[None, :]
    some = small_stage(jnp.broadcast_to(own[None], (8, feats, tokens)))
    wide, tall = turned_weights(chips, head_weight)
    got = gathered_groups(some.reshape(8 * feats, tokens))
    part = half_logits(0, [a for group in got for a in group[:2]], wide)
    logits, stats = half_logits(1, [a for group in got for a in group[2:]], wide, part, tgt)
    stats = lax.all_to_all(stats, VOCAB, 0, 0, tiled=True)
    a_part = a_part_of(chips, [a for group in got for a in group], own)
    grad, tok_loss = signal_of(stats, logits, loss_cot[None, :], tgt)
    sums = summed_groups(half_grads(1, tall, grad), half_grads(0, tall, grad))
    sums = small_stage(sums.reshape(8, feats, tokens))
    hidden_grad = jnp.sum(sums.astype(F32), axis=0).astype(BF16).T
    rows = vocab_rows // 2

    def gram(x):
        mine = lax.dynamic_slice_in_dim(x, core * rows, rows, 0)
        return lax.dot_general(mine, x, (((1,), (1,)), ((), ())), preferred_element_type=F32)

    g_factor = (gram(grad) + gram(lax.ppermute(grad, "dp", SWAP))) / TOK_DEV
    a_factor = (a_part + lax.ppermute(a_part, "dp", SWAP)) / TOK_DEV
    return (tok_loss[0], hidden_grad, g_factor, a_factor)


def solution(mesh):
    finer = Mesh(mesh.devices.reshape(4, 4, 4, mesh.shape["dp"]), ALL)
    return jax.shard_map(
        body,
        mesh=finer,
        in_specs=(P("dp", VOCAB), P(VOCAB, None), P("dp"), P("dp")),
        out_specs=(P("dp"), P("dp", VOCAB), P(ALL, None), P(VOCAB, None)),
        check_vma=False,
    )
```

profile of v0, /device:TPU:0, one launch (start us, length us, event | category | flops | bytes accessed | tf_op | source)
XLA Modules:
  0.0 199.2 jit_solution(5591862805169647391)
XLA Ops:
  1.7 16.2 %all_to_all.15 = bf16[8,64,1024]{2,1,0:T(8,128)(2,1)S(1)} all-to-all(bf16[8,64,1024]{2,1,0:T(8,128)(2,1)S(1)} %broadcast_in_dim.12), channel_id=1, replica_groups={{0,2,8,10,32,34,40,42},{4,6,12,14,36,38,44,46},{16,18,24,26,48,50,56,58..., dimensions={0} | all-to-all | bytes 2097152 | tf_op jit(solution)/shard_map/all_to_all | solution.py:81
  17.9 2.1 %collective-permute-start = (bf16[176,1024]{1,0:T(8,128)(2,1)S(1)}, bf16[176,1024]{1,0:T(8,128)(2,1)S(1)}, u32[]{:S(2)}, u32[]{:S(2)}) collective-permute-start(bf16[176,1024]{1,0:T(8,128)(2,1)S(1)} %get-tuple-element.29), channel_id=1, source_target_pairs={{0,96},{1,33},{2,98},{3,35},{4,100},{5,37},{6,102},{7,39},{8,104},... | collective-permute-start | bytes 1081352 | tf_op jit(solution)/shard_map/ppermute | solution.py:86
  20.0 2.7 %collective-permute-start.4 = (bf16[176,1024]{1,0:T(8,128)(2,1)S(1)}, bf16[176,1024]{1,0:T(8,128)(2,1)S(1)}, u32[]{:S(2)}, u32[]{:S(2)}) collective-permute-start(bf16[176,1024]{1,0:T(8,128)(2,1)S(1)} %get-tuple-element.28), channel_id=1, source_target_pairs={{0,24},{1,9},{2,26},{3,11},{4,28},{5,13},{6,30},{7,15},{8,16},{9,1... | collective-permute-start | bytes 1081352 | tf_op jit(solution)/shard_map/ppermute | solution.py:86
  22.7 1.9 collective-permute-start.8
  24.6 2.0 %collective-permute-done = bf16[176,1024]{1,0:T(8,128)(2,1)S(1)} collective-permute-done((bf16[176,1024]{1,0:T(8,128)(2,1)S(1)}, bf16[176,1024]{1,0:T(8,128)(2,1)S(1)}, u32[]{:S(2)}, u32[]{:S(2)}) %collective-permute-start) | collective-permute-done | bytes 360480 | tf_op jit(solution)/shard_map/ppermute | solution.py:86
  26.7 2.8 %collective-permute-start.2 = (bf16[352,1024]{1,0:T(8,128)(2,1)S(1)}, bf16[352,1024]{1,0:T(8,128)(2,1)S(1)}, u32[]{:S(2)}, u32[]{:S(2)}) collective-permute-start(bf16[352,1024]{1,0:T(8,128)(2,1)S(1)} %pad_maximum_fusion.1.refs_0_), channel_id=1, source_target_pairs={{0,24},{1,9},{2,26},{3,11},{4,28},{5,13},{6,30},{7,15},{8,16},{9,1... | collective-permute-start | bytes 2162696 | tf_op jit(solution)/shard_map/ppermute | solution.py:88
  29.5 1.9 collective-permute-start.6
  31.5 2.1 %collective-permute-start.10 = (bf16[320,1024]{1,0:T(8,128)(2,1)S(1)}, bf16[320,1024]{1,0:T(8,128)(2,1)}, u32[]{:S(2)}, u32[]{:S(2)}) collective-permute-start(bf16[320,1024]{1,0:T(8,128)(2,1)S(1)} %pad_maximum_fusion.3.refs_4_.refs_8_), channel_id=1, source_target_pairs={{0,96},{1,33},{2,98},{3,35},{4,100},{5,37},{6,102},{7,39},{8,104},... | collective-permute-start | bytes 1966088 | tf_op jit(solution)/shard_map/ppermute | solution.py:88
  36.4 7.0 %collective-permute-done.10.refs_5_.refs_9_ = bf16[320,1024]{1,0:T(8,128)(2,1)} collective-permute-done((bf16[320,1024]{1,0:T(8,128)(2,1)S(1)}, bf16[320,1024]{1,0:T(8,128)(2,1)}, u32[]{:S(2)}, u32[]{:S(2)}) %collective-permute-start.10) | collective-permute-done | bytes 655392 | tf_op jit(solution)/shard_map/ppermute | solution.py:88
  43.5 2.0 %collective-permute-start.5 = (bf16[352,1024]{1,0:T(8,128)(2,1)S(1)}, bf16[352,1024]{1,0:T(8,128)(2,1)}, u32[]{:S(2)}, u32[]{:S(2)}) collective-permute-start(bf16[352,1024]{1,0:T(8,128)(2,1)S(1)} %pad_maximum_fusion.2.refs_2_.refs_4_), channel_id=1, source_target_pairs={{0,96},{1,33},{2,98},{3,35},{4,100},{5,37},{6,102},{7,39},{8,104},... | collective-permute-start | bytes 2162696 | tf_op jit(solution)/shard_map/ppermute | solution.py:90
  46.4 2.7 %collective-permute-start.11 = (bf16[320,1024]{1,0:T(8,128)(2,1)}, bf16[320,1024]{1,0:T(8,128)(2,1)}, u32[]{:S(2)}, u32[]{:S(2)}) collective-permute-start(bf16[320,1024]{1,0:T(8,128)(2,1)} %collective-permute-done.10.refs_5_.refs_9_), channel_id=1, source_target_pairs={{0,24},{1,9},{2,26},{3,11},{4,28},{5,13},{6,30},{7,15},{8,16},{9,1... | collective-permute-start | bytes 1966088 | tf_op jit(solution)/shard_map/ppermute | solution.py:90
  49.1 1.8 collective-permute-start.3
  50.9 2.0 %collective-permute-start.7 = (bf16[352,1024]{1,0:T(8,128)(2,1)S(1)}, bf16[352,1024]{1,0:T(8,128)(2,1)}, u32[]{:S(2)}, u32[]{:S(2)}) collective-permute-start(bf16[352,1024]{1,0:T(8,128)(2,1)S(1)} %collective-permute-done.6.refs_3_.refs_5_), channel_id=1, source_target_pairs={{0,96},{1,33},{2,98},{3,35},{4,100},{5,37},{6,102},{7,39},{8,104},... | collective-permute-start | bytes 2162696 | tf_op jit(solution)/shard_map/ppermute | solution.py:90
  52.9 3.4 %copy-done.9 = bf16[1024,4096]{1,0:T(8,128)(2,1)S(1)} copy-done((bf16[1024,4096]{1,0:T(8,128)(2,1)S(1)}, bf16[1024,4096]{1,0:T(8,128)(2,1)}, u32[]{:S(2)}) %copy-start.9) | copy-done | bytes 8388632
  56.3 11.8 %shard_map.84 = (bf16[1024,4096]{1,0:T(8,128)(2,1)}, bf16[4096,1024]{1,0:T(8,128)(2,1)}) custom-call(s32[192]{0:T(256)S(1)} %bitcast.33, bf16[1024,4096]{1,0:T(8,128)(2,1)S(1)} %copy-done.9), custom_call_target="tpu_custom_call" | custom-call | flops 8589934592 | bytes 25165824 | tf_op jit(solution)/shard_map/pallas_call | solution.py:188
  68.1 3.4 %copy-done = bf16[1024,4096]{1,0:T(8,128)(2,1)S(1)} copy-done((bf16[1024,4096]{1,0:T(8,128)(2,1)S(1)}, bf16[1024,4096]{1,0:T(8,128)(2,1)}, u32[]{:S(2)}) %copy-start) | copy-done | bytes 8388632
  71.5 8.8 %shard_map.85.refs_7_ = f32[1024,1024]{1,0:T(8,128)} custom-call(bf16[352,1024]{1,0:T(8,128)(2,1)S(1)} %pad_maximum_fusion.1.refs_0_, bf16[352,1024]{1,0:T(8,128)(2,1)S(1)} %collective-permute-done.2.refs_1_, bf16[352,1024]{1,0:T(8,128)(2,1)S(1)} %pad_maximum_fusion.2.refs_2_.refs_4_, bf16[352,1024]{1,0:T(8,128)(2,1)S(1)} %collective-permute-done.6.refs_3_.refs_5_, ...), custom_call_target="tpu_custom_call" | custom-call | flops 4294967296 | bytes 12582912 | tf_op jit(solution)/shard_map/pallas_call | solution.py:270
  80.4 2.2 %copy-done.1 = f32[1024,1024]{1,0:T(8,128)S(1)} copy-done((f32[1024,1024]{1,0:T(8,128)S(1)}, f32[1024,1024]{1,0:T(8,128)}, u32[]{:S(2)}) %copy-start.1) | copy-done | bytes 4194328
  82.6 9.6 %shard_map.86 = (f32[1024,1024]{1,0:T(8,128)}, f32[64,16,128]{2,1,0:T(8,128)S(1)}) custom-call(bf16[352,1024]{1,0:T(8,128)(2,1)} %collective-permute-done.1.refs_0_.refs_2_, bf16[352,1024]{1,0:T(8,128)(2,1)} %collective-permute-done.3.refs_1_.refs_3_, bf16[352,1024]{1,0:T(8,128)(2,1)} %collective-permute-done.5.refs_2_.refs_6_, ...), custom_call_target="tpu_custom_call" | custom-call | flops 4294967296 | bytes 12582912 | tf_op jit(solution)/shard_map/pallas_call | solution.py:270
  92.3 16.2 %all_to_all.16.stats = f32[64,16,128]{2,1,0:T(8,128)S(1)} all-to-all(f32[64,16,128]{2,1,0:T(8,128)S(1)} %get-tuple-element.17), channel_id=1, replica_groups=mesh['vocab_0'=4,'vocab_1'=4,'vocab_2'=4,'dp'=2] {'vocab_0','vocab_1','v..., dimensions={0} | all-to-all | bytes 1048576 | tf_op jit(solution)/shard_map/all_to_all | solution.py:383
  108.5 2.2 %copy-done.2 = f32[1024,1024]{1,0:T(8,128)S(1)} copy-done((f32[1024,1024]{1,0:T(8,128)S(1)}, f32[1024,1024]{1,0:T(8,128)}, u32[]{:S(2)}) %copy-start.2) | copy-done | bytes 4194328
  110.7 3.7 %shard_map.87 = (bf16[1024,1024]{1,0:T(8,128)(2,1)}, f32[1,1024]{1,0:T(1,128)}) custom-call(f32[64,16,128]{2,1,0:T(8,128)S(1)} %all_to_all.16.stats, f32[1024,1024]{1,0:T(8,128)S(1)} %copy-done.2, f32[1,1024]{1,0:T(1,128)S(1)} %bitcast.32, s32[1,1024]{1,0:T(1,128)S(1)} %bitcast.31), custom_call_target="tpu_custom_call" | custom-call | flops 8388608 | bytes 6291456 | tf_op jit(solution)/shard_map/pallas_call | solution.py:318
  114.3 7.5 %shard_map.89 = (bf16[4,176,1024]{2,1,0:T(8,128)(2,1)}, bf16[4,176,1024]{2,1,0:T(8,128)(2,1)}, bf16[4,160,1024]{2,1,0:T(8,128)(2,1)}) custom-call(bf16[4096,1024]{1,0:T(8,128)(2,1)S(1)} %bitcast.36, bf16[1024,1024]{1,0:T(8,128)(2,1)} %get-tuple-element.21.grad), custom_call_target="tpu_custom_call" | custom-call | flops 4294967296 | bytes 8388608 | tf_op jit(solution)/shard_map/pallas_call | solution.py:352
  122.3 1.4 collective-permute-start.12
  124.9 7.5 %shard_map.88 = (bf16[4,176,1024]{2,1,0:T(8,128)(2,1)}, bf16[4,176,1024]{2,1,0:T(8,128)(2,1)}, bf16[4,160,1024]{2,1,0:T(8,128)(2,1)}) custom-call(bf16[4096,1024]{1,0:T(8,128)(2,1)S(1)} %bitcast.36, bf16[1024,1024]{1,0:T(8,128)(2,1)} %get-tuple-element.21.grad), custom_call_target="tpu_custom_call" | custom-call | flops 4294967296 | bytes 8388608 | tf_op jit(solution)/shard_map/pallas_call | solution.py:352
  132.4 8.5 %collective-permute-done.18 = bf16[4,160,1024]{2,1,0:T(8,128)(2,1)S(1)} collective-permute-done((bf16[4,160,1024]{2,1,0:T(8,128)(2,1)}, bf16[4,160,1024]{2,1,0:T(8,128)(2,1)S(1)}, u32[]{:S(2)}, u32[]{:S(2)}) %collective-permute-start.18) | collective-permute-done | bytes 1310752 | tf_op jit(solution)/shard_map/ppermute | solution.py:104
  140.9 1.1 copy-done.18
  142.0 2.2 %add_convert_fusion.2 = bf16[2,160,1024]{2,1,0:T(8,128)(2,1)} fusion(bf16[4,160,1024]{2,1,0:T(8,128)(2,1)S(1)} %collective-permute-done.18, bf16[4,160,1024]{2,1,0:T(8,128)(2,1)} %get-tuple-element.26), kind=kLoop, calls=%fused_computation.3 | loop fusion | flops 1310720 | bytes 1966080 | tf_op jit(solution)/shard_map/convert_element_type | solution.py:100
  145.0 1.1 copy-done.14
  146.2 1.1 add_convert_fusion.1
  149.2 1.1 add_convert_fusion
  150.4 1.4 collective-permute-start.16
  154.0 10.5 %shard_map.90 = f32[64,4096]{1,0:T(8,128)S(1)} custom-call(s32[192]{0:T(256)S(1)} %bitcast.34, bf16[352,1024]{1,0:T(8,128)(2,1)S(1)} %pad_maximum_fusion.1.refs_0_, bf16[352,1024]{1,0:T(8,128)(2,1)S(1)} %copy-done.4, bf16[352,1024]{1,0:T(8,128)(2,1)} %collective-permute-done.1.refs_0_.refs_2_, bf16[352,1024]{1,0:T(8,128)(2,1)} %collective-permute-done.3.refs_1_.refs_3_, ...), custom_call_target="tpu_custom_call" | custom-call | flops 536870912 | bytes 8388608 | tf_op jit(solution)/shard_map/pallas_call | solution.py:146
  165.1 1.1 fusion.8
  166.2 1.9 collective-permute-start.20
  168.2 1.2 fusion.6
  169.3 2.2 %collective-permute-start.14 = (bf16[176,1024]{1,0:T(8,128)(2,1)S(1)}, bf16[176,1024]{1,0:T(8,128)(2,1)S(1)}, u32[]{:S(2)}, u32[]{:S(2)}) collective-permute-start(bf16[176,1024]{1,0:T(8,128)(2,1)S(1)} %fusion.6), channel_id=1, source_target_pairs={{0,96},{1,33},{2,98},{3,35},{4,100},{5,37},{6,102},{7,39},{8,104},... | collective-permute-start | bytes 1081352 | tf_op jit(solution)/shard_map/ppermute | solution.py:104
  171.5 1.2 fusion.7
  172.7 2.9 %collective-permute-start.17 = (bf16[176,1024]{1,0:T(8,128)(2,1)S(1)}, bf16[176,1024]{1,0:T(8,128)(2,1)S(1)}, u32[]{:S(2)}, u32[]{:S(2)}) collective-permute-start(bf16[176,1024]{1,0:T(8,128)(2,1)S(1)} %fusion.7), channel_id=1, source_target_pairs={{0,24},{1,9},{2,26},{3,11},{4,28},{5,13},{6,30},{7,15},{8,16},{9,1... | collective-permute-start | bytes 1081352 | tf_op jit(solution)/shard_map/ppermute | solution.py:104
  175.5 1.2 fusion.5
  176.7 1.3 collective-permute-done.14
  178.0 1.2 fusion.4
  179.3 2.1 %collective-permute-done.17 = bf16[176,1024]{1,0:T(8,128)(2,1)S(1)} collective-permute-done((bf16[176,1024]{1,0:T(8,128)(2,1)S(1)}, bf16[176,1024]{1,0:T(8,128)(2,1)S(1)}, u32[]{:S(2)}, u32[]{:S(2)}) %collective-permute-start.17) | collective-permute-done | bytes 360480 | tf_op jit(solution)/shard_map/ppermute | solution.py:104
  181.4 1.2 fusion.3
  183.6 3.6 %all-to-all-start.2 = ((bf16[8,64,1024]{2,1,0:T(8,128)(2,1)}), bf16[8,64,1024]{2,1,0:T(8,128)(2,1)S(1)}, u32[]{:S(2)}, u32[]{:S(2)}) async-start(bf16[8,64,1024]{2,1,0:T(8,128)(2,1)} %bitcast.12), calls=%async_computation.2 | async-start | bytes 2097152 | tf_op jit(solution)/shard_map/all_to_all | solution.py:81
  188.3 3.2 %fusion = f32[512,1024]{1,0:T(8,128)S(1)} fusion(bf16[1024,1024]{1,0:T(8,128)(2,1)} %collective-permute-done.21, s32[]{:T(128)S(6)} %select_n.9), kind=kOutput, calls=%fused_computation.6 | convolution fusion | flops 1073741824 | bytes 5242884 | tf_op jit(solution)/shard_map/dot_general | solution.py:393
  191.5 4.5 %add_multiply_fusion = f32[512,1024]{1,0:T(8,128)} fusion(f32[512,1024]{1,0:T(8,128)S(1)} %fusion, bf16[1024,1024]{1,0:T(8,128)(2,1)} %get-tuple-element.21.grad, s32[]{:T(128)S(6)} %select_n.9), kind=kOutput, calls=%fused_computation | convolution fusion | flops 1074790400 | bytes 7340036 | tf_op jit(solution)/shard_map/dot_general | solution.py:393
  196.1 2.3 %all-to-all-done.2 = bf16[8,64,1024]{2,1,0:T(8,128)(2,1)S(1)} async-done(((bf16[8,64,1024]{2,1,0:T(8,128)(2,1)}), bf16[8,64,1024]{2,1,0:T(8,128)(2,1)S(1)}, u32[]{:S(2)}, u32[]{:S(2)}) %all-to-all-start.2) | async-done | bytes 1048608 | tf_op jit(solution)/shard_map/all_to_all | solution.py:81
  (80 shorter events, 15.2 us)
Async XLA Ops:
  17.9 8.7 %collective-permute-start = (bf16[176,1024]{1,0:T(8,128)(2,1)S(1)}, bf16[176,1024]{1,0:T(8,128)(2,1)S(1)}, u32[]{:S(2)}, u32[]{:S(2)}) collective-permute-start(bf16[176,1024]{1,0:T(8,128)(2,1)S(1)} %get-tuple-element.29), channel_id=1, source_target_pairs={{0,96},{1,33},{2,98},{3,35},{4,100},{5,37},{6,102},{7,39},{8,104},... | collective-permute-start | bytes 1081352 | tf_op jit(solution)/shard_map/ppermute | solution.py:86
  20.0 9.5 %collective-permute-start.4 = (bf16[176,1024]{1,0:T(8,128)(2,1)S(1)}, bf16[176,1024]{1,0:T(8,128)(2,1)S(1)}, u32[]{:S(2)}, u32[]{:S(2)}) collective-permute-start(bf16[176,1024]{1,0:T(8,128)(2,1)S(1)} %get-tuple-element.28), channel_id=1, source_target_pairs={{0,24},{1,9},{2,26},{3,11},{4,28},{5,13},{6,30},{7,15},{8,16},{9,1... | collective-permute-start | bytes 1081352 | tf_op jit(solution)/shard_map/ppermute | solution.py:86
  22.7 8.7 %collective-permute-start.8 = (bf16[160,1024]{1,0:T(8,128)(2,1)S(1)}, bf16[160,1024]{1,0:T(8,128)(2,1)S(1)}, u32[]{:S(2)}, u32[]{:S(2)}) collective-permute-start(bf16[160,1024]{1,0:T(8,128)(2,1)S(1)} %slice.110), channel_id=1, source_target_pairs={{0,6},{1,3},{2,4},{3,1},{4,2},{5,7},{6,0},{7,5},{8,14},{9,11},{10,... | collective-permute-start | bytes 983048 | tf_op jit(solution)/shard_map/ppermute | solution.py:86
  26.7 22.4 %collective-permute-start.2 = (bf16[352,1024]{1,0:T(8,128)(2,1)S(1)}, bf16[352,1024]{1,0:T(8,128)(2,1)S(1)}, u32[]{:S(2)}, u32[]{:S(2)}) collective-permute-start(bf16[352,1024]{1,0:T(8,128)(2,1)S(1)} %pad_maximum_fusion.1.refs_0_), channel_id=1, source_target_pairs={{0,24},{1,9},{2,26},{3,11},{4,28},{5,13},{6,30},{7,15},{8,16},{9,1... | collective-permute-start | bytes 2162696 | tf_op jit(solution)/shard_map/ppermute | solution.py:88
  29.5 21.4 %collective-permute-start.6 = (bf16[352,1024]{1,0:T(8,128)(2,1)S(1)}, bf16[352,1024]{1,0:T(8,128)(2,1)S(1)}, u32[]{:S(2)}, u32[]{:S(2)}) collective-permute-start(bf16[352,1024]{1,0:T(8,128)(2,1)S(1)} %pad_maximum_fusion.2.refs_2_.refs_4_), channel_id=1, source_target_pairs={{0,6},{1,3},{2,4},{3,1},{4,2},{5,7},{6,0},{7,5},{8,14},{9,11},{10,... | collective-permute-start | bytes 2162696 | tf_op jit(solution)/shard_map/ppermute | solution.py:88
  31.5 12.0 %collective-permute-start.10 = (bf16[320,1024]{1,0:T(8,128)(2,1)S(1)}, bf16[320,1024]{1,0:T(8,128)(2,1)}, u32[]{:S(2)}, u32[]{:S(2)}) collective-permute-start(bf16[320,1024]{1,0:T(8,128)(2,1)S(1)} %pad_maximum_fusion.3.refs_4_.refs_8_), channel_id=1, source_target_pairs={{0,96},{1,33},{2,98},{3,35},{4,100},{5,37},{6,102},{7,39},{8,104},... | collective-permute-start | bytes 1966088 | tf_op jit(solution)/shard_map/ppermute | solution.py:88
  33.6 12.8 %collective-permute-start.9 = (bf16[320,1024]{1,0:T(8,128)(2,1)S(1)}, bf16[320,1024]{1,0:T(8,128)(2,1)}, u32[]{:S(2)}, u32[]{:S(2)}) collective-permute-start(bf16[320,1024]{1,0:T(8,128)(2,1)S(1)} %pad_maximum_fusion.3.refs_4_.refs_8_), channel_id=1, source_target_pairs={{0,24},{1,9},{2,26},{3,11},{4,28},{5,13},{6,30},{7,15},{8,16},{9,1... | collective-permute-start | bytes 1966088 | tf_op jit(solution)/shard_map/ppermute | solution.py:90
  35.4 45.0 %collective-permute-start.1 = (bf16[352,1024]{1,0:T(8,128)(2,1)S(1)}, bf16[352,1024]{1,0:T(8,128)(2,1)}, u32[]{:S(2)}, u32[]{:S(2)}) collective-permute-start(bf16[352,1024]{1,0:T(8,128)(2,1)S(1)} %pad_maximum_fusion.1.refs_0_), channel_id=1, source_target_pairs={{0,6},{1,3},{2,4},{3,1},{4,2},{5,7},{6,0},{7,5},{8,14},{9,11},{10,... | collective-permute-start | bytes 2162696 | tf_op jit(solution)/shard_map/ppermute | solution.py:90
  43.5 36.9 %collective-permute-start.5 = (bf16[352,1024]{1,0:T(8,128)(2,1)S(1)}, bf16[352,1024]{1,0:T(8,128)(2,1)}, u32[]{:S(2)}, u32[]{:S(2)}) collective-permute-start(bf16[352,1024]{1,0:T(8,128)(2,1)S(1)} %pad_maximum_fusion.2.refs_2_.refs_4_), channel_id=1, source_target_pairs={{0,96},{1,33},{2,98},{3,35},{4,100},{5,37},{6,102},{7,39},{8,104},... | collective-permute-start | bytes 2162696 | tf_op jit(solution)/shard_map/ppermute | solution.py:90
  46.4 34.0 %collective-permute-start.11 = (bf16[320,1024]{1,0:T(8,128)(2,1)}, bf16[320,1024]{1,0:T(8,128)(2,1)}, u32[]{:S(2)}, u32[]{:S(2)}) collective-permute-start(bf16[320,1024]{1,0:T(8,128)(2,1)} %collective-permute-done.10.refs_5_.refs_9_), channel_id=1, source_target_pairs={{0,24},{1,9},{2,26},{3,11},{4,28},{5,13},{6,30},{7,15},{8,16},{9,1... | collective-permute-start | bytes 1966088 | tf_op jit(solution)/shard_map/ppermute | solution.py:90
  49.1 19.0 %copy-start.3 = (bf16[352,1024]{1,0:T(8,128)(2,1)}, bf16[352,1024]{1,0:T(8,128)(2,1)S(1)}, u32[]{:S(2)}) copy-start(bf16[352,1024]{1,0:T(8,128)(2,1)S(1)} %collective-permute-done.2.refs_1_) | copy-start | bytes 2162692
  49.1 31.3 %collective-permute-start.3 = (bf16[352,1024]{1,0:T(8,128)(2,1)S(1)}, bf16[352,1024]{1,0:T(8,128)(2,1)}, u32[]{:S(2)}, u32[]{:S(2)}) collective-permute-start(bf16[352,1024]{1,0:T(8,128)(2,1)S(1)} %collective-permute-done.2.refs_1_), channel_id=1, source_target_pairs={{0,6},{1,3},{2,4},{3,1},{4,2},{5,7},{6,0},{7,5},{8,14},{9,11},{10,... | collective-permute-start | bytes 2162696 | tf_op jit(solution)/shard_map/ppermute | solution.py:90
  50.9 17.2 %copy-start.5 = (bf16[352,1024]{1,0:T(8,128)(2,1)}, bf16[352,1024]{1,0:T(8,128)(2,1)S(1)}, u32[]{:S(2)}) copy-start(bf16[352,1024]{1,0:T(8,128)(2,1)S(1)} %collective-permute-done.6.refs_3_.refs_5_) | copy-start | bytes 2162692
  50.9 29.5 %collective-permute-start.7 = (bf16[352,1024]{1,0:T(8,128)(2,1)S(1)}, bf16[352,1024]{1,0:T(8,128)(2,1)}, u32[]{:S(2)}, u32[]{:S(2)}) collective-permute-start(bf16[352,1024]{1,0:T(8,128)(2,1)S(1)} %collective-permute-done.6.refs_3_.refs_5_), channel_id=1, source_target_pairs={{0,96},{1,33},{2,98},{3,35},{4,100},{5,37},{6,102},{7,39},{8,104},... | collective-permute-start | bytes 2162696 | tf_op jit(solution)/shard_map/ppermute | solution.py:90
  52.9 3.4 %copy-start.9 = (bf16[1024,4096]{1,0:T(8,128)(2,1)S(1)}, bf16[1024,4096]{1,0:T(8,128)(2,1)}, u32[]{:S(2)}) copy-start(bf16[1024,4096]{1,0:T(8,128)(2,1)} %w.1) | copy-start | bytes 25165828
  56.3 11.8 %copy-start.21 = (s32[1024]{0:T(1024)S(1)}, s32[1024]{0:T(1024)}, u32[]{:S(2)}) copy-start(s32[1024]{0:T(1024)} %param.7) | copy-start | bytes 12292
  68.1 3.4 %copy-start = (bf16[1024,4096]{1,0:T(8,128)(2,1)S(1)}, bf16[1024,4096]{1,0:T(8,128)(2,1)}, u32[]{:S(2)}) copy-start(bf16[1024,4096]{1,0:T(8,128)(2,1)} %get-tuple-element.16.refs_6_) | copy-start | bytes 25165828
  71.5 42.8 %slice-start = ((s8[8388608]{0:T(1024)(128)(4,1)}), s8[4194304]{0:T(1024)(128)(4,1)S(1)}, s32[]{:S(2)}) async-start(s8[8388608]{0:T(1024)(128)(4,1)} %bitcast.35), calls=%async_computation.3 | async-start | bytes 8388608
  80.4 2.2 %copy-start.1 = (f32[1024,1024]{1,0:T(8,128)S(1)}, f32[1024,1024]{1,0:T(8,128)}, u32[]{:S(2)}) copy-start(f32[1024,1024]{1,0:T(8,128)} %shard_map.85.refs_7_) | copy-start | bytes 12582916
  82.6 25.9 %copy-start.8 = (f32[1024]{0:T(1024)S(1)}, f32[1024]{0:T(1024)}, u32[]{:S(2)}) copy-start(f32[1024]{0:T(1024)} %param.8) | copy-start | bytes 12292
  82.6 31.7 %slice-start.1 = ((s8[8388608]{0:T(1024)(128)(4,1)}), s8[4194304]{0:T(1024)(128)(4,1)S(1)}, s32[]{:S(2)}) async-start(s8[8388608]{0:T(1024)(128)(4,1)} %bitcast.35), calls=%async_computation.4 | async-start | bytes 8388608
  108.5 2.2 %copy-start.2 = (f32[1024,1024]{1,0:T(8,128)S(1)}, f32[1024,1024]{1,0:T(8,128)}, u32[]{:S(2)}) copy-start(f32[1024,1024]{1,0:T(8,128)} %get-tuple-element.18.logits) | copy-start | bytes 12582916
  121.9 19.0 %collective-permute-start.18 = (bf16[4,160,1024]{2,1,0:T(8,128)(2,1)}, bf16[4,160,1024]{2,1,0:T(8,128)(2,1)S(1)}, u32[]{:S(2)}, u32[]{:S(2)}) collective-permute-start(bf16[4,160,1024]{2,1,0:T(8,128)(2,1)} %get-tuple-element.27), channel_id=1, source_target_pairs={{0,24},{1,9},{2,26},{3,11},{4,28},{5,13},{6,30},{7,15},{8,16},{9,1... | collective-permute-start | bytes 3932168 | tf_op jit(solution)/shard_map/ppermute | solution.py:104
  122.3 22.7 %collective-permute-start.12 = (bf16[4,176,1024]{2,1,0:T(8,128)(2,1)}, bf16[4,176,1024]{2,1,0:T(8,128)(2,1)S(1)}, u32[]{:S(2)}, u32[]{:S(2)}) collective-permute-start(bf16[4,176,1024]{2,1,0:T(8,128)(2,1)} %get-tuple-element.23), channel_id=1, source_target_pairs={{0,6},{1,3},{2,4},{3,1},{4,2},{5,7},{6,0},{7,5},{8,14},{9,11},{10,... | collective-permute-start | bytes 4325384 | tf_op jit(solution)/shard_map/ppermute | solution.py:104
  123.8 24.4 %collective-permute-start.15 = (bf16[4,176,1024]{2,1,0:T(8,128)(2,1)}, bf16[4,176,1024]{2,1,0:T(8,128)(2,1)S(1)}, u32[]{:S(2)}, u32[]{:S(2)}) collective-permute-start(bf16[4,176,1024]{2,1,0:T(8,128)(2,1)} %get-tuple-element.25), channel_id=1, source_target_pairs={{0,96},{1,33},{2,98},{3,35},{4,100},{5,37},{6,102},{7,39},{8,104},... | collective-permute-start | bytes 4325384 | tf_op jit(solution)/shard_map/ppermute | solution.py:104
  132.4 13.8 %copy-start.16 = (bf16[4,176,1024]{2,1,0:T(8,128)(2,1)S(1)}, bf16[4,176,1024]{2,1,0:T(8,128)(2,1)}, u32[]{:S(2)}) copy-start(bf16[4,176,1024]{2,1,0:T(8,128)(2,1)} %get-tuple-element.22) | copy-start | bytes 4325380
  140.9 1.1 copy-start.18
  144.2 5.0 %copy-start.12 = (bf16[4,176,1024]{2,1,0:T(8,128)(2,1)S(1)}, bf16[4,176,1024]{2,1,0:T(8,128)(2,1)}, u32[]{:S(2)}) copy-start(bf16[4,176,1024]{2,1,0:T(8,128)(2,1)} %get-tuple-element.24) | copy-start | bytes 4325380
  144.2 20.8 %collective-permute-start.19 = (bf16[2,160,1024]{2,1,0:T(8,128)(2,1)}, bf16[2,160,1024]{2,1,0:T(8,128)(2,1)}, u32[]{:S(2)}, u32[]{:S(2)}) collective-permute-start(bf16[2,160,1024]{2,1,0:T(8,128)(2,1)} %add_convert_fusion.2), channel_id=1, source_target_pairs={{0,96},{1,33},{2,98},{3,35},{4,100},{5,37},{6,102},{7,39},{8,104},... | collective-permute-start | bytes 1966088 | tf_op jit(solution)/shard_map/ppermute | solution.py:104
  145.0 1.1 copy-start.14
  147.3 4.4 %copy-start.7 = (bf16[1024,64]{0,1:T(8,128)(2,1)S(1)}, bf16[1024,64]{0,1:T(8,128)(2,1)}, u32[]{:S(2)}) copy-start(bf16[1024,64]{0,1:T(8,128)(2,1)} %param.5) | copy-start | bytes 393220
  147.3 20.8 %collective-permute-start.13 = (bf16[2,176,1024]{2,1,0:T(8,128)(2,1)}, bf16[2,176,1024]{2,1,0:T(8,128)(2,1)}, u32[]{:S(2)}, u32[]{:S(2)}) collective-permute-start(bf16[2,176,1024]{2,1,0:T(8,128)(2,1)} %add_convert_fusion.1), channel_id=1, source_target_pairs={{0,24},{1,9},{2,26},{3,11},{4,28},{5,13},{6,30},{7,15},{8,16},{9,1... | collective-permute-start | bytes 2162696 | tf_op jit(solution)/shard_map/ppermute | solution.py:104
  148.1 1.1 copy-start.10
  150.4 21.1 %collective-permute-start.16 = (bf16[2,176,1024]{2,1,0:T(8,128)(2,1)}, bf16[2,176,1024]{2,1,0:T(8,128)(2,1)}, u32[]{:S(2)}, u32[]{:S(2)}) collective-permute-start(bf16[2,176,1024]{2,1,0:T(8,128)(2,1)} %add_convert_fusion), channel_id=1, source_target_pairs={{0,6},{1,3},{2,4},{3,1},{4,2},{5,7},{6,0},{7,5},{8,14},{9,11},{10,... | collective-permute-start | bytes 2162696 | tf_op jit(solution)/shard_map/ppermute | solution.py:104
  151.7 1.1 copy-start.4
  152.9 1.1 copy-start.6
  154.0 11.1 %copy-start.19 = (bf16[4,160,1024]{2,1,0:T(8,128)(2,1)S(1)}, bf16[4,160,1024]{2,1,0:T(8,128)(2,1)}, u32[]{:S(2)}) copy-start(bf16[4,160,1024]{2,1,0:T(8,128)(2,1)} %copy-done.18) | copy-start | bytes 3932164
  154.0 11.1 %copy-start.20 = (bf16[4,160,1024]{2,1,0:T(8,128)(2,1)S(1)}, bf16[4,160,1024]{2,1,0:T(8,128)(2,1)}, u32[]{:S(2)}) copy-start(bf16[4,160,1024]{2,1,0:T(8,128)(2,1)} %get-tuple-element.26) | copy-start | bytes 3932164
  154.0 14.2 %copy-start.15 = (bf16[4,176,1024]{2,1,0:T(8,128)(2,1)S(1)}, bf16[4,176,1024]{2,1,0:T(8,128)(2,1)}, u32[]{:S(2)}) copy-start(bf16[4,176,1024]{2,1,0:T(8,128)(2,1)} %copy-done.14) | copy-start | bytes 4325380
  154.0 14.2 %copy-start.17 = (bf16[4,176,1024]{2,1,0:T(8,128)(2,1)S(1)}, bf16[4,176,1024]{2,1,0:T(8,128)(2,1)}, u32[]{:S(2)}) copy-start(bf16[4,176,1024]{2,1,0:T(8,128)(2,1)} %get-tuple-element.22) | copy-start | bytes 4325380
  154.0 17.5 %copy-start.13 = (bf16[4,176,1024]{2,1,0:T(8,128)(2,1)S(1)}, bf16[4,176,1024]{2,1,0:T(8,128)(2,1)}, u32[]{:S(2)}) copy-start(bf16[4,176,1024]{2,1,0:T(8,128)(2,1)} %get-tuple-element.24) | copy-start | bytes 4325380
  164.5 7.0 %copy-start.11 = (bf16[4,176,1024]{2,1,0:T(8,128)(2,1)S(1)}, bf16[4,176,1024]{2,1,0:T(8,128)(2,1)}, u32[]{:S(2)}) copy-start(bf16[4,176,1024]{2,1,0:T(8,128)(2,1)} %copy-done.10) | copy-start | bytes 4325380
  164.5 22.8 %collective-permute-start.22 = (f32[64,4096]{1,0:T(8,128)S(1)}, f32[64,4096]{1,0:T(8,128)S(1)}, u32[]{:S(2)}, u32[]{:S(2)}) collective-permute-start(f32[64,4096]{1,0:T(8,128)S(1)} %shard_map.90), channel_id=1, source_target_pairs={{0,1},{1,0},{2,3},{3,2},{4,5},{5,4},{6,7},{7,6},{8,9},{9,8},{10,11... | collective-permute-start | bytes 3145736 | tf_op jit(solution)/shard_map/ppermute | solution.py:396
  164.6 23.8 %collective-permute-start.21 = (bf16[1024,1024]{1,0:T(8,128)(2,1)}, bf16[1024,1024]{1,0:T(8,128)(2,1)}, u32[]{:S(2)}, u32[]{:S(2)}) collective-permute-start(bf16[1024,1024]{1,0:T(8,128)(2,1)} %get-tuple-element.21.grad), channel_id=1, source_target_pairs={{0,1},{1,0},{2,3},{3,2},{4,5},{5,4},{6,7},{7,6},{8,9},{9,8},{10,11... | collective-permute-start | bytes 6291464 | tf_op jit(solution)/shard_map/ppermute | solution.py:395
  166.2 9.3 %collective-permute-start.20 = (bf16[160,1024]{1,0:T(8,128)(2,1)S(1)}, bf16[160,1024]{1,0:T(8,128)(2,1)S(1)}, u32[]{:S(2)}, u32[]{:S(2)}) collective-permute-start(bf16[160,1024]{1,0:T(8,128)(2,1)S(1)} %fusion.8), channel_id=1, source_target_pairs={{0,6},{1,3},{2,4},{3,1},{4,2},{5,7},{6,0},{7,5},{8,14},{9,11},{10,... | collective-permute-start | bytes 983048 | tf_op jit(solution)/shard_map/ppermute | solution.py:104
  169.3 8.7 %collective-permute-start.14 = (bf16[176,1024]{1,0:T(8,128)(2,1)S(1)}, bf16[176,1024]{1,0:T(8,128)(2,1)S(1)}, u32[]{:S(2)}, u32[]{:S(2)}) collective-permute-start(bf16[176,1024]{1,0:T(8,128)(2,1)S(1)} %fusion.6), channel_id=1, source_target_pairs={{0,96},{1,33},{2,98},{3,35},{4,100},{5,37},{6,102},{7,39},{8,104},... | collective-permute-start | bytes 1081352 | tf_op jit(solution)/shard_map/ppermute | solution.py:104
  172.7 8.7 %collective-permute-start.17 = (bf16[176,1024]{1,0:T(8,128)(2,1)S(1)}, bf16[176,1024]{1,0:T(8,128)(2,1)S(1)}, u32[]{:S(2)}, u32[]{:S(2)}) collective-permute-start(bf16[176,1024]{1,0:T(8,128)(2,1)S(1)} %fusion.7), channel_id=1, source_target_pairs={{0,24},{1,9},{2,26},{3,11},{4,28},{5,13},{6,30},{7,15},{8,16},{9,1... | collective-permute-start | bytes 1081352 | tf_op jit(solution)/shard_map/ppermute | solution.py:104
  183.6 14.7 %all-to-all-start.2 = ((bf16[8,64,1024]{2,1,0:T(8,128)(2,1)}), bf16[8,64,1024]{2,1,0:T(8,128)(2,1)S(1)}, u32[]{:S(2)}, u32[]{:S(2)}) async-start(bf16[8,64,1024]{2,1,0:T(8,128)(2,1)} %bitcast.12), calls=%async_computation.2 | async-start | bytes 2097152 | tf_op jit(solution)/shard_map/all_to_all | solution.py:81
where the time goes:
time: 201 us; the launch traced here: 199 us
  Pallas kernels  59.5 us (30%)
  starting transfers between devices  41.2 us (20%)
  blocking collectives  32.4 us (16%)
  waiting for transfers between devices  24.2 us (12%)
  local copies, waits for them, and re-layouts  18.6 us (9%)
  other arithmetic  14.7 us (7%)
  matrix products  7.74 us (4%)
    pallas_call x2, Pallas kernels, half_logits(): pl.pallas_call(late_kernel if late else early_kernel, grid=(vocab_rows //...  18.5 us
    unnamed x48, local copies, waits for them, and re-layouts  16.8 us
    all_to_all x1, blocking collectives, small_stage(): lax.all_to_all(x, ALL, 0, 0, axis_index_groups=SMALL_CUBES, tiled=True)  16.2 us
    all_to_all x1, blocking collectives, body(): stats = lax.all_to_all(stats, VOCAB, 0, 0, tiled=True)  16.2 us
    pallas_call x2, Pallas kernels, half_grads(): pl.pallas_call(grad_kernel, grid=(4,), in_specs=[pl.BlockSpec((width // 8...  15.1 us
    ppermute x9, starting transfers between devices, summed_groups(): trade = lambda x, g, step: lax.ppermute(x, ALL, LARGE_PAIRS[(g + step) % 3])  12.9 us
    ppermute x9, waiting for transfers between devices, summed_groups(): trade = lambda x, g, step: lax.ppermute(x, ALL, LARGE_PAIRS[(g + step) % 3])  11.9 us
    pallas_call x1, Pallas kernels, turned_weights(): pl.pallas_call(turn_kernel, grid_spec=pltpu.PrefetchScalarGridSpec(num_sc...  11.8 us
  transfers between devices with their start and end apart: 24, of which 7 were waited for; matrix products, arithmetic and copies ran while one was open for 11% of the time, Pallas kernels for 19%

commit v1 on v0

--- a/solution.py
+++ b/solution.py
@@ -10,6 +10,7 @@
 TOK_DEV = 1024
 VOCAB = ("vocab_0", "vocab_1", "vocab_2")
 ALL = ("vocab_0", "vocab_1", "vocab_2", "dp")
+ALL_VMEM = (64 << 20) - (256 << 10)
 
 SMALL = (((0, 1), (2, 3)), ((0, 3), (1, 2)))
 LARGE = (((1, 2), (0, 3)), ((0, 1), (3, 2)))
@@ -81,33 +82,78 @@
     return lax.all_to_all(x, ALL, 0, 0, axis_index_groups=SMALL_CUBES, tiled=True)
 
 
+def in_hbm(x):
+    return pltpu.with_memory_space_constraint(x, pltpu.HBM)
+
+
 def gathered_groups(some):
+    def get(x, g, step):
+        return lax.ppermute(x, ALL, LARGE_PAIRS[(g + step) % 3])
+
     held = [some[start : start + size] for start, size in zip(STARTS, SIZES)]
-    got = [lax.ppermute(held[g], ALL, LARGE_PAIRS[g]) for g in range(3)]
+    got = [get(held[g], g, 0) for g in range(3)]
     first = [jnp.concatenate([h, r]) for h, r in zip(held, got)]
-    second = [lax.ppermute(first[g], ALL, LARGE_PAIRS[(g + 1) % 3]) for g in range(3)]
-    third = [
-        [lax.ppermute(part, ALL, LARGE_PAIRS[(g + 2) % 3]) for part in (first[g], second[g])]
-        for g in range(3)
-    ]
-    return [[first[g], second[g], *third[g]] for g in range(3)]
-
-
-def add_up(*terms):
-    total = terms[0].astype(F32)
+    second = [get(first[g], g, 1) for g in range(3)]
+    third = [get(first[g], g, 2) for g in range(3)]
+    fourth = [get(second[g], g, 2) for g in range(3)]
+    return [[first[g], second[g], third[g], fourth[g]] for g in range(3)]
+
+
+def add_kernel(*refs):
+    *terms, out = refs
+    total = terms[0][...].astype(F32)
     for term in terms[1:]:
-        total = total + term.astype(F32)
-    return total.astype(BF16)
+        total = total + term[...].astype(F32)
+    out[...] = total.astype(BF16)
+
+
+def add_up(count, *terms):
+    _, rows, tokens = terms[0][0].shape
+    block = lambda first: pl.BlockSpec((None, rows, tokens), lambda i: (first + i, 0, 0))
+    return pl.pallas_call(
+        add_kernel,
+        grid=(count,),
+        in_specs=[block(first) for _, first in terms],
+        out_specs=block(0),
+        out_shape=jax.ShapeDtypeStruct((count, rows, tokens), BF16),
+        compiler_params=pltpu.CompilerParams(
+            dimension_semantics=("arbitrary",), vmem_limit_bytes=ALL_VMEM
+        ),
+        cost_estimate=pl.CostEstimate(
+            flops=len(terms) * count * rows * tokens,
+            bytes_accessed=2 * (len(terms) + 1) * count * rows * tokens, transcendentals=0,
+        ),
+    )(*[in_hbm(x) for x, _ in terms])
 
 
 def summed_groups(sends, keeps):
     trade = lambda x, g, step: lax.ppermute(x, ALL, LARGE_PAIRS[(g + step) % 3])
     far = [trade(sends[g], g, 2) for g in range(3)]
-    mid = [trade(add_up(keeps[g][2:], far[g][2:]), g, 1) for g in range(3)]
-    near = [trade(add_up(keeps[g][1], far[g][1], mid[g][1]), g, 0) for g in range(3)]
+    mid = [trade(add_up(2, (keeps[g], 2), (far[g], 2)), g, 1) for g in range(3)]
+    near = [
+        trade(add_up(1, (keeps[g], 1), (far[g], 1), (mid[g], 1)), g, 0) for g in range(3)
+    ]
     return jnp.concatenate(
-        [add_up(keeps[g][0], far[g][0], mid[g][0], near[g]) for g in range(3)]
+        [add_up(1, (keeps[g], 0), (far[g], 0), (mid[g], 0), (near[g], 0))[0] for g in range(3)]
     )
+
+
+def sum_kernel(pieces, out):
+    out[...] = jnp.sum(pieces[...].astype(F32), axis=0).astype(BF16)
+
+
+def summed(pieces):
+    count, rows, tokens = pieces.shape
+    return pl.pallas_call(
+        sum_kernel,
+        grid=(2,),
+        in_specs=[pl.BlockSpec((count, rows, tokens // 2), lambda i: (0, 0, i))],
+        out_specs=pl.BlockSpec((rows, tokens // 2), lambda i: (0, i)),
+        out_shape=jax.ShapeDtypeStruct((rows, tokens), BF16),
+        compiler_params=pltpu.CompilerParams(
+            dimension_semantics=("arbitrary",), vmem_limit_bytes=8 << 20
+        ),
+    )(pieces)
 
 
 def gather_copies(chips, got, h):
@@ -148,17 +194,17 @@
         grid_spec=pltpu.PrefetchScalarGridSpec(
             num_scalar_prefetch=1,
             grid=(),
-            in_specs=[pl.BlockSpec(memory_space=pl.ANY)] * len(got)
+            in_specs=[pl.BlockSpec(memory_space=pltpu.HBM)] * len(got)
             + [pl.BlockSpec(memory_space=pltpu.VMEM)],
             out_specs=pl.BlockSpec(memory_space=pltpu.VMEM),
             scratch_shapes=[pltpu.VMEM((width, tokens), BF16), pltpu.SemaphoreType.DMA],
         ),
         out_shape=jax.ShapeDtypeStruct((feats, width), F32),
-        compiler_params=pltpu.CompilerParams(vmem_limit_bytes=32 << 20),
+        compiler_params=pltpu.CompilerParams(vmem_limit_bytes=ALL_VMEM),
         cost_estimate=pl.CostEstimate(
             flops=2 * feats * width * tokens, bytes_accessed=2 * width * tokens, transcendentals=0
         ),
-    )(chips, *got, own)
+    )(chips, *[in_hbm(x) for x in got], own)
 
 
 def turn_kernel(chips, w, wide, tall, turned):
@@ -204,7 +250,7 @@
         cost_estimate=pl.CostEstimate(
             flops=2048 * vocab_rows * width, bytes_accessed=6 * vocab_rows * width, transcendentals=0
         ),
-    )(chips, w)
+    )(chips, in_hbm(w))
 
 
 def half_copies(got, h):
@@ -281,14 +327,14 @@
         + [pltpu.VMEM((1, tokens), F32)] * (3 if late else 0)
         + [pltpu.SemaphoreType.DMA],
         compiler_params=pltpu.CompilerParams(
-            dimension_semantics=("arbitrary",), vmem_limit_bytes=32 << 20
+            dimension_semantics=("arbitrary",), vmem_limit_bytes=ALL_VMEM
         ),
         cost_estimate=pl.CostEstimate(
             flops=vocab_rows * width * tokens,
             bytes_accessed=width * (vocab_rows + tokens) + 4 * vocab_rows * tokens,
             transcendentals=vocab_rows * tokens,
         ),
-    )(*got, wide, *([part, tgt] if late else []))
+    )(*got, in_hbm(wide), *([in_hbm(part), tgt] if late else []))
 
 
 def signal_kernel(stats, logits, cot, tgt, grad, loss, row):
@@ -337,7 +383,7 @@
             flops=8 * vocab_rows * tokens, bytes_accessed=6 * vocab_rows * tokens,
             transcendentals=vocab_rows * tokens,
         ),
-    )(stats, logits, cot, tgt)
+    )(stats, in_hbm(logits), cot, tgt)
 
 
 def grad_kernel(tall, grad, *outs):
@@ -359,13 +405,13 @@
         out_specs=[pl.BlockSpec((None, size, tokens), lambda i: (i, 0, 0)) for size in SIZES],
         out_shape=[pltpu.HBM((4, size, tokens), BF16) for size in SIZES],
         compiler_params=pltpu.CompilerParams(
-            dimension_semantics=("arbitrary",), vmem_limit_bytes=32 << 20
+            dimension_semantics=("arbitrary",), vmem_limit_bytes=ALL_VMEM
         ),
         cost_estimate=pl.CostEstimate(
             flops=vocab_rows * width * tokens, bytes_accessed=width * (vocab_rows + tokens),
             transcendentals=0,
         ),
-    )(tall, grad)
+    )(in_hbm(tall), grad)
 
 
 def body(hidden, head_weight, targets, loss_cot):
@@ -385,7 +431,7 @@
     grad, tok_loss = signal_of(stats, logits, loss_cot[None, :], tgt)
     sums = summed_groups(half_grads(1, tall, grad), half_grads(0, tall, grad))
     sums = small_stage(sums.reshape(8, feats, tokens))
-    hidden_grad = jnp.sum(sums.astype(F32), axis=0).astype(BF16).T
+    hidden_grad = summed(sums).T
     rows = vocab_rows // 2
 
     def gram(x):

time: 201 us -> 207 us (1.030)
  Pallas kernels: 59.5 us -> 87.4 us
  local copies, waits for them, and re-layouts: 18.6 us -> 3.14 us
  other arithmetic: 14.7 us -> 7.14 us
  waiting for transfers between devices: 24.2 us -> 28 us
    pallas_call x0 -> x10, Pallas kernels: none -> 20 us  [the longest x9 19.1 us: add_up(): pl.pallas_call(add_kernel, grid=(count,), in_specs=[block(first) for _, f...]
    unnamed x48 -> x18, local copies, waits for them, and re-layouts: 16.8 us -> 1.35 us
    convert_element_type x9 -> x0, other arithmetic: 11.6 us -> none  [add_up(): return total.astype(BF16)]
    ppermute x9, waiting for transfers between devices: 11.9 us -> 15.6 us  [summed_groups(): trade = lambda x, g, step: lax.ppermute(x, ALL, LARGE_PAIRS[(g + step) % 3])]
    pallas_call x1, Pallas kernels: 11.8 us -> 15.2 us  [turned_weights(): pl.pallas_call(turn_kernel, grid_spec=pltpu.PrefetchScalarGridSpec(num_sc...]
    pallas_call x2, Pallas kernels: 18.5 us -> 21.6 us  [half_logits(): pl.pallas_call(late_kernel if late else early_kernel, grid=(vocab_rows //...]
  transfers between devices with their start and end apart: 24 -> 24, of which waited for: 7 -> 6; matrix products, arithmetic and copies ran while one was open for 11% -> 7% of each run, Pallas kernels for 19% -> 30%
where the time goes in v1:
time: 207 us; the launch traced here: 206 us
  Pallas kernels  87.4 us (42%)
  starting transfers between devices  40.6 us (20%)
  blocking collectives  33 us (16%)
  waiting for transfers between devices  28 us (14%)
  other arithmetic  7.14 us (3%)
  matrix products  5.96 us (3%)
  local copies, waits for them, and re-layouts  3.14 us (2%)
    ppermute x12, starting transfers between devices, get(): return lax.ppermute(x, ALL, LARGE_PAIRS[(g + step) % 3])  23.7 us
    pallas_call x2, Pallas kernels, half_logits(): pl.pallas_call(late_kernel if late else early_kernel, grid=(vocab_rows //...  21.6 us
    pallas_call x9, Pallas kernels, add_up(): pl.pallas_call(add_kernel, grid=(count,), in_specs=[block(first) for _, f...  19.1 us
    all_to_all x1, blocking collectives, body(): stats = lax.all_to_all(stats, VOCAB, 0, 0, tiled=True)  16.8 us
    pallas_call x2, Pallas kernels, half_grads(): pl.pallas_call(grad_kernel, grid=(4,), in_specs=[pl.BlockSpec((width // 8...  16.4 us
    all_to_all x1, blocking collectives, small_stage(): lax.all_to_all(x, ALL, 0, 0, axis_index_groups=SMALL_CUBES, tiled=True)  16.2 us
    ppermute x9, waiting for transfers between devices, summed_groups(): trade = lambda x, g, step: lax.ppermute(x, ALL, LARGE_PAIRS[(g + step) % 3])  15.6 us
    pallas_call x1, Pallas kernels, turned_weights(): pl.pallas_call(turn_kernel, grid_spec=pltpu.PrefetchScalarGridSpec(num_sc...  15.2 us
  transfers between devices with their start and end apart: 24, of which 6 were waited for; matrix products, arithmetic and copies ran while one was open for 7% of the time, Pallas kernels for 30%

profile of v1, /device:TPU:0, one launch (start us, length us, event | category | flops | bytes accessed | tf_op | source)
XLA Modules:
  0.0 206.1 jit_solution(8623027064314506405)
XLA Ops:
  0.6 1.0 broadcast_in_dim.12
  1.7 16.2 %all_to_all.15 = bf16[8,64,1024]{2,1,0:T(8,128)(2,1)S(1)} all-to-all(bf16[8,64,1024]{2,1,0:T(8,128)(2,1)S(1)} %broadcast_in_dim.12), channel_id=1, replica_groups={{0,2,8,10,32,34,40,42},{4,6,12,14,36,38,44,46},{16,18,24,26,48,50,56,58..., dimensions={0} | all-to-all | bytes 2097152 | tf_op jit(solution)/shard_map/all_to_all | solution.py:82
  17.9 2.1 %collective-permute-start = (bf16[176,1024]{1,0:T(8,128)(2,1)S(1)}, bf16[176,1024]{1,0:T(8,128)(2,1)S(1)}, u32[]{:S(2)}, u32[]{:S(2)}) collective-permute-start(bf16[176,1024]{1,0:T(8,128)(2,1)S(1)} %get-tuple-element.29), channel_id=1, source_target_pairs={{0,96},{1,33},{2,98},{3,35},{4,100},{5,37},{6,102},{7,39},{8,104},... | collective-permute-start | bytes 1081352 | tf_op jit(solution)/shard_map/ppermute | solution.py:91
  20.0 2.7 %collective-permute-start.4 = (bf16[176,1024]{1,0:T(8,128)(2,1)S(1)}, bf16[176,1024]{1,0:T(8,128)(2,1)S(1)}, u32[]{:S(2)}, u32[]{:S(2)}) collective-permute-start(bf16[176,1024]{1,0:T(8,128)(2,1)S(1)} %get-tuple-element.28), channel_id=1, source_target_pairs={{0,24},{1,9},{2,26},{3,11},{4,28},{5,13},{6,30},{7,15},{8,16},{9,1... | collective-permute-start | bytes 1081352 | tf_op jit(solution)/shard_map/ppermute | solution.py:91
  22.7 1.9 collective-permute-start.8
  24.6 2.0 collective-permute-done
  26.7 1.0 pad_maximum_fusion.1.refs_0_
  27.6 2.7 %collective-permute-start.2 = (bf16[352,1024]{1,0:T(8,128)(2,1)}, bf16[352,1024]{1,0:T(8,128)(2,1)}, u32[]{:S(2)}, u32[]{:S(2)}) collective-permute-start(bf16[352,1024]{1,0:T(8,128)(2,1)} %pad_maximum_fusion.1.refs_0_), channel_id=1, source_target_pairs={{0,24},{1,9},{2,26},{3,11},{4,28},{5,13},{6,30},{7,15},{8,16},{9,1... | collective-permute-start | bytes 2162696 | tf_op jit(solution)/shard_map/ppermute | solution.py:91
  31.2 1.8 collective-permute-start.6
  33.1 2.1 %collective-permute-start.10 = (bf16[320,1024]{1,0:T(8,128)(2,1)S(1)}, bf16[320,1024]{1,0:T(8,128)(2,1)}, u32[]{:S(2)}, u32[]{:S(2)}) collective-permute-start(bf16[320,1024]{1,0:T(8,128)(2,1)S(1)} %pad_maximum_fusion.3.refs_4_.refs_8_), channel_id=1, source_target_pairs={{0,96},{1,33},{2,98},{3,35},{4,100},{5,37},{6,102},{7,39},{8,104},... | collective-permute-start | bytes 1966088 | tf_op jit(solution)/shard_map/ppermute | solution.py:91
  36.4 1.4 collective-permute-start.1
  37.8 7.2 %collective-permute-done.10.refs_5_.refs_9_ = bf16[320,1024]{1,0:T(8,128)(2,1)} collective-permute-done((bf16[320,1024]{1,0:T(8,128)(2,1)S(1)}, bf16[320,1024]{1,0:T(8,128)(2,1)}, u32[]{:S(2)}, u32[]{:S(2)}) %collective-permute-start.10) | collective-permute-done | bytes 655392 | tf_op jit(solution)/shard_map/ppermute | solution.py:91
  45.1 2.0 collective-permute-start.5
  47.3 2.7 %collective-permute-start.11 = (bf16[320,1024]{1,0:T(8,128)(2,1)}, bf16[320,1024]{1,0:T(8,128)(2,1)}, u32[]{:S(2)}, u32[]{:S(2)}) collective-permute-start(bf16[320,1024]{1,0:T(8,128)(2,1)} %collective-permute-done.10.refs_5_.refs_9_), channel_id=1, source_target_pairs={{0,24},{1,9},{2,26},{3,11},{4,28},{5,13},{6,30},{7,15},{8,16},{9,1... | collective-permute-start | bytes 1966088 | tf_op jit(solution)/shard_map/ppermute | solution.py:91
  50.0 1.8 collective-permute-start.3
  51.9 2.0 collective-permute-start.7
  53.9 15.2 %shard_map.84 = (bf16[1024,4096]{1,0:T(8,128)(2,1)}, bf16[4096,1024]{1,0:T(8,128)(2,1)}) custom-call(s32[192]{0:T(256)S(1)} %bitcast.16, bf16[1024,4096]{1,0:T(8,128)(2,1)} %w.1), custom_call_target="tpu_custom_call" | custom-call | flops 8589934592 | bytes 25165824 | tf_op jit(solution)/shard_map/pallas_call | solution.py:234
  69.7 9.9 %shard_map.85.refs_7_ = f32[1024,1024]{1,0:T(8,128)} custom-call(bf16[352,1024]{1,0:T(8,128)(2,1)} %pad_maximum_fusion.1.refs_0_, bf16[352,1024]{1,0:T(8,128)(2,1)} %collective-permute-done.2.refs_1_, bf16[352,1024]{1,0:T(8,128)(2,1)} %pad_maximum_fusion.2.refs_2_.refs_4_, bf16[352,1024]{1,0:T(8,128)(2,1)} %collective-permute-done.6.refs_3_.refs_5_, ...), custom_call_target="tpu_custom_call" | custom-call | flops 4294967296 | bytes 12582912 | tf_op jit(solution)/shard_map/pallas_call | solution.py:316
  79.7 11.7 %shard_map.86 = (f32[1024,1024]{1,0:T(8,128)}, f32[64,16,128]{2,1,0:T(8,128)}) custom-call(bf16[352,1024]{1,0:T(8,128)(2,1)} %collective-permute-done.1.refs_0_.refs_2_, bf16[352,1024]{1,0:T(8,128)(2,1)} %collective-permute-done.3.refs_1_.refs_3_, bf16[352,1024]{1,0:T(8,128)(2,1)} %collective-permute-done.5.refs_2_.refs_6_, ...), custom_call_target="tpu_custom_call" | custom-call | flops 4294967296 | bytes 12582912 | tf_op jit(solution)/shard_map/pallas_call | solution.py:316
  91.4 16.8 %all_to_all.16.stats = f32[64,16,128]{2,1,0:T(8,128)S(1)} all-to-all(f32[64,16,128]{2,1,0:T(8,128)} %get-tuple-element.17), channel_id=1, replica_groups=mesh['vocab_0'=4,'vocab_1'=4,'vocab_2'=4,'dp'=2] {'vocab_0','vocab_1','v..., dimensions={0} | all-to-all | bytes 1048576 | tf_op jit(solution)/shard_map/all_to_all | solution.py:429
  108.2 5.6 %shard_map.87 = (bf16[1024,1024]{1,0:T(8,128)(2,1)S(1)}, f32[1,1024]{1,0:T(1,128)}) custom-call(f32[64,16,128]{2,1,0:T(8,128)S(1)} %all_to_all.16.stats, f32[1024,1024]{1,0:T(8,128)} %get-tuple-element.18.logits, f32[1,1024]{1,0:T(1,128)S(1)} %bitcast.15, s32[1,1024]{1,0:T(1,128)S(1)} %bitcast.14), custom_call_target="tpu_custom_call" | custom-call | flops 8388608 | bytes 6291456 | tf_op jit(solution)/shard_map/pallas_call | solution.py:364
  113.8 1.3 copy-done.3
  115.1 8.2 %shard_map.89 = (bf16[4,176,1024]{2,1,0:T(8,128)(2,1)}, bf16[4,176,1024]{2,1,0:T(8,128)(2,1)}, bf16[4,160,1024]{2,1,0:T(8,128)(2,1)}) custom-call(bf16[4096,1024]{1,0:T(8,128)(2,1)} %get-tuple-element.20.tall, bf16[1024,1024]{1,0:T(8,128)(2,1)} %copy-done.3), custom_call_target="tpu_custom_call" | custom-call | flops 4294967296 | bytes 8388608 | tf_op jit(solution)/shard_map/pallas_call | solution.py:398
  124.8 1.4 collective-permute-start.18
  126.3 8.2 %shard_map.88 = (bf16[4,176,1024]{2,1,0:T(8,128)(2,1)}, bf16[4,176,1024]{2,1,0:T(8,128)(2,1)}, bf16[4,160,1024]{2,1,0:T(8,128)(2,1)}) custom-call(bf16[4096,1024]{1,0:T(8,128)(2,1)} %get-tuple-element.20.tall, bf16[1024,1024]{1,0:T(8,128)(2,1)} %copy-done.3), custom_call_target="tpu_custom_call" | custom-call | flops 4294967296 | bytes 8388608 | tf_op jit(solution)/shard_map/pallas_call | solution.py:398
  134.4 9.4 %collective-permute-done.12.refs_1_ = bf16[4,176,1024]{2,1,0:T(8,128)(2,1)} collective-permute-done((bf16[4,176,1024]{2,1,0:T(8,128)(2,1)}, bf16[4,176,1024]{2,1,0:T(8,128)(2,1)}, u32[]{:S(2)}, u32[]{:S(2)}) %collective-permute-start.12) | collective-permute-done | bytes 1441824 | tf_op jit(solution)/shard_map/ppermute | solution.py:130
  143.8 2.1 %shard_map.90 = bf16[2,176,1024]{2,1,0:T(8,128)(2,1)} custom-call(bf16[4,176,1024]{2,1,0:T(8,128)(2,1)} %get-tuple-element.22.refs_0_, bf16[4,176,1024]{2,1,0:T(8,128)(2,1)} %collective-permute-done.12.refs_1_), custom_call_target="tpu_custom_call" | custom-call | flops 720896 | bytes 2162688 | tf_op jit(solution)/shard_map/pallas_call | solution.py:113
  146.4 2.1 %shard_map.93 = bf16[2,176,1024]{2,1,0:T(8,128)(2,1)} custom-call(bf16[4,176,1024]{2,1,0:T(8,128)(2,1)} %get-tuple-element.24.refs_0_, bf16[4,176,1024]{2,1,0:T(8,128)(2,1)} %collective-permute-done.15.refs_1_), custom_call_target="tpu_custom_call" | custom-call | flops 720896 | bytes 2162688 | tf_op jit(solution)/shard_map/pallas_call | solution.py:113
  148.5 1.4 collective-permute-start.16
  150.0 2.1 %shard_map.96 = bf16[2,160,1024]{2,1,0:T(8,128)(2,1)} custom-call(bf16[4,160,1024]{2,1,0:T(8,128)(2,1)} %get-tuple-element.26.refs_0_, bf16[4,160,1024]{2,1,0:T(8,128)(2,1)} %collective-permute-done.18.refs_1_), custom_call_target="tpu_custom_call" | custom-call | flops 655360 | bytes 1966080 | tf_op jit(solution)/shard_map/pallas_call | solution.py:113
  152.0 1.1 collective-permute-start.19
  153.2 8.7 %shard_map.100 = f32[64,4096]{1,0:T(8,128)} custom-call(s32[192]{0:T(256)} %bitcast.17, bf16[352,1024]{1,0:T(8,128)(2,1)} %pad_maximum_fusion.1.refs_0_, bf16[352,1024]{1,0:T(8,128)(2,1)} %collective-permute-done.2.refs_1_, bf16[352,1024]{1,0:T(8,128)(2,1)} %collective-permute-done.1.refs_0_.refs_2_, ...), custom_call_target="tpu_custom_call" | custom-call | flops 536870912 | bytes 8388608 | tf_op jit(solution)/shard_map/pallas_call | solution.py:192
  162.4 2.1 %shard_map.91 = bf16[1,176,1024]{2,1,0:T(8,128)(2,1)} custom-call(bf16[4,176,1024]{2,1,0:T(8,128)(2,1)} %get-tuple-element.22.refs_0_, bf16[4,176,1024]{2,1,0:T(8,128)(2,1)} %collective-permute-done.12.refs_1_, bf16[2,176,1024]{2,1,0:T(8,128)(2,1)} %collective-permute-done.13.refs_2_), custom_call_target="tpu_custom_call" | custom-call | flops 540672 | bytes 1441792 | tf_op jit(solution)/shard_map/pallas_call | solution.py:113
  164.5 2.1 %collective-permute-start.14 = (bf16[1,176,1024]{2,1,0:T(8,128)(2,1)}, bf16[1,176,1024]{2,1,0:T(8,128)(2,1)}, u32[]{:S(2)}, u32[]{:S(2)}) collective-permute-start(bf16[1,176,1024]{2,1,0:T(8,128)(2,1)} %shard_map.91), channel_id=1, source_target_pairs={{0,96},{1,33},{2,98},{3,35},{4,100},{5,37},{6,102},{7,39},{8,104},... | collective-permute-start | bytes 1081352 | tf_op jit(solution)/shard_map/ppermute | solution.py:130
  166.6 2.1 %shard_map.94 = bf16[1,176,1024]{2,1,0:T(8,128)(2,1)} custom-call(bf16[4,176,1024]{2,1,0:T(8,128)(2,1)} %get-tuple-element.24.refs_0_, bf16[4,176,1024]{2,1,0:T(8,128)(2,1)} %collective-permute-done.15.refs_1_, bf16[2,176,1024]{2,1,0:T(8,128)(2,1)} %collective-permute-done.16.refs_2_), custom_call_target="tpu_custom_call" | custom-call | flops 540672 | bytes 1441792 | tf_op jit(solution)/shard_map/pallas_call | solution.py:113
  168.7 2.2 %collective-permute-start.17 = (bf16[1,176,1024]{2,1,0:T(8,128)(2,1)}, bf16[1,176,1024]{2,1,0:T(8,128)(2,1)}, u32[]{:S(2)}, u32[]{:S(2)}) collective-permute-start(bf16[1,176,1024]{2,1,0:T(8,128)(2,1)} %shard_map.94), channel_id=1, source_target_pairs={{0,24},{1,9},{2,26},{3,11},{4,28},{5,13},{6,30},{7,15},{8,16},{9,1... | collective-permute-start | bytes 1081352 | tf_op jit(solution)/shard_map/ppermute | solution.py:130
  170.9 2.0 shard_map.97
  172.9 2.4 %collective-permute-start.20 = (bf16[1,160,1024]{2,1,0:T(8,128)(2,1)}, bf16[1,160,1024]{2,1,0:T(8,128)(2,1)}, u32[]{:S(2)}, u32[]{:S(2)}) collective-permute-start(bf16[1,160,1024]{2,1,0:T(8,128)(2,1)} %shard_map.97), channel_id=1, source_target_pairs={{0,6},{1,3},{2,4},{3,1},{4,2},{5,7},{6,0},{7,5},{8,14},{9,11},{10,... | collective-permute-start | bytes 983048 | tf_op jit(solution)/shard_map/ppermute | solution.py:130
  175.3 6.2 %collective-permute-done.20.refs_3_ = bf16[1,160,1024]{2,1,0:T(8,128)(2,1)} collective-permute-done((bf16[1,160,1024]{2,1,0:T(8,128)(2,1)}, bf16[1,160,1024]{2,1,0:T(8,128)(2,1)}, u32[]{:S(2)}, u32[]{:S(2)}) %collective-permute-start.20) | collective-permute-done | bytes 327712 | tf_op jit(solution)/shard_map/ppermute | solution.py:130
  181.5 2.1 %shard_map.98 = bf16[1,160,1024]{2,1,0:T(8,128)(2,1)} custom-call(bf16[4,160,1024]{2,1,0:T(8,128)(2,1)} %get-tuple-element.26.refs_0_, bf16[4,160,1024]{2,1,0:T(8,128)(2,1)} %collective-permute-done.18.refs_1_, bf16[2,160,1024]{2,1,0:T(8,128)(2,1)} %collective-permute-done.19.refs_2_, bf16[1,160,1024]{2,1,0:T(8,128)(2,1)} %collective-permute-done.20.refs_3_), custom_call_target="tpu_custom_call" | custom-call | flops 655360 | bytes 1638400 | tf_op jit(solution)/shard_map/pallas_call | solution.py:113
  183.6 2.2 %shard_map.92 = bf16[1,176,1024]{2,1,0:T(8,128)(2,1)} custom-call(bf16[4,176,1024]{2,1,0:T(8,128)(2,1)} %get-tuple-element.22.refs_0_, bf16[4,176,1024]{2,1,0:T(8,128)(2,1)} %collective-permute-done.12.refs_1_, bf16[2,176,1024]{2,1,0:T(8,128)(2,1)} %collective-permute-done.13.refs_2_, bf16[1,176,1024]{2,1,0:T(8,128)(2,1)} %collective-permute-done.14.refs_3_), custom_call_target="tpu_custom_call" | custom-call | flops 720896 | bytes 1802240 | tf_op jit(solution)/shard_map/pallas_call | solution.py:113
  185.9 2.2 %shard_map.95 = bf16[1,176,1024]{2,1,0:T(8,128)(2,1)} custom-call(bf16[4,176,1024]{2,1,0:T(8,128)(2,1)} %get-tuple-element.24.refs_0_, bf16[4,176,1024]{2,1,0:T(8,128)(2,1)} %collective-permute-done.15.refs_1_, bf16[2,176,1024]{2,1,0:T(8,128)(2,1)} %collective-permute-done.16.refs_2_, bf16[1,176,1024]{2,1,0:T(8,128)(2,1)} %collective-permute-done.17.refs_3_), custom_call_target="tpu_custom_call" | custom-call | flops 720896 | bytes 1802240 | tf_op jit(solution)/shard_map/pallas_call | solution.py:113
  188.1 2.3 %pad_maximum_fusion = bf16[512,1024]{1,0:T(8,128)(2,1)} fusion(bf16[160,1024]{1,0:T(8,128)(2,1)} %bitcast.22, bf16[176,1024]{1,0:T(8,128)(2,1)} %bitcast.21, bf16[176,1024]{1,0:T(8,128)(2,1)} %bitcast.20), kind=kLoop, calls=%fused_computation.1 | loop fusion | flops 3145728 | bytes 2097152 | tf_op jit(solution)/shard_map/concatenate | solution.py:136
  190.4 3.6 %all-to-all-start.2 = ((bf16[8,64,1024]{2,1,0:T(8,128)(2,1)}), bf16[8,64,1024]{2,1,0:T(8,128)(2,1)S(1)}, u32[]{:S(2)}, u32[]{:S(2)}) async-start(bf16[8,64,1024]{2,1,0:T(8,128)(2,1)} %bitcast.9), calls=%async_computation.2 | async-start | bytes 2097152 | tf_op jit(solution)/shard_map/all_to_all | solution.py:82
  194.0 2.3 %add_multiply_fusion.1 = f32[64,4096]{1,0:T(8,128)} fusion(f32[64,4096]{1,0:T(8,128)S(1)} %copy-done.6, f32[64,4096]{1,0:T(8,128)} %collective-permute-done.22), kind=kLoop, calls=%fused_computation.2 | loop fusion | flops 524288 | bytes 3145728 | tf_op jit(solution)/shard_map/div | solution.py:442
  196.3 3.3 %fusion = f32[512,1024]{1,0:T(8,128)S(1)} fusion(bf16[1024,1024]{1,0:T(8,128)(2,1)} %collective-permute-done.21, s32[]{:T(128)S(6)} %select_n.9), kind=kOutput, calls=%fused_computation.3 | convolution fusion | flops 1073741824 | bytes 5242884 | tf_op jit(solution)/shard_map/dot_general | solution.py:439
  199.7 2.6 %add_multiply_fusion = f32[512,1024]{1,0:T(8,128)} fusion(f32[512,1024]{1,0:T(8,128)S(1)} %fusion, bf16[1024,1024]{1,0:T(8,128)(2,1)S(1)} %copy-done.4, s32[]{:T(128)S(6)} %select_n.9), kind=kOutput, calls=%fused_computation | convolution fusion | flops 1074790400 | bytes 7340036 | tf_op jit(solution)/shard_map/dot_general | solution.py:439
  202.3 2.9 %all-to-all-done.2.pieces = bf16[8,64,1024]{2,1,0:T(8,128)(2,1)S(1)} async-done(((bf16[8,64,1024]{2,1,0:T(8,128)(2,1)}), bf16[8,64,1024]{2,1,0:T(8,128)(2,1)S(1)}, u32[]{:S(2)}, u32[]{:S(2)}) %all-to-all-start.2) | async-done | bytes 1048608 | tf_op jit(solution)/shard_map/all_to_all | solution.py:82
  (49 shorter events, 6.7 us)
Async XLA Ops:
  17.9 8.7 %collective-permute-start = (bf16[176,1024]{1,0:T(8,128)(2,1)S(1)}, bf16[176,1024]{1,0:T(8,128)(2,1)S(1)}, u32[]{:S(2)}, u32[]{:S(2)}) collective-permute-start(bf16[176,1024]{1,0:T(8,128)(2,1)S(1)} %get-tuple-element.29), channel_id=1, source_target_pairs={{0,96},{1,33},{2,98},{3,35},{4,100},{5,37},{6,102},{7,39},{8,104},... | collective-permute-start | bytes 1081352 | tf_op jit(solution)/shard_map/ppermute | solution.py:91
  20.0 10.3 %collective-permute-start.4 = (bf16[176,1024]{1,0:T(8,128)(2,1)S(1)}, bf16[176,1024]{1,0:T(8,128)(2,1)S(1)}, u32[]{:S(2)}, u32[]{:S(2)}) collective-permute-start(bf16[176,1024]{1,0:T(8,128)(2,1)S(1)} %get-tuple-element.28), channel_id=1, source_target_pairs={{0,24},{1,9},{2,26},{3,11},{4,28},{5,13},{6,30},{7,15},{8,16},{9,1... | collective-permute-start | bytes 1081352 | tf_op jit(solution)/shard_map/ppermute | solution.py:91
  22.7 10.3 %collective-permute-start.8 = (bf16[160,1024]{1,0:T(8,128)(2,1)S(1)}, bf16[160,1024]{1,0:T(8,128)(2,1)S(1)}, u32[]{:S(2)}, u32[]{:S(2)}) collective-permute-start(bf16[160,1024]{1,0:T(8,128)(2,1)S(1)} %slice.14), channel_id=1, source_target_pairs={{0,6},{1,3},{2,4},{3,1},{4,2},{5,7},{6,0},{7,5},{8,14},{9,11},{10,... | collective-permute-start | bytes 983048 | tf_op jit(solution)/shard_map/ppermute | solution.py:91
  27.6 22.4 %collective-permute-start.2 = (bf16[352,1024]{1,0:T(8,128)(2,1)}, bf16[352,1024]{1,0:T(8,128)(2,1)}, u32[]{:S(2)}, u32[]{:S(2)}) collective-permute-start(bf16[352,1024]{1,0:T(8,128)(2,1)} %pad_maximum_fusion.1.refs_0_), channel_id=1, source_target_pairs={{0,24},{1,9},{2,26},{3,11},{4,28},{5,13},{6,30},{7,15},{8,16},{9,1... | collective-permute-start | bytes 2162696 | tf_op jit(solution)/shard_map/ppermute | solution.py:91
  31.2 20.7 %collective-permute-start.6 = (bf16[352,1024]{1,0:T(8,128)(2,1)}, bf16[352,1024]{1,0:T(8,128)(2,1)}, u32[]{:S(2)}, u32[]{:S(2)}) collective-permute-start(bf16[352,1024]{1,0:T(8,128)(2,1)} %pad_maximum_fusion.2.refs_2_.refs_4_), channel_id=1, source_target_pairs={{0,6},{1,3},{2,4},{3,1},{4,2},{5,7},{6,0},{7,5},{8,14},{9,11},{10,... | collective-permute-start | bytes 2162696 | tf_op jit(solution)/shard_map/ppermute | solution.py:91
  33.1 36.0 %copy-start.5 = (bf16[320,1024]{1,0:T(8,128)(2,1)}, bf16[320,1024]{1,0:T(8,128)(2,1)S(1)}, u32[]{:S(2)}) copy-start(bf16[320,1024]{1,0:T(8,128)(2,1)S(1)} %pad_maximum_fusion.3.refs_4_.refs_8_) | copy-start | bytes 1966084
  33.1 12.0 %collective-permute-start.10 = (bf16[320,1024]{1,0:T(8,128)(2,1)S(1)}, bf16[320,1024]{1,0:T(8,128)(2,1)}, u32[]{:S(2)}, u32[]{:S(2)}) collective-permute-start(bf16[320,1024]{1,0:T(8,128)(2,1)S(1)} %pad_maximum_fusion.3.refs_4_.refs_8_), channel_id=1, source_target_pairs={{0,96},{1,33},{2,98},{3,35},{4,100},{5,37},{6,102},{7,39},{8,104},... | collective-permute-start | bytes 1966088 | tf_op jit(solution)/shard_map/ppermute | solution.py:91
  35.2 12.2 %collective-permute-start.9 = (bf16[320,1024]{1,0:T(8,128)(2,1)S(1)}, bf16[320,1024]{1,0:T(8,128)(2,1)S(1)}, u32[]{:S(2)}, u32[]{:S(2)}) collective-permute-start(bf16[320,1024]{1,0:T(8,128)(2,1)S(1)} %pad_maximum_fusion.3.refs_4_.refs_8_), channel_id=1, source_target_pairs={{0,24},{1,9},{2,26},{3,11},{4,28},{5,13},{6,30},{7,15},{8,16},{9,1... | collective-permute-start | bytes 1966088 | tf_op jit(solution)/shard_map/ppermute | solution.py:91
  36.4 32.6 %copy-start.2 = (s32[1,192]{1,0:T(1,128)}, s32[1,192]{1,0:T(1,128)S(1)}, u32[]{:S(2)}) copy-start(s32[1,192]{1,0:T(1,128)S(1)} %constant_dynamic-slice_fusion) | copy-start | bytes 2308
  36.4 43.1 %collective-permute-start.1 = (bf16[352,1024]{1,0:T(8,128)(2,1)}, bf16[352,1024]{1,0:T(8,128)(2,1)}, u32[]{:S(2)}, u32[]{:S(2)}) collective-permute-start(bf16[352,1024]{1,0:T(8,128)(2,1)} %pad_maximum_fusion.1.refs_0_), channel_id=1, source_target_pairs={{0,6},{1,3},{2,4},{3,1},{4,2},{5,7},{6,0},{7,5},{8,14},{9,11},{10,... | collective-permute-start | bytes 2162696 | tf_op jit(solution)/shard_map/ppermute | solution.py:91
  45.1 34.5 %collective-permute-start.5 = (bf16[352,1024]{1,0:T(8,128)(2,1)}, bf16[352,1024]{1,0:T(8,128)(2,1)}, u32[]{:S(2)}, u32[]{:S(2)}) collective-permute-start(bf16[352,1024]{1,0:T(8,128)(2,1)} %pad_maximum_fusion.2.refs_2_.refs_4_), channel_id=1, source_target_pairs={{0,96},{1,33},{2,98},{3,35},{4,100},{5,37},{6,102},{7,39},{8,104},... | collective-permute-start | bytes 2162696 | tf_op jit(solution)/shard_map/ppermute | solution.py:91
  47.3 21.7 %copy-start.7 = (bf16[320,1024]{1,0:T(8,128)(2,1)}, bf16[320,1024]{1,0:T(8,128)(2,1)S(1)}, u32[]{:S(2)}) copy-start(bf16[320,1024]{1,0:T(8,128)(2,1)S(1)} %collective-permute-done.9.refs_4_.refs_10_) | copy-start | bytes 1966084
  47.3 32.3 %collective-permute-start.11 = (bf16[320,1024]{1,0:T(8,128)(2,1)}, bf16[320,1024]{1,0:T(8,128)(2,1)}, u32[]{:S(2)}, u32[]{:S(2)}) collective-permute-start(bf16[320,1024]{1,0:T(8,128)(2,1)} %collective-permute-done.10.refs_5_.refs_9_), channel_id=1, source_target_pairs={{0,24},{1,9},{2,26},{3,11},{4,28},{5,13},{6,30},{7,15},{8,16},{9,1... | collective-permute-start | bytes 1966088 | tf_op jit(solution)/shard_map/ppermute | solution.py:91
  50.0 29.6 %collective-permute-start.3 = (bf16[352,1024]{1,0:T(8,128)(2,1)}, bf16[352,1024]{1,0:T(8,128)(2,1)}, u32[]{:S(2)}, u32[]{:S(2)}) collective-permute-start(bf16[352,1024]{1,0:T(8,128)(2,1)} %collective-permute-done.2.refs_1_), channel_id=1, source_target_pairs={{0,6},{1,3},{2,4},{3,1},{4,2},{5,7},{6,0},{7,5},{8,14},{9,11},{10,... | collective-permute-start | bytes 2162696 | tf_op jit(solution)/shard_map/ppermute | solution.py:91
  51.9 27.8 %collective-permute-start.7 = (bf16[352,1024]{1,0:T(8,128)(2,1)}, bf16[352,1024]{1,0:T(8,128)(2,1)}, u32[]{:S(2)}, u32[]{:S(2)}) collective-permute-start(bf16[352,1024]{1,0:T(8,128)(2,1)} %collective-permute-done.6.refs_3_.refs_5_), channel_id=1, source_target_pairs={{0,96},{1,33},{2,98},{3,35},{4,100},{5,37},{6,102},{7,39},{8,104},... | collective-permute-start | bytes 2162696 | tf_op jit(solution)/shard_map/ppermute | solution.py:91
  53.9 15.2 %copy-start.8 = (s32[1024]{0:T(1024)S(1)}, s32[1024]{0:T(1024)}, u32[]{:S(2)}) copy-start(s32[1024]{0:T(1024)} %param.7) | copy-start | bytes 12292
  79.6 28.5 %copy-start = (s32[1024]{0:T(1024)S(1)}, s32[1024]{0:T(1024)}, u32[]{:S(2)}) copy-start(s32[1024]{0:T(1024)} %broadcast_subtract_fusion) | copy-start | bytes 12292
  79.6 28.5 %copy-start.1 = (f32[1024]{0:T(1024)S(1)}, f32[1024]{0:T(1024)}, u32[]{:S(2)}) copy-start(f32[1024]{0:T(1024)} %param.8) | copy-start | bytes 12292
  113.8 1.3 copy-start.3
  123.3 20.5 %collective-permute-start.12 = (bf16[4,176,1024]{2,1,0:T(8,128)(2,1)}, bf16[4,176,1024]{2,1,0:T(8,128)(2,1)}, u32[]{:S(2)}, u32[]{:S(2)}) collective-permute-start(bf16[4,176,1024]{2,1,0:T(8,128)(2,1)} %get-tuple-element.23), channel_id=1, source_target_pairs={{0,6},{1,3},{2,4},{3,1},{4,2},{5,7},{6,0},{7,5},{8,14},{9,11},{10,... | collective-permute-start | bytes 4325384 | tf_op jit(solution)/shard_map/ppermute | solution.py:130
  124.1 22.3 %collective-permute-start.15 = (bf16[4,176,1024]{2,1,0:T(8,128)(2,1)}, bf16[4,176,1024]{2,1,0:T(8,128)(2,1)}, u32[]{:S(2)}, u32[]{:S(2)}) collective-permute-start(bf16[4,176,1024]{2,1,0:T(8,128)(2,1)} %get-tuple-element.25), channel_id=1, source_target_pairs={{0,96},{1,33},{2,98},{3,35},{4,100},{5,37},{6,102},{7,39},{8,104},... | collective-permute-start | bytes 4325384 | tf_op jit(solution)/shard_map/ppermute | solution.py:130
  124.8 25.1 %collective-permute-start.18 = (bf16[4,160,1024]{2,1,0:T(8,128)(2,1)}, bf16[4,160,1024]{2,1,0:T(8,128)(2,1)}, u32[]{:S(2)}, u32[]{:S(2)}) collective-permute-start(bf16[4,160,1024]{2,1,0:T(8,128)(2,1)} %get-tuple-element.27), channel_id=1, source_target_pairs={{0,24},{1,9},{2,26},{3,11},{4,28},{5,13},{6,30},{7,15},{8,16},{9,1... | collective-permute-start | bytes 3932168 | tf_op jit(solution)/shard_map/ppermute | solution.py:130
  145.9 16.5 %collective-permute-start.13 = (bf16[2,176,1024]{2,1,0:T(8,128)(2,1)}, bf16[2,176,1024]{2,1,0:T(8,128)(2,1)}, u32[]{:S(2)}, u32[]{:S(2)}) collective-permute-start(bf16[2,176,1024]{2,1,0:T(8,128)(2,1)} %shard_map.90), channel_id=1, source_target_pairs={{0,24},{1,9},{2,26},{3,11},{4,28},{5,13},{6,30},{7,15},{8,16},{9,1... | collective-permute-start | bytes 2162696 | tf_op jit(solution)/shard_map/ppermute | solution.py:130
  148.5 18.1 %collective-permute-start.16 = (bf16[2,176,1024]{2,1,0:T(8,128)(2,1)}, bf16[2,176,1024]{2,1,0:T(8,128)(2,1)}, u32[]{:S(2)}, u32[]{:S(2)}) collective-permute-start(bf16[2,176,1024]{2,1,0:T(8,128)(2,1)} %shard_map.93), channel_id=1, source_target_pairs={{0,6},{1,3},{2,4},{3,1},{4,2},{5,7},{6,0},{7,5},{8,14},{9,11},{10,... | collective-permute-start | bytes 2162696 | tf_op jit(solution)/shard_map/ppermute | solution.py:130
  152.0 18.8 %collective-permute-start.19 = (bf16[2,160,1024]{2,1,0:T(8,128)(2,1)}, bf16[2,160,1024]{2,1,0:T(8,128)(2,1)}, u32[]{:S(2)}, u32[]{:S(2)}) collective-permute-start(bf16[2,160,1024]{2,1,0:T(8,128)(2,1)} %shard_map.96), channel_id=1, source_target_pairs={{0,96},{1,33},{2,98},{3,35},{4,100},{5,37},{6,102},{7,39},{8,104},... | collective-permute-start | bytes 1966088 | tf_op jit(solution)/shard_map/ppermute | solution.py:130
  153.2 43.2 %collective-permute-start.21 = (bf16[1024,1024]{1,0:T(8,128)(2,1)}, bf16[1024,1024]{1,0:T(8,128)(2,1)}, u32[]{:S(2)}, u32[]{:S(2)}) collective-permute-start(bf16[1024,1024]{1,0:T(8,128)(2,1)} %copy-done.3), channel_id=1, source_target_pairs={{0,1},{1,0},{2,3},{3,2},{4,5},{5,4},{6,7},{7,6},{8,9},{9,8},{10,11... | collective-permute-start | bytes 6291464 | tf_op jit(solution)/shard_map/ppermute | solution.py:441
  161.8 32.2 %collective-permute-start.22 = (f32[64,4096]{1,0:T(8,128)}, f32[64,4096]{1,0:T(8,128)}, u32[]{:S(2)}, u32[]{:S(2)}) collective-permute-start(f32[64,4096]{1,0:T(8,128)} %shard_map.100), channel_id=1, source_target_pairs={{0,1},{1,0},{2,3},{3,2},{4,5},{5,4},{6,7},{7,6},{8,9},{9,8},{10,11... | collective-permute-start | bytes 3145736 | tf_op jit(solution)/shard_map/ppermute | solution.py:442
  164.5 19.1 %collective-permute-start.14 = (bf16[1,176,1024]{2,1,0:T(8,128)(2,1)}, bf16[1,176,1024]{2,1,0:T(8,128)(2,1)}, u32[]{:S(2)}, u32[]{:S(2)}) collective-permute-start(bf16[1,176,1024]{2,1,0:T(8,128)(2,1)} %shard_map.91), channel_id=1, source_target_pairs={{0,96},{1,33},{2,98},{3,35},{4,100},{5,37},{6,102},{7,39},{8,104},... | collective-permute-start | bytes 1081352 | tf_op jit(solution)/shard_map/ppermute | solution.py:130
  168.7 17.2 %collective-permute-start.17 = (bf16[1,176,1024]{2,1,0:T(8,128)(2,1)}, bf16[1,176,1024]{2,1,0:T(8,128)(2,1)}, u32[]{:S(2)}, u32[]{:S(2)}) collective-permute-start(bf16[1,176,1024]{2,1,0:T(8,128)(2,1)} %shard_map.94), channel_id=1, source_target_pairs={{0,24},{1,9},{2,26},{3,11},{4,28},{5,13},{6,30},{7,15},{8,16},{9,1... | collective-permute-start | bytes 1081352 | tf_op jit(solution)/shard_map/ppermute | solution.py:130
  172.9 8.6 %collective-permute-start.20 = (bf16[1,160,1024]{2,1,0:T(8,128)(2,1)}, bf16[1,160,1024]{2,1,0:T(8,128)(2,1)}, u32[]{:S(2)}, u32[]{:S(2)}) collective-permute-start(bf16[1,160,1024]{2,1,0:T(8,128)(2,1)} %shard_map.97), channel_id=1, source_target_pairs={{0,6},{1,3},{2,4},{3,1},{4,2},{5,7},{6,0},{7,5},{8,14},{9,11},{10,... | collective-permute-start | bytes 983048 | tf_op jit(solution)/shard_map/ppermute | solution.py:130
  188.1 5.9 %copy-start.6 = (f32[64,4096]{1,0:T(8,128)S(1)}, f32[64,4096]{1,0:T(8,128)}, u32[]{:S(2)}) copy-start(f32[64,4096]{1,0:T(8,128)} %shard_map.100) | copy-start | bytes 3145732
  190.4 14.7 %all-to-all-start.2 = ((bf16[8,64,1024]{2,1,0:T(8,128)(2,1)}), bf16[8,64,1024]{2,1,0:T(8,128)(2,1)S(1)}, u32[]{:S(2)}, u32[]{:S(2)}) async-start(bf16[8,64,1024]{2,1,0:T(8,128)(2,1)} %bitcast.9), calls=%async_computation.2 | async-start | bytes 2097152 | tf_op jit(solution)/shard_map/all_to_all | solution.py:82
  196.3 3.4 %copy-start.4 = (bf16[1024,1024]{1,0:T(8,128)(2,1)S(1)}, bf16[1024,1024]{1,0:T(8,128)(2,1)}, u32[]{:S(2)}) copy-start(bf16[1024,1024]{1,0:T(8,128)(2,1)} %copy-done.3) | copy-start | bytes 6291460

commit v2 on v1

--- a/solution.py
+++ b/solution.py
@@ -126,16 +126,45 @@
     )(*[in_hbm(x) for x, _ in terms])
 
 
+def last_kernel(*refs):
+    *terms, out = refs
+    for g in range(3):
+        total = terms[4 * g][...].astype(F32)
+        for term in terms[4 * g + 1 : 4 * g + 4]:
+            total = total + term[...].astype(F32)
+        out[STARTS[g] : STARTS[g] + SIZES[g]] = total.astype(BF16)
+
+
+def add_last(terms):
+    tokens = terms[0].shape[2]
+    part = tokens // 2
+    return pl.pallas_call(
+        last_kernel,
+        grid=(2,),
+        in_specs=[
+            pl.BlockSpec((None, x.shape[1], part), lambda i: (0, 0, i)) for x in terms
+        ],
+        out_specs=pl.BlockSpec((sum(SIZES), part), lambda i: (0, i)),
+        out_shape=jax.ShapeDtypeStruct((sum(SIZES), tokens), BF16),
+        compiler_params=pltpu.CompilerParams(
+            dimension_semantics=("arbitrary",), vmem_limit_bytes=ALL_VMEM
+        ),
+        cost_estimate=pl.CostEstimate(
+            flops=4 * sum(SIZES) * tokens, bytes_accessed=10 * sum(SIZES) * tokens, transcendentals=0
+        ),
+    )(*[in_hbm(x) for x in terms])
+
+
 def summed_groups(sends, keeps):
-    trade = lambda x, g, step: lax.ppermute(x, ALL, LARGE_PAIRS[(g + step) % 3])
+    def trade(x, g, step):
+        return lax.ppermute(x, ALL, LARGE_PAIRS[(g + step) % 3])
+
     far = [trade(sends[g], g, 2) for g in range(3)]
     mid = [trade(add_up(2, (keeps[g], 2), (far[g], 2)), g, 1) for g in range(3)]
     near = [
         trade(add_up(1, (keeps[g], 1), (far[g], 1), (mid[g], 1)), g, 0) for g in range(3)
     ]
-    return jnp.concatenate(
-        [add_up(1, (keeps[g], 0), (far[g], 0), (mid[g], 0), (near[g], 0))[0] for g in range(3)]
-    )
+    return add_last([x for g in range(3) for x in (keeps[g], far[g], mid[g], near[g])])
 
 
 def sum_kernel(pieces, out):
@@ -337,10 +366,12 @@
     )(*got, in_hbm(wide), *([in_hbm(part), tgt] if late else []))
 
 
-def signal_kernel(stats, logits, cot, tgt, grad, loss, row):
+def signal_kernel(stats, logits, cot, tgt, tall, grad, loss, *refs):
+    outs, (row, whole) = refs[:3], refs[3:]
     step = pl.program_id(0)
     rows, tokens = logits.shape
     lines = tokens // 128
+    count = whole.shape[0] // rows
 
     @pl.when(step == 0)
     def _():
@@ -351,39 +382,57 @@
         row[...] = jnp.concatenate([full[k : k + 1] for k in range(lines)], axis=1)
         loss[...] = jnp.concatenate([tok[k : k + 1] for k in range(lines)], axis=1)
 
-    block = logits[...]
-    at = lax.broadcasted_iota(jnp.int32, block.shape, 0) + step * rows
-    one = jnp.where(at == tgt[...], F32(1.0), F32(0.0))
-    grad[...] = (cot[...] * (jnp.exp(block - row[...]) - one)).astype(BF16)
-
-
-def signal_of(stats, logits, cot, tgt):
+    @pl.when(step < count)
+    def _():
+        block = logits[...]
+        at = lax.broadcasted_iota(jnp.int32, block.shape, 0) + step * rows
+        one = jnp.where(at == tgt[...], F32(1.0), F32(0.0))
+        done = (cot[...] * (jnp.exp(block - row[...]) - one)).astype(BF16)
+        grad[...] = done
+        whole[pl.ds(pl.multiple_of(step * rows, rows), rows)] = done
+
+    @pl.when(step >= count)
+    def _():
+        block = jnp.dot(tall[...], whole[...], preferred_element_type=F32).astype(BF16)
+        for start, size, out in zip(STARTS, SIZES, outs):
+            out[...] = block[start : start + size]
+
+
+def signal_of(stats, logits, cot, tgt, tall):
     vocab_rows, tokens = logits.shape
-    rows = 128
+    width = tall.shape[0]
+    rows = 256
+    count = vocab_rows // rows
+    early = lambda i: jnp.minimum(i, count - 1)
+    late = lambda i: jnp.maximum(i - count, 0)
     whole = lambda *shape: pl.BlockSpec(shape, lambda i: (0,) * len(shape))
-    return pl.pallas_call(
+    grad, loss, *sums = pl.pallas_call(
         signal_kernel,
-        grid=(vocab_rows // rows,),
+        grid=(count + 4,),
         in_specs=[
             whole(*stats.shape),
-            pl.BlockSpec((rows, tokens), lambda i: (i, 0)),
+            pl.BlockSpec((rows, tokens), lambda i: (early(i), 0)),
             whole(1, tokens),
             whole(1, tokens),
+            pl.BlockSpec((width // 8, vocab_rows), lambda i: (4 + late(i), 0)),
         ],
-        out_specs=[pl.BlockSpec((rows, tokens), lambda i: (i, 0)), whole(1, tokens)],
+        out_specs=[pl.BlockSpec((rows, tokens), lambda i: (early(i), 0)), whole(1, tokens)]
+        + [pl.BlockSpec((None, size, tokens), lambda i: (late(i), 0, 0)) for size in SIZES],
         out_shape=[
-            jax.ShapeDtypeStruct((vocab_rows, tokens), BF16),
+            pltpu.HBM((vocab_rows, tokens), BF16),
             jax.ShapeDtypeStruct((1, tokens), F32),
-        ],
-        scratch_shapes=[pltpu.VMEM((1, tokens), F32)],
-        compiler_params=pltpu.CompilerParams(
-            dimension_semantics=("arbitrary",), vmem_limit_bytes=16 << 20
-        ),
-        cost_estimate=pl.CostEstimate(
-            flops=8 * vocab_rows * tokens, bytes_accessed=6 * vocab_rows * tokens,
+        ] + [pltpu.HBM((4, size, tokens), BF16) for size in SIZES],
+        scratch_shapes=[pltpu.VMEM((1, tokens), F32), pltpu.VMEM((vocab_rows, tokens), BF16)],
+        compiler_params=pltpu.CompilerParams(
+            dimension_semantics=("arbitrary",), vmem_limit_bytes=ALL_VMEM
+        ),
+        cost_estimate=pl.CostEstimate(
+            flops=vocab_rows * width * tokens,
+            bytes_accessed=6 * vocab_rows * tokens + width * (vocab_rows + tokens),
             transcendentals=vocab_rows * tokens,
         ),
-    )(stats, in_hbm(logits), cot, tgt)
+    )(stats, in_hbm(logits), cot, tgt, in_hbm(tall))
+    return grad, loss, sums
 
 
 def grad_kernel(tall, grad, *outs):
@@ -428,8 +477,8 @@
     logits, stats = half_logits(1, [a for group in got for a in group[2:]], wide, part, tgt)
     stats = lax.all_to_all(stats, VOCAB, 0, 0, tiled=True)
     a_part = a_part_of(chips, [a for group in got for a in group], own)
-    grad, tok_loss = signal_of(stats, logits, loss_cot[None, :], tgt)
-    sums = summed_groups(half_grads(1, tall, grad), half_grads(0, tall, grad))
+    grad, tok_loss, sends = signal_of(stats, logits, loss_cot[None, :], tgt, tall)
+    sums = summed_groups(sends, half_grads(0, tall, grad))
     sums = small_stage(sums.reshape(8, feats, tokens))
     hidden_grad = summed(sums).T
     rows = vocab_rows // 2

time: 207 us -> 202 us (0.976)
  Pallas kernels: 87.4 us -> 81.7 us
  waiting for transfers between devices: 28 us -> 31 us
  other arithmetic: 7.14 us -> 4.82 us
    pallas_call x1 -> x2, Pallas kernels: 5.59 us -> 14.8 us  [the longest x1 11.4 us: signal_of(): pl.pallas_call(signal_kernel, grid=(count + 4,), in_specs=[whole(*stats.s...]
    pallas_call x2 -> x1, Pallas kernels: 16.4 us -> 8.2 us  [half_grads(): pl.pallas_call(grad_kernel, grid=(4,), in_specs=[pl.BlockSpec((width // 8...]
    pallas_call x9 -> x6, Pallas kernels: 19.1 us -> 12.6 us  [add_up(): pl.pallas_call(add_kernel, grid=(count,), in_specs=[block(first) for _, f...]
    ppermute x9, waiting for transfers between devices: 15.6 us -> 18.6 us  [trade(): return lax.ppermute(x, ALL, LARGE_PAIRS[(g + step) % 3])]
    concatenate x1 -> x0, other arithmetic: 2.33 us -> none  [summed_groups(): jnp.concatenate([add_up(1, (keeps[g], 0), (far[g], 0), (mid[g], 0), (near...]
  transfers between devices with their start and end apart: 24 -> 24, of which waited for: 6 -> 7; matrix products, arithmetic and copies ran while one was open for 7% -> 6% of each run, Pallas kernels for 30% -> 29%
where the time goes in v2:
time: 202 us; the launch traced here: 200 us
  Pallas kernels  81.7 us (40%)
  starting transfers between devices  39.6 us (20%)
  blocking collectives  33.7 us (17%)
  waiting for transfers between devices  31 us (15%)
  matrix products  5.96 us (3%)
  other arithmetic  4.82 us (2%)
    ppermute x12, starting transfers between devices, get(): return lax.ppermute(x, ALL, LARGE_PAIRS[(g + step) % 3])  23.7 us
    pallas_call x2, Pallas kernels, half_logits(): pl.pallas_call(late_kernel if late else early_kernel, grid=(vocab_rows //...  21.5 us
    ppermute x9, waiting for transfers between devices, trade(): return lax.ppermute(x, ALL, LARGE_PAIRS[(g + step) % 3])  18.6 us
    all_to_all x1, blocking collectives, body(): stats = lax.all_to_all(stats, VOCAB, 0, 0, tiled=True)  17.5 us
    all_to_all x1, blocking collectives, small_stage(): lax.all_to_all(x, ALL, 0, 0, axis_index_groups=SMALL_CUBES, tiled=True)  16.2 us
    pallas_call x1, Pallas kernels, turned_weights(): pl.pallas_call(turn_kernel, grid_spec=pltpu.PrefetchScalarGridSpec(num_sc...  15.2 us
    pallas_call x6, Pallas kernels, add_up(): pl.pallas_call(add_kernel, grid=(count,), in_specs=[block(first) for _, f...  12.6 us
    ppermute x9, starting transfers between devices, trade(): return lax.ppermute(x, ALL, LARGE_PAIRS[(g + step) % 3])  12.1 us
  transfers between devices with their start and end apart: 24, of which 7 were waited for; matrix products, arithmetic and copies ran while one was open for 6% of the time, Pallas kernels for 29%

profile of v2, /device:TPU:0, one launch (start us, length us, event | category | flops | bytes accessed | tf_op | source)
XLA Modules:
  0.0 199.5 jit_solution(14297568361846896567)
XLA Ops:
  0.6 1.0 broadcast_in_dim.12
  1.7 16.2 %all_to_all.15 = bf16[8,64,1024]{2,1,0:T(8,128)(2,1)S(1)} all-to-all(bf16[8,64,1024]{2,1,0:T(8,128)(2,1)S(1)} %broadcast_in_dim.12), channel_id=1, replica_groups={{0,2,8,10,32,34,40,42},{4,6,12,14,36,38,44,46},{16,18,24,26,48,50,56,58..., dimensions={0} | all-to-all | bytes 2097152 | tf_op jit(solution)/shard_map/all_to_all | solution.py:82
  17.9 2.1 %collective-permute-start = (bf16[176,1024]{1,0:T(8,128)(2,1)S(1)}, bf16[176,1024]{1,0:T(8,128)(2,1)S(1)}, u32[]{:S(2)}, u32[]{:S(2)}) collective-permute-start(bf16[176,1024]{1,0:T(8,128)(2,1)S(1)} %get-tuple-element.29), channel_id=1, source_target_pairs={{0,96},{1,33},{2,98},{3,35},{4,100},{5,37},{6,102},{7,39},{8,104},... | collective-permute-start | bytes 1081352 | tf_op jit(solution)/shard_map/ppermute | solution.py:91
  20.0 2.7 %collective-permute-start.4 = (bf16[176,1024]{1,0:T(8,128)(2,1)S(1)}, bf16[176,1024]{1,0:T(8,128)(2,1)S(1)}, u32[]{:S(2)}, u32[]{:S(2)}) collective-permute-start(bf16[176,1024]{1,0:T(8,128)(2,1)S(1)} %get-tuple-element.28), channel_id=1, source_target_pairs={{0,24},{1,9},{2,26},{3,11},{4,28},{5,13},{6,30},{7,15},{8,16},{9,1... | collective-permute-start | bytes 1081352 | tf_op jit(solution)/shard_map/ppermute | solution.py:91
  22.7 1.9 collective-permute-start.8
  24.6 2.0 %collective-permute-done = bf16[176,1024]{1,0:T(8,128)(2,1)S(1)} collective-permute-done((bf16[176,1024]{1,0:T(8,128)(2,1)S(1)}, bf16[176,1024]{1,0:T(8,128)(2,1)S(1)}, u32[]{:S(2)}, u32[]{:S(2)}) %collective-permute-start) | collective-permute-done | bytes 360480 | tf_op jit(solution)/shard_map/ppermute | solution.py:91
  26.7 1.0 pad_maximum_fusion.refs_0_
  27.6 2.7 %collective-permute-start.2 = (bf16[352,1024]{1,0:T(8,128)(2,1)}, bf16[352,1024]{1,0:T(8,128)(2,1)}, u32[]{:S(2)}, u32[]{:S(2)}) collective-permute-start(bf16[352,1024]{1,0:T(8,128)(2,1)} %pad_maximum_fusion.refs_0_), channel_id=1, source_target_pairs={{0,24},{1,9},{2,26},{3,11},{4,28},{5,13},{6,30},{7,15},{8,16},{9,1... | collective-permute-start | bytes 2162696 | tf_op jit(solution)/shard_map/ppermute | solution.py:91
  30.3 0.9 pad_maximum_fusion.1.refs_2_.refs_4_
  31.2 1.8 collective-permute-start.6
  33.1 2.1 %collective-permute-start.10 = (bf16[320,1024]{1,0:T(8,128)(2,1)S(1)}, bf16[320,1024]{1,0:T(8,128)(2,1)}, u32[]{:S(2)}, u32[]{:S(2)}) collective-permute-start(bf16[320,1024]{1,0:T(8,128)(2,1)S(1)} %pad_maximum_fusion.2.refs_4_.refs_8_), channel_id=1, source_target_pairs={{0,96},{1,33},{2,98},{3,35},{4,100},{5,37},{6,102},{7,39},{8,104},... | collective-permute-start | bytes 1966088 | tf_op jit(solution)/shard_map/ppermute | solution.py:91
  36.5 1.4 collective-permute-start.1
  37.9 7.2 %collective-permute-done.10.refs_5_.refs_9_ = bf16[320,1024]{1,0:T(8,128)(2,1)} collective-permute-done((bf16[320,1024]{1,0:T(8,128)(2,1)S(1)}, bf16[320,1024]{1,0:T(8,128)(2,1)}, u32[]{:S(2)}, u32[]{:S(2)}) %collective-permute-start.10) | collective-permute-done | bytes 655392 | tf_op jit(solution)/shard_map/ppermute | solution.py:91
  45.1 2.0 %collective-permute-start.5 = (bf16[352,1024]{1,0:T(8,128)(2,1)}, bf16[352,1024]{1,0:T(8,128)(2,1)}, u32[]{:S(2)}, u32[]{:S(2)}) collective-permute-start(bf16[352,1024]{1,0:T(8,128)(2,1)} %pad_maximum_fusion.1.refs_2_.refs_4_), channel_id=1, source_target_pairs={{0,96},{1,33},{2,98},{3,35},{4,100},{5,37},{6,102},{7,39},{8,104},... | collective-permute-start | bytes 2162696 | tf_op jit(solution)/shard_map/ppermute | solution.py:91
  47.4 2.7 %collective-permute-start.11 = (bf16[320,1024]{1,0:T(8,128)(2,1)}, bf16[320,1024]{1,0:T(8,128)(2,1)}, u32[]{:S(2)}, u32[]{:S(2)}) collective-permute-start(bf16[320,1024]{1,0:T(8,128)(2,1)} %collective-permute-done.10.refs_5_.refs_9_), channel_id=1, source_target_pairs={{0,24},{1,9},{2,26},{3,11},{4,28},{5,13},{6,30},{7,15},{8,16},{9,1... | collective-permute-start | bytes 1966088 | tf_op jit(solution)/shard_map/ppermute | solution.py:91
  50.0 1.8 collective-permute-start.3
  51.9 2.0 %collective-permute-start.7 = (bf16[352,1024]{1,0:T(8,128)(2,1)}, bf16[352,1024]{1,0:T(8,128)(2,1)}, u32[]{:S(2)}, u32[]{:S(2)}) collective-permute-start(bf16[352,1024]{1,0:T(8,128)(2,1)} %collective-permute-done.6.refs_3_.refs_5_), channel_id=1, source_target_pairs={{0,96},{1,33},{2,98},{3,35},{4,100},{5,37},{6,102},{7,39},{8,104},... | collective-permute-start | bytes 2162696 | tf_op jit(solution)/shard_map/ppermute | solution.py:91
  53.9 15.2 %shard_map.84 = (bf16[1024,4096]{1,0:T(8,128)(2,1)}, bf16[4096,1024]{1,0:T(8,128)(2,1)}) custom-call(s32[192]{0:T(256)S(1)} %bitcast.10, bf16[1024,4096]{1,0:T(8,128)(2,1)} %w.1), custom_call_target="tpu_custom_call" | custom-call | flops 8589934592 | bytes 25165824 | tf_op jit(solution)/shard_map/pallas_call | solution.py:263
  69.7 10.0 %shard_map.85.refs_7_ = f32[1024,1024]{1,0:T(8,128)} custom-call(bf16[352,1024]{1,0:T(8,128)(2,1)} %pad_maximum_fusion.refs_0_, bf16[352,1024]{1,0:T(8,128)(2,1)} %collective-permute-done.2.refs_1_, bf16[352,1024]{1,0:T(8,128)(2,1)} %pad_maximum_fusion.1.refs_2_.refs_4_, bf16[352,1024]{1,0:T(8,128)(2,1)} %collective-permute-done.6.refs_3_.refs_5_, ...), custom_call_target="tpu_custom_call" | custom-call | flops 4294967296 | bytes 12582912 | tf_op jit(solution)/shard_map/pallas_call | solution.py:345
  79.7 11.5 %shard_map.86 = (f32[1024,1024]{1,0:T(8,128)}, f32[64,16,128]{2,1,0:T(8,128)}) custom-call(bf16[352,1024]{1,0:T(8,128)(2,1)} %collective-permute-done.1.refs_0_.refs_2_, bf16[352,1024]{1,0:T(8,128)(2,1)} %collective-permute-done.3.refs_1_.refs_3_, bf16[352,1024]{1,0:T(8,128)(2,1)} %collective-permute-done.5.refs_2_.refs_6_, ...), custom_call_target="tpu_custom_call" | custom-call | flops 4294967296 | bytes 12582912 | tf_op jit(solution)/shard_map/pallas_call | solution.py:345
  91.2 17.5 %all_to_all.16.stats = f32[64,16,128]{2,1,0:T(8,128)} all-to-all(f32[64,16,128]{2,1,0:T(8,128)} %get-tuple-element.17), channel_id=1, replica_groups=mesh['vocab_0'=4,'vocab_1'=4,'vocab_2'=4,'dp'=2] {'vocab_0','vocab_1','v..., dimensions={0} | all-to-all | bytes 1048576 | tf_op jit(solution)/shard_map/all_to_all | solution.py:478
  108.7 11.4 %shard_map.87 = (bf16[1024,1024]{1,0:T(8,128)(2,1)}, f32[1,1024]{1,0:T(1,128)}, bf16[4,176,1024]{2,1,0:T(8,128)(2,1)}, bf16[4,176,1024]{2,1,0:T(8,128)(2,1)}, bf16[4,160,1024]{2,1,0:T(8,128)(2,1)}) custom-call(f32[64,16,128]{2,1,0:T(8,128)} %all_to_all.16.stats, f32[1024,1024]{1,0:T(8,128)} %get-tuple-element.18.logits, f32[1,1024]{1,0:T(1,128)} %bitcast.20, ...), custom_call_target="tpu_custom_call" | custom-call | flops 4294967296 | bytes 14680064 | tf_op jit(solution)/shard_map/pallas_call | solution.py:409
  120.1 0.8 collective-permute-start.12
  120.9 0.7 collective-permute-start.15
  121.7 1.4 collective-permute-start.18
  123.1 8.2 %shard_map.88 = (bf16[4,176,1024]{2,1,0:T(8,128)(2,1)}, bf16[4,176,1024]{2,1,0:T(8,128)(2,1)}, bf16[4,160,1024]{2,1,0:T(8,128)(2,1)}) custom-call(bf16[4096,1024]{1,0:T(8,128)(2,1)} %get-tuple-element.19.tall, bf16[1024,1024]{1,0:T(8,128)(2,1)} %get-tuple-element.21.grad), custom_call_target="tpu_custom_call" | custom-call | flops 4294967296 | bytes 8388608 | tf_op jit(solution)/shard_map/pallas_call | solution.py:447
  131.3 9.3 %collective-permute-done.12.refs_1_ = bf16[4,176,1024]{2,1,0:T(8,128)(2,1)} collective-permute-done((bf16[4,176,1024]{2,1,0:T(8,128)(2,1)}, bf16[4,176,1024]{2,1,0:T(8,128)(2,1)}, u32[]{:S(2)}, u32[]{:S(2)}) %collective-permute-start.12) | collective-permute-done | bytes 1441824 | tf_op jit(solution)/shard_map/ppermute | solution.py:160
  140.6 2.2 %shard_map.89 = bf16[2,176,1024]{2,1,0:T(8,128)(2,1)} custom-call(bf16[4,176,1024]{2,1,0:T(8,128)(2,1)} %get-tuple-element.22.refs_0_, bf16[4,176,1024]{2,1,0:T(8,128)(2,1)} %collective-permute-done.12.refs_1_), custom_call_target="tpu_custom_call" | custom-call | flops 720896 | bytes 2162688 | tf_op jit(solution)/shard_map/pallas_call | solution.py:113
  143.3 2.1 %shard_map.91 = bf16[2,176,1024]{2,1,0:T(8,128)(2,1)} custom-call(bf16[4,176,1024]{2,1,0:T(8,128)(2,1)} %get-tuple-element.24.refs_0_.refs_4_, bf16[4,176,1024]{2,1,0:T(8,128)(2,1)} %collective-permute-done.15.refs_1_.refs_5_), custom_call_target="tpu_custom_call" | custom-call | flops 720896 | bytes 2162688 | tf_op jit(solution)/shard_map/pallas_call | solution.py:113
  145.4 1.4 collective-permute-start.16
  146.8 8.7 %shard_map.97 = f32[64,4096]{1,0:T(8,128)} custom-call(s32[192]{0:T(256)} %bitcast.11, bf16[352,1024]{1,0:T(8,128)(2,1)} %pad_maximum_fusion.refs_0_, bf16[352,1024]{1,0:T(8,128)(2,1)} %collective-permute-done.2.refs_1_, bf16[352,1024]{1,0:T(8,128)(2,1)} %collective-permute-done.1.refs_0_.refs_2_, bf16[352,1024]{1,0:T(8,128)(2,1)} %collective-permute-done.3.refs_1_.refs_3_, ...), custom_call_target="tpu_custom_call" | custom-call | flops 536870912 | bytes 8388608 | tf_op jit(solution)/shard_map/pallas_call | solution.py:221
  155.6 2.1 %shard_map.93 = bf16[2,160,1024]{2,1,0:T(8,128)(2,1)} custom-call(bf16[4,160,1024]{2,1,0:T(8,128)(2,1)} %get-tuple-element.26.refs_0_.refs_8_, bf16[4,160,1024]{2,1,0:T(8,128)(2,1)} %collective-permute-done.18.refs_1_.refs_9_), custom_call_target="tpu_custom_call" | custom-call | flops 655360 | bytes 1966080 | tf_op jit(solution)/shard_map/pallas_call | solution.py:113
  157.7 1.1 collective-permute-start.19
  158.8 2.1 %shard_map.90 = bf16[1,176,1024]{2,1,0:T(8,128)(2,1)} custom-call(bf16[4,176,1024]{2,1,0:T(8,128)(2,1)} %get-tuple-element.22.refs_0_, bf16[4,176,1024]{2,1,0:T(8,128)(2,1)} %collective-permute-done.12.refs_1_, bf16[2,176,1024]{2,1,0:T(8,128)(2,1)} %collective-permute-done.13.refs_2_), custom_call_target="tpu_custom_call" | custom-call | flops 540672 | bytes 1441792 | tf_op jit(solution)/shard_map/pallas_call | solution.py:113
  160.9 2.1 %collective-permute-start.14 = (bf16[1,176,1024]{2,1,0:T(8,128)(2,1)}, bf16[1,176,1024]{2,1,0:T(8,128)(2,1)}, u32[]{:S(2)}, u32[]{:S(2)}) collective-permute-start(bf16[1,176,1024]{2,1,0:T(8,128)(2,1)} %shard_map.90), channel_id=1, source_target_pairs={{0,96},{1,33},{2,98},{3,35},{4,100},{5,37},{6,102},{7,39},{8,104},... | collective-permute-start | bytes 1081352 | tf_op jit(solution)/shard_map/ppermute | solution.py:160
  163.0 2.1 %shard_map.92 = bf16[1,176,1024]{2,1,0:T(8,128)(2,1)} custom-call(bf16[4,176,1024]{2,1,0:T(8,128)(2,1)} %get-tuple-element.24.refs_0_.refs_4_, bf16[4,176,1024]{2,1,0:T(8,128)(2,1)} %collective-permute-done.15.refs_1_.refs_5_, bf16[2,176,1024]{2,1,0:T(8,128)(2,1)} %collective-permute-done.16.refs_2_.refs_6_), custom_call_target="tpu_custom_call" | custom-call | flops 540672 | bytes 1441792 | tf_op jit(solution)/shard_map/pallas_call | solution.py:113
  165.1 2.2 %collective-permute-start.17 = (bf16[1,176,1024]{2,1,0:T(8,128)(2,1)}, bf16[1,176,1024]{2,1,0:T(8,128)(2,1)}, u32[]{:S(2)}, u32[]{:S(2)}) collective-permute-start(bf16[1,176,1024]{2,1,0:T(8,128)(2,1)} %shard_map.92), channel_id=1, source_target_pairs={{0,24},{1,9},{2,26},{3,11},{4,28},{5,13},{6,30},{7,15},{8,16},{9,1... | collective-permute-start | bytes 1081352 | tf_op jit(solution)/shard_map/ppermute | solution.py:160
  167.3 2.5 %collective-permute-done.19.refs_2_.refs_10_ = bf16[2,160,1024]{2,1,0:T(8,128)(2,1)} collective-permute-done((bf16[2,160,1024]{2,1,0:T(8,128)(2,1)}, bf16[2,160,1024]{2,1,0:T(8,128)(2,1)}, u32[]{:S(2)}, u32[]{:S(2)}) %collective-permute-start.19) | collective-permute-done | bytes 655392 | tf_op jit(solution)/shard_map/ppermute | solution.py:160
  169.8 2.0 %shard_map.94 = bf16[1,160,1024]{2,1,0:T(8,128)(2,1)} custom-call(bf16[4,160,1024]{2,1,0:T(8,128)(2,1)} %get-tuple-element.26.refs_0_.refs_8_, bf16[4,160,1024]{2,1,0:T(8,128)(2,1)} %collective-permute-done.18.refs_1_.refs_9_, bf16[2,160,1024]{2,1,0:T(8,128)(2,1)} %collective-permute-done.19.refs_2_.refs_10_), custom_call_target="tpu_custom_call" | custom-call | flops 491520 | bytes 1310720 | tf_op jit(solution)/shard_map/pallas_call | solution.py:113
  171.8 1.8 collective-permute-start.20
  173.7 6.8 %collective-permute-done.20.refs_11_ = bf16[1,160,1024]{2,1,0:T(8,128)(2,1)} collective-permute-done((bf16[1,160,1024]{2,1,0:T(8,128)(2,1)}, bf16[1,160,1024]{2,1,0:T(8,128)(2,1)}, u32[]{:S(2)}, u32[]{:S(2)}) %collective-permute-start.20) | collective-permute-done | bytes 327712 | tf_op jit(solution)/shard_map/ppermute | solution.py:160
  180.4 3.3 %shard_map.95 = bf16[512,1024]{1,0:T(8,128)(2,1)} custom-call(bf16[4,176,1024]{2,1,0:T(8,128)(2,1)} %get-tuple-element.22.refs_0_, bf16[4,176,1024]{2,1,0:T(8,128)(2,1)} %collective-permute-done.12.refs_1_, bf16[2,176,1024]{2,1,0:T(8,128)(2,1)} %collective-permute-done.13.refs_2_, bf16[1,176,1024]{2,1,0:T(8,128)(2,1)} %collective-permute-done.14.refs_3_, ...), custom_call_target="tpu_custom_call" | custom-call | flops 2097152 | bytes 5242880 | tf_op jit(solution)/shard_map/pallas_call | solution.py:141
  183.8 3.7 %all-to-all-start.2 = ((bf16[8,64,1024]{2,1,0:T(8,128)(2,1)}), bf16[8,64,1024]{2,1,0:T(8,128)(2,1)S(1)}, u32[]{:S(2)}, u32[]{:S(2)}) async-start(bf16[8,64,1024]{2,1,0:T(8,128)(2,1)} %bitcast.12), calls=%async_computation.2 | async-start | bytes 2097152 | tf_op jit(solution)/shard_map/all_to_all | solution.py:82
  187.5 2.3 %add_multiply_fusion.1 = f32[64,4096]{1,0:T(8,128)} fusion(f32[64,4096]{1,0:T(8,128)S(1)} %copy-done.2, f32[64,4096]{1,0:T(8,128)} %collective-permute-done.22), kind=kLoop, calls=%fused_computation.1 | loop fusion | flops 524288 | bytes 3145728 | tf_op jit(solution)/shard_map/div | solution.py:491
  189.8 3.3 %fusion = f32[512,1024]{1,0:T(8,128)S(1)} fusion(bf16[1024,1024]{1,0:T(8,128)(2,1)} %collective-permute-done.21, s32[]{:T(128)S(6)} %select_n.9), kind=kOutput, calls=%fused_computation.2 | convolution fusion | flops 1073741824 | bytes 5242884 | tf_op jit(solution)/shard_map/dot_general | solution.py:488
  193.2 2.6 %add_multiply_fusion = f32[512,1024]{1,0:T(8,128)} fusion(f32[512,1024]{1,0:T(8,128)S(1)} %fusion, bf16[1024,1024]{1,0:T(8,128)(2,1)S(1)} %copy-done.5, s32[]{:T(128)S(6)} %select_n.9), kind=kOutput, calls=%fused_computation | convolution fusion | flops 1074790400 | bytes 7340036 | tf_op jit(solution)/shard_map/dot_general | solution.py:488
  195.8 2.9 %all-to-all-done.2.pieces = bf16[8,64,1024]{2,1,0:T(8,128)(2,1)S(1)} async-done(((bf16[8,64,1024]{2,1,0:T(8,128)(2,1)}), bf16[8,64,1024]{2,1,0:T(8,128)(2,1)S(1)}, u32[]{:S(2)}, u32[]{:S(2)}) %all-to-all-start.2) | async-done | bytes 1048608 | tf_op jit(solution)/shard_map/all_to_all | solution.py:82
  198.7 0.9 shard_map.96
  (39 shorter events, 2.8 us)
Async XLA Ops:
  17.9 8.7 %collective-permute-start = (bf16[176,1024]{1,0:T(8,128)(2,1)S(1)}, bf16[176,1024]{1,0:T(8,128)(2,1)S(1)}, u32[]{:S(2)}, u32[]{:S(2)}) collective-permute-start(bf16[176,1024]{1,0:T(8,128)(2,1)S(1)} %get-tuple-element.29), channel_id=1, source_target_pairs={{0,96},{1,33},{2,98},{3,35},{4,100},{5,37},{6,102},{7,39},{8,104},... | collective-permute-start | bytes 1081352 | tf_op jit(solution)/shard_map/ppermute | solution.py:91
  20.0 10.3 %collective-permute-start.4 = (bf16[176,1024]{1,0:T(8,128)(2,1)S(1)}, bf16[176,1024]{1,0:T(8,128)(2,1)S(1)}, u32[]{:S(2)}, u32[]{:S(2)}) collective-permute-start(bf16[176,1024]{1,0:T(8,128)(2,1)S(1)} %get-tuple-element.28), channel_id=1, source_target_pairs={{0,24},{1,9},{2,26},{3,11},{4,28},{5,13},{6,30},{7,15},{8,16},{9,1... | collective-permute-start | bytes 1081352 | tf_op jit(solution)/shard_map/ppermute | solution.py:91
  22.7 10.3 %collective-permute-start.8 = (bf16[160,1024]{1,0:T(8,128)(2,1)S(1)}, bf16[160,1024]{1,0:T(8,128)(2,1)S(1)}, u32[]{:S(2)}, u32[]{:S(2)}) collective-permute-start(bf16[160,1024]{1,0:T(8,128)(2,1)S(1)} %slice.14), channel_id=1, source_target_pairs={{0,6},{1,3},{2,4},{3,1},{4,2},{5,7},{6,0},{7,5},{8,14},{9,11},{10,... | collective-permute-start | bytes 983048 | tf_op jit(solution)/shard_map/ppermute | solution.py:91
  27.6 22.4 %collective-permute-start.2 = (bf16[352,1024]{1,0:T(8,128)(2,1)}, bf16[352,1024]{1,0:T(8,128)(2,1)}, u32[]{:S(2)}, u32[]{:S(2)}) collective-permute-start(bf16[352,1024]{1,0:T(8,128)(2,1)} %pad_maximum_fusion.refs_0_), channel_id=1, source_target_pairs={{0,24},{1,9},{2,26},{3,11},{4,28},{5,13},{6,30},{7,15},{8,16},{9,1... | collective-permute-start | bytes 2162696 | tf_op jit(solution)/shard_map/ppermute | solution.py:91
  31.2 20.7 %collective-permute-start.6 = (bf16[352,1024]{1,0:T(8,128)(2,1)}, bf16[352,1024]{1,0:T(8,128)(2,1)}, u32[]{:S(2)}, u32[]{:S(2)}) collective-permute-start(bf16[352,1024]{1,0:T(8,128)(2,1)} %pad_maximum_fusion.1.refs_2_.refs_4_), channel_id=1, source_target_pairs={{0,6},{1,3},{2,4},{3,1},{4,2},{5,7},{6,0},{7,5},{8,14},{9,11},{10,... | collective-permute-start | bytes 2162696 | tf_op jit(solution)/shard_map/ppermute | solution.py:91
  33.1 36.0 %copy-start.1 = (bf16[320,1024]{1,0:T(8,128)(2,1)}, bf16[320,1024]{1,0:T(8,128)(2,1)S(1)}, u32[]{:S(2)}) copy-start(bf16[320,1024]{1,0:T(8,128)(2,1)S(1)} %pad_maximum_fusion.2.refs_4_.refs_8_) | copy-start | bytes 1966084
  33.1 12.0 %collective-permute-start.10 = (bf16[320,1024]{1,0:T(8,128)(2,1)S(1)}, bf16[320,1024]{1,0:T(8,128)(2,1)}, u32[]{:S(2)}, u32[]{:S(2)}) collective-permute-start(bf16[320,1024]{1,0:T(8,128)(2,1)S(1)} %pad_maximum_fusion.2.refs_4_.refs_8_), channel_id=1, source_target_pairs={{0,96},{1,33},{2,98},{3,35},{4,100},{5,37},{6,102},{7,39},{8,104},... | collective-permute-start | bytes 1966088 | tf_op jit(solution)/shard_map/ppermute | solution.py:91
  35.2 12.2 %collective-permute-start.9 = (bf16[320,1024]{1,0:T(8,128)(2,1)S(1)}, bf16[320,1024]{1,0:T(8,128)(2,1)S(1)}, u32[]{:S(2)}, u32[]{:S(2)}) collective-permute-start(bf16[320,1024]{1,0:T(8,128)(2,1)S(1)} %pad_maximum_fusion.2.refs_4_.refs_8_), channel_id=1, source_target_pairs={{0,24},{1,9},{2,26},{3,11},{4,28},{5,13},{6,30},{7,15},{8,16},{9,1... | collective-permute-start | bytes 1966088 | tf_op jit(solution)/shard_map/ppermute | solution.py:91
  36.5 32.6 %copy-start = (s32[1,192]{1,0:T(1,128)}, s32[1,192]{1,0:T(1,128)S(1)}, u32[]{:S(2)}) copy-start(s32[1,192]{1,0:T(1,128)S(1)} %constant_dynamic-slice_fusion) | copy-start | bytes 2308
  36.5 43.2 %collective-permute-start.1 = (bf16[352,1024]{1,0:T(8,128)(2,1)}, bf16[352,1024]{1,0:T(8,128)(2,1)}, u32[]{:S(2)}, u32[]{:S(2)}) collective-permute-start(bf16[352,1024]{1,0:T(8,128)(2,1)} %pad_maximum_fusion.refs_0_), channel_id=1, source_target_pairs={{0,6},{1,3},{2,4},{3,1},{4,2},{5,7},{6,0},{7,5},{8,14},{9,11},{10,... | collective-permute-start | bytes 2162696 | tf_op jit(solution)/shard_map/ppermute | solution.py:91
  45.1 34.6 %collective-permute-start.5 = (bf16[352,1024]{1,0:T(8,128)(2,1)}, bf16[352,1024]{1,0:T(8,128)(2,1)}, u32[]{:S(2)}, u32[]{:S(2)}) collective-permute-start(bf16[352,1024]{1,0:T(8,128)(2,1)} %pad_maximum_fusion.1.refs_2_.refs_4_), channel_id=1, source_target_pairs={{0,96},{1,33},{2,98},{3,35},{4,100},{5,37},{6,102},{7,39},{8,104},... | collective-permute-start | bytes 2162696 | tf_op jit(solution)/shard_map/ppermute | solution.py:91
  47.4 21.7 %copy-start.3 = (bf16[320,1024]{1,0:T(8,128)(2,1)}, bf16[320,1024]{1,0:T(8,128)(2,1)S(1)}, u32[]{:S(2)}) copy-start(bf16[320,1024]{1,0:T(8,128)(2,1)S(1)} %collective-permute-done.9.refs_4_.refs_10_) | copy-start | bytes 1966084
  47.4 32.3 %collective-permute-start.11 = (bf16[320,1024]{1,0:T(8,128)(2,1)}, bf16[320,1024]{1,0:T(8,128)(2,1)}, u32[]{:S(2)}, u32[]{:S(2)}) collective-permute-start(bf16[320,1024]{1,0:T(8,128)(2,1)} %collective-permute-done.10.refs_5_.refs_9_), channel_id=1, source_target_pairs={{0,24},{1,9},{2,26},{3,11},{4,28},{5,13},{6,30},{7,15},{8,16},{9,1... | collective-permute-start | bytes 1966088 | tf_op jit(solution)/shard_map/ppermute | solution.py:91
  50.0 29.7 %collective-permute-start.3 = (bf16[352,1024]{1,0:T(8,128)(2,1)}, bf16[352,1024]{1,0:T(8,128)(2,1)}, u32[]{:S(2)}, u32[]{:S(2)}) collective-permute-start(bf16[352,1024]{1,0:T(8,128)(2,1)} %collective-permute-done.2.refs_1_), channel_id=1, source_target_pairs={{0,6},{1,3},{2,4},{3,1},{4,2},{5,7},{6,0},{7,5},{8,14},{9,11},{10,... | collective-permute-start | bytes 2162696 | tf_op jit(solution)/shard_map/ppermute | solution.py:91
  51.9 27.8 %collective-permute-start.7 = (bf16[352,1024]{1,0:T(8,128)(2,1)}, bf16[352,1024]{1,0:T(8,128)(2,1)}, u32[]{:S(2)}, u32[]{:S(2)}) collective-permute-start(bf16[352,1024]{1,0:T(8,128)(2,1)} %collective-permute-done.6.refs_3_.refs_5_), channel_id=1, source_target_pairs={{0,96},{1,33},{2,98},{3,35},{4,100},{5,37},{6,102},{7,39},{8,104},... | collective-permute-start | bytes 2162696 | tf_op jit(solution)/shard_map/ppermute | solution.py:91
  53.9 15.2 %copy-start.4 = (s32[1024]{0:T(1024)S(1)}, s32[1024]{0:T(1024)}, u32[]{:S(2)}) copy-start(s32[1024]{0:T(1024)} %param.7) | copy-start | bytes 12292
  120.1 20.5 %collective-permute-start.12 = (bf16[4,176,1024]{2,1,0:T(8,128)(2,1)}, bf16[4,176,1024]{2,1,0:T(8,128)(2,1)}, u32[]{:S(2)}, u32[]{:S(2)}) collective-permute-start(bf16[4,176,1024]{2,1,0:T(8,128)(2,1)} %get-tuple-element.23), channel_id=1, source_target_pairs={{0,6},{1,3},{2,4},{3,1},{4,2},{5,7},{6,0},{7,5},{8,14},{9,11},{10,... | collective-permute-start | bytes 4325384 | tf_op jit(solution)/shard_map/ppermute | solution.py:160
  120.9 22.4 %collective-permute-start.15 = (bf16[4,176,1024]{2,1,0:T(8,128)(2,1)}, bf16[4,176,1024]{2,1,0:T(8,128)(2,1)}, u32[]{:S(2)}, u32[]{:S(2)}) collective-permute-start(bf16[4,176,1024]{2,1,0:T(8,128)(2,1)} %get-tuple-element.25), channel_id=1, source_target_pairs={{0,96},{1,33},{2,98},{3,35},{4,100},{5,37},{6,102},{7,39},{8,104},... | collective-permute-start | bytes 4325384 | tf_op jit(solution)/shard_map/ppermute | solution.py:160
  121.7 33.9 %collective-permute-start.18 = (bf16[4,160,1024]{2,1,0:T(8,128)(2,1)}, bf16[4,160,1024]{2,1,0:T(8,128)(2,1)}, u32[]{:S(2)}, u32[]{:S(2)}) collective-permute-start(bf16[4,160,1024]{2,1,0:T(8,128)(2,1)} %get-tuple-element.27), channel_id=1, source_target_pairs={{0,24},{1,9},{2,26},{3,11},{4,28},{5,13},{6,30},{7,15},{8,16},{9,1... | collective-permute-start | bytes 3932168 | tf_op jit(solution)/shard_map/ppermute | solution.py:160
  123.1 66.7 %collective-permute-start.21 = (bf16[1024,1024]{1,0:T(8,128)(2,1)}, bf16[1024,1024]{1,0:T(8,128)(2,1)}, u32[]{:S(2)}, u32[]{:S(2)}) collective-permute-start(bf16[1024,1024]{1,0:T(8,128)(2,1)} %get-tuple-element.21.grad), channel_id=1, source_target_pairs={{0,1},{1,0},{2,3},{3,2},{4,5},{5,4},{6,7},{7,6},{8,9},{9,8},{10,11... | collective-permute-start | bytes 6291464 | tf_op jit(solution)/shard_map/ppermute | solution.py:490
  142.8 16.0 %collective-permute-start.13 = (bf16[2,176,1024]{2,1,0:T(8,128)(2,1)}, bf16[2,176,1024]{2,1,0:T(8,128)(2,1)}, u32[]{:S(2)}, u32[]{:S(2)}) collective-permute-start(bf16[2,176,1024]{2,1,0:T(8,128)(2,1)} %shard_map.89), channel_id=1, source_target_pairs={{0,24},{1,9},{2,26},{3,11},{4,28},{5,13},{6,30},{7,15},{8,16},{9,1... | collective-permute-start | bytes 2162696 | tf_op jit(solution)/shard_map/ppermute | solution.py:160
  145.4 17.6 %collective-permute-start.16 = (bf16[2,176,1024]{2,1,0:T(8,128)(2,1)}, bf16[2,176,1024]{2,1,0:T(8,128)(2,1)}, u32[]{:S(2)}, u32[]{:S(2)}) collective-permute-start(bf16[2,176,1024]{2,1,0:T(8,128)(2,1)} %shard_map.91), channel_id=1, source_target_pairs={{0,6},{1,3},{2,4},{3,1},{4,2},{5,7},{6,0},{7,5},{8,14},{9,11},{10,... | collective-permute-start | bytes 2162696 | tf_op jit(solution)/shard_map/ppermute | solution.py:160
  155.5 32.0 %collective-permute-start.22 = (f32[64,4096]{1,0:T(8,128)}, f32[64,4096]{1,0:T(8,128)}, u32[]{:S(2)}, u32[]{:S(2)}) collective-permute-start(f32[64,4096]{1,0:T(8,128)} %shard_map.97), channel_id=1, source_target_pairs={{0,1},{1,0},{2,3},{3,2},{4,5},{5,4},{6,7},{7,6},{8,9},{9,8},{10,11... | collective-permute-start | bytes 3145736 | tf_op jit(solution)/shard_map/ppermute | solution.py:491
  157.7 12.1 %collective-permute-start.19 = (bf16[2,160,1024]{2,1,0:T(8,128)(2,1)}, bf16[2,160,1024]{2,1,0:T(8,128)(2,1)}, u32[]{:S(2)}, u32[]{:S(2)}) collective-permute-start(bf16[2,160,1024]{2,1,0:T(8,128)(2,1)} %shard_map.93), channel_id=1, source_target_pairs={{0,96},{1,33},{2,98},{3,35},{4,100},{5,37},{6,102},{7,39},{8,104},... | collective-permute-start | bytes 1966088 | tf_op jit(solution)/shard_map/ppermute | solution.py:160
  160.9 19.5 %collective-permute-start.14 = (bf16[1,176,1024]{2,1,0:T(8,128)(2,1)}, bf16[1,176,1024]{2,1,0:T(8,128)(2,1)}, u32[]{:S(2)}, u32[]{:S(2)}) collective-permute-start(bf16[1,176,1024]{2,1,0:T(8,128)(2,1)} %shard_map.90), channel_id=1, source_target_pairs={{0,96},{1,33},{2,98},{3,35},{4,100},{5,37},{6,102},{7,39},{8,104},... | collective-permute-start | bytes 1081352 | tf_op jit(solution)/shard_map/ppermute | solution.py:160
  165.1 15.3 %collective-permute-start.17 = (bf16[1,176,1024]{2,1,0:T(8,128)(2,1)}, bf16[1,176,1024]{2,1,0:T(8,128)(2,1)}, u32[]{:S(2)}, u32[]{:S(2)}) collective-permute-start(bf16[1,176,1024]{2,1,0:T(8,128)(2,1)} %shard_map.92), channel_id=1, source_target_pairs={{0,24},{1,9},{2,26},{3,11},{4,28},{5,13},{6,30},{7,15},{8,16},{9,1... | collective-permute-start | bytes 1081352 | tf_op jit(solution)/shard_map/ppermute | solution.py:160
  171.8 8.6 %collective-permute-start.20 = (bf16[1,160,1024]{2,1,0:T(8,128)(2,1)}, bf16[1,160,1024]{2,1,0:T(8,128)(2,1)}, u32[]{:S(2)}, u32[]{:S(2)}) collective-permute-start(bf16[1,160,1024]{2,1,0:T(8,128)(2,1)} %shard_map.94), channel_id=1, source_target_pairs={{0,6},{1,3},{2,4},{3,1},{4,2},{5,7},{6,0},{7,5},{8,14},{9,11},{10,... | collective-permute-start | bytes 983048 | tf_op jit(solution)/shard_map/ppermute | solution.py:160
  183.8 3.7 %copy-start.2 = (f32[64,4096]{1,0:T(8,128)S(1)}, f32[64,4096]{1,0:T(8,128)}, u32[]{:S(2)}) copy-start(f32[64,4096]{1,0:T(8,128)} %shard_map.97) | copy-start | bytes 3145732
  183.8 14.9 %all-to-all-start.2 = ((bf16[8,64,1024]{2,1,0:T(8,128)(2,1)}), bf16[8,64,1024]{2,1,0:T(8,128)(2,1)S(1)}, u32[]{:S(2)}, u32[]{:S(2)}) async-start(bf16[8,64,1024]{2,1,0:T(8,128)(2,1)} %bitcast.12), calls=%async_computation.2 | async-start | bytes 2097152 | tf_op jit(solution)/shard_map/all_to_all | solution.py:82
  189.8 3.4 %copy-start.5 = (bf16[1024,1024]{1,0:T(8,128)(2,1)S(1)}, bf16[1024,1024]{1,0:T(8,128)(2,1)}, u32[]{:S(2)}) copy-start(bf16[1024,1024]{1,0:T(8,128)(2,1)} %get-tuple-element.21.grad) | copy-start | bytes 6291460

commit v3 on v2

--- a/solution.py
+++ b/solution.py
@@ -236,50 +236,74 @@
     )(chips, *[in_hbm(x) for x in got], own)
 
 
-def turn_kernel(chips, w, wide, tall, turned):
-    step = pl.program_id(0)
-    size = w.shape[1]
-
-    @pl.when(step < 8)
-    def _():
-        turned[pl.ds(pl.multiple_of(step * size, size), size)] = w[...].T
-
-    @pl.when(step >= 8)
-    def _():
-        pieces = []
-        for g, group in enumerate(GROUPS):
-            for s, count, first in group:
-                at = pl.multiple_of(chips[64 * g + 8 * (step - 8) + s] * 64 + first, 16)
-                pieces.append(turned[pl.ds(at, count)])
-        rows = jnp.concatenate(pieces, axis=0)
-        tall[...] = rows
-        wide[...] = rows.T
-
-
-def turned_weights(chips, w):
+def columns_kernel(chips, w, wide):
+    rows = w.shape[0]
+    lane = lax.broadcasted_iota(jnp.int32, (rows, 128), 1)
+    for l in range(8):
+        for tile in range(4):
+            done = None
+            for g, group in enumerate(GROUPS):
+                for s, count, first in group:
+                    if s // 2 != tile:
+                        continue
+                    chip, side = chips[64 * g + 8 * l + s], s % 2
+                    block = w[:, pl.ds(pl.multiple_of(chip // 2 * 128, 128), 128)].astype(F32)
+                    block = pltpu.roll(block, 64 * (chip % 2 != side).astype(jnp.int32), 1)
+                    done = block if done is None else jnp.where(
+                        lane >= 64 * side + first, block, done
+                    )
+            wide[:, (4 * l + tile) * 128 : (4 * l + tile + 1) * 128] = done.astype(BF16)
+
+
+def columns_turned(chips, w):
+    vocab_rows, width = w.shape
+    block = pl.BlockSpec((128, width), lambda i, t: (i, 0))
+    return pl.pallas_call(
+        columns_kernel,
+        grid_spec=pltpu.PrefetchScalarGridSpec(
+            num_scalar_prefetch=1, grid=(vocab_rows // 128,), in_specs=[block], out_specs=block
+        ),
+        out_shape=pltpu.HBM((vocab_rows, width), BF16),
+        compiler_params=pltpu.CompilerParams(
+            dimension_semantics=("arbitrary",), vmem_limit_bytes=24 << 20
+        ),
+        cost_estimate=pl.CostEstimate(
+            flops=1024 * vocab_rows * width, bytes_accessed=4 * vocab_rows * width, transcendentals=0
+        ),
+    )(chips, in_hbm(w))
+
+
+def rows_kernel(w, tall):
+    tall[...] = w[...].T
+
+
+def rows_turned(w):
     vocab_rows, width = w.shape
     size = width // 8
-    late = lambda i: jnp.maximum(i - 8, 0)
-    return pl.pallas_call(
-        turn_kernel,
-        grid_spec=pltpu.PrefetchScalarGridSpec(
-            num_scalar_prefetch=1,
-            grid=(16,),
-            in_specs=[pl.BlockSpec((vocab_rows, size), lambda i, t: (0, jnp.minimum(i, 7)))],
-            out_specs=[
-                pl.BlockSpec((vocab_rows, size), lambda i, t: (0, late(i))),
-                pl.BlockSpec((size, vocab_rows), lambda i, t: (late(i), 0)),
-            ],
-            scratch_shapes=[pltpu.VMEM((width, vocab_rows), BF16)],
-        ),
-        out_shape=[pltpu.HBM((vocab_rows, width), BF16), pltpu.HBM((width, vocab_rows), BF16)],
-        compiler_params=pltpu.CompilerParams(
-            dimension_semantics=("arbitrary",), vmem_limit_bytes=32 << 20
-        ),
-        cost_estimate=pl.CostEstimate(
-            flops=2048 * vocab_rows * width, bytes_accessed=6 * vocab_rows * width, transcendentals=0
-        ),
-    )(chips, in_hbm(w))
+    return pl.pallas_call(
+        rows_kernel,
+        grid=(8,),
+        in_specs=[pl.BlockSpec((vocab_rows, size), lambda i: (0, i))],
+        out_specs=pl.BlockSpec((size, vocab_rows), lambda i: (i, 0)),
+        out_shape=pltpu.HBM((width, vocab_rows), BF16),
+        compiler_params=pltpu.CompilerParams(
+            dimension_semantics=("arbitrary",), vmem_limit_bytes=24 << 20
+        ),
+        cost_estimate=pl.CostEstimate(
+            flops=1024 * vocab_rows * width, bytes_accessed=4 * vocab_rows * width, transcendentals=0
+        ),
+    )(in_hbm(w))
+
+
+def row_pieces(step, vocab_rows):
+    def spec(g, s, count, first):
+        place = lambda i, t: (t[64 * g + 8 * step(i) + s], first // count, 0)
+        return pl.BlockSpec((None, count, vocab_rows), place)
+
+    return [spec(g, s, count, first) for g, group in enumerate(GROUPS) for s, count, first in group]
+
+
+PIECES = sum(len(group) for group in GROUPS)
 
 
 def half_copies(got, h):
@@ -366,8 +390,10 @@
     )(*got, in_hbm(wide), *([in_hbm(part), tgt] if late else []))
 
 
-def signal_kernel(stats, logits, cot, tgt, tall, grad, loss, *refs):
-    outs, (row, whole) = refs[:3], refs[3:]
+def signal_kernel(chips, stats, logits, cot, tgt, *refs):
+    pieces, (grad, loss), outs, (row, whole) = (
+        refs[:PIECES], refs[PIECES : PIECES + 2], refs[PIECES + 2 : -2], refs[-2:]
+    )
     step = pl.program_id(0)
     rows, tokens = logits.shape
     lines = tokens // 128
@@ -393,36 +419,35 @@
 
     @pl.when(step >= count)
     def _():
-        block = jnp.dot(tall[...], whole[...], preferred_element_type=F32).astype(BF16)
+        rows_here = jnp.concatenate([p[...] for p in pieces], axis=0)
+        block = jnp.dot(rows_here, whole[...], preferred_element_type=F32).astype(BF16)
         for start, size, out in zip(STARTS, SIZES, outs):
             out[...] = block[start : start + size]
 
 
-def signal_of(stats, logits, cot, tgt, tall):
+def signal_of(chips, stats, logits, cot, tgt, tall):
     vocab_rows, tokens = logits.shape
     width = tall.shape[0]
     rows = 256
     count = vocab_rows // rows
     early = lambda i: jnp.minimum(i, count - 1)
     late = lambda i: jnp.maximum(i - count, 0)
-    whole = lambda *shape: pl.BlockSpec(shape, lambda i: (0,) * len(shape))
+    whole = lambda *shape: pl.BlockSpec(shape, lambda i, t: (0,) * len(shape))
     grad, loss, *sums = pl.pallas_call(
         signal_kernel,
-        grid=(count + 4,),
-        in_specs=[
+        grid_spec=pltpu.PrefetchScalarGridSpec(num_scalar_prefetch=1, grid=(count + 4,), in_specs=[
             whole(*stats.shape),
-            pl.BlockSpec((rows, tokens), lambda i: (early(i), 0)),
+            pl.BlockSpec((rows, tokens), lambda i, t: (early(i), 0)),
             whole(1, tokens),
             whole(1, tokens),
-            pl.BlockSpec((width // 8, vocab_rows), lambda i: (4 + late(i), 0)),
-        ],
-        out_specs=[pl.BlockSpec((rows, tokens), lambda i: (early(i), 0)), whole(1, tokens)]
-        + [pl.BlockSpec((None, size, tokens), lambda i: (late(i), 0, 0)) for size in SIZES],
+        ] + row_pieces(lambda i: 4 + late(i), vocab_rows),
+        out_specs=[pl.BlockSpec((rows, tokens), lambda i, t: (early(i), 0)), whole(1, tokens)]
+        + [pl.BlockSpec((None, size, tokens), lambda i, t: (late(i), 0, 0)) for size in SIZES],
+        scratch_shapes=[pltpu.VMEM((1, tokens), F32), pltpu.VMEM((vocab_rows, tokens), BF16)]),
         out_shape=[
             pltpu.HBM((vocab_rows, tokens), BF16),
             jax.ShapeDtypeStruct((1, tokens), F32),
         ] + [pltpu.HBM((4, size, tokens), BF16) for size in SIZES],
-        scratch_shapes=[pltpu.VMEM((1, tokens), F32), pltpu.VMEM((vocab_rows, tokens), BF16)],
         compiler_params=pltpu.CompilerParams(
             dimension_semantics=("arbitrary",), vmem_limit_bytes=ALL_VMEM
         ),
@@ -431,27 +456,33 @@
             bytes_accessed=6 * vocab_rows * tokens + width * (vocab_rows + tokens),
             transcendentals=vocab_rows * tokens,
         ),
-    )(stats, in_hbm(logits), cot, tgt, in_hbm(tall))
+    )(
+        chips, stats, in_hbm(logits), cot, tgt,
+        *[in_hbm(tall.reshape(64, width // 64, vocab_rows))] * PIECES,
+    )
     return grad, loss, sums
 
 
-def grad_kernel(tall, grad, *outs):
-    block = jnp.dot(tall[...], grad[...], preferred_element_type=F32).astype(BF16)
+def grad_kernel(chips, *refs):
+    pieces, grad, outs = refs[:PIECES], refs[PIECES], refs[PIECES + 1 :]
+    rows_here = jnp.concatenate([p[...] for p in pieces], axis=0)
+    block = jnp.dot(rows_here, grad[...], preferred_element_type=F32).astype(BF16)
     for start, size, out in zip(STARTS, SIZES, outs):
         out[...] = block[start : start + size]
 
 
-def half_grads(half, tall, grad):
+def half_grads(chips, half, tall, grad):
     vocab_rows, tokens = grad.shape
     width = tall.shape[0]
     return pl.pallas_call(
         grad_kernel,
-        grid=(4,),
-        in_specs=[
-            pl.BlockSpec((width // 8, vocab_rows), lambda i: (4 * half + i, 0)),
-            pl.BlockSpec((vocab_rows, tokens), lambda i: (0, 0)),
-        ],
-        out_specs=[pl.BlockSpec((None, size, tokens), lambda i: (i, 0, 0)) for size in SIZES],
+        grid_spec=pltpu.PrefetchScalarGridSpec(
+            num_scalar_prefetch=1,
+            grid=(4,),
+            in_specs=row_pieces(lambda i: 4 * half + i, vocab_rows)
+            + [pl.BlockSpec((vocab_rows, tokens), lambda i, t: (0, 0))],
+            out_specs=[pl.BlockSpec((None, size, tokens), lambda i, t: (i, 0, 0)) for size in SIZES],
+        ),
         out_shape=[pltpu.HBM((4, size, tokens), BF16) for size in SIZES],
         compiler_params=pltpu.CompilerParams(
             dimension_semantics=("arbitrary",), vmem_limit_bytes=ALL_VMEM
@@ -460,7 +491,7 @@
             flops=vocab_rows * width * tokens, bytes_accessed=width * (vocab_rows + tokens),
             transcendentals=0,
         ),
-    )(in_hbm(tall), grad)
+    )(chips, *[in_hbm(tall.reshape(64, width // 64, vocab_rows))] * PIECES, grad)
 
 
 def body(hidden, head_weight, targets, loss_cot):
@@ -471,14 +502,15 @@
     chips = lax.dynamic_index_in_dim(jnp.asarray(CHIPS), lax.axis_index(ALL), 0, keepdims=False)
     tgt = (targets - lax.axis_index(VOCAB) * vocab_rows)[None, :]
     some = small_stage(jnp.broadcast_to(own[None], (8, feats, tokens)))
-    wide, tall = turned_weights(chips, head_weight)
+    wide = columns_turned(chips, head_weight)
     got = gathered_groups(some.reshape(8 * feats, tokens))
     part = half_logits(0, [a for group in got for a in group[:2]], wide)
     logits, stats = half_logits(1, [a for group in got for a in group[2:]], wide, part, tgt)
     stats = lax.all_to_all(stats, VOCAB, 0, 0, tiled=True)
+    tall = rows_turned(head_weight)
     a_part = a_part_of(chips, [a for group in got for a in group], own)
-    grad, tok_loss, sends = signal_of(stats, logits, loss_cot[None, :], tgt, tall)
-    sums = summed_groups(sends, half_grads(0, tall, grad))
+    grad, tok_loss, sends = signal_of(chips, stats, logits, loss_cot[None, :], tgt, tall)
+    sums = summed_groups(sends, half_grads(chips, 0, tall, grad))
     sums = small_stage(sums.reshape(8, feats, tokens))
     hidden_grad = summed(sums).T
     rows = vocab_rows // 2

time: 202 us -> 201 us (level)
  blocking collectives: 33.7 us -> 16.2 us
  Pallas kernels: 81.7 us -> 91 us
  starting transfers between devices: 39.6 us -> 47.5 us
    all_to_all x1 -> x0, blocking collectives: 17.5 us -> none  [body(): stats = lax.all_to_all(stats, VOCAB, 0, 0, tiled=True)]
    pallas_call x3 -> x4, Pallas kernels: 34.8 us -> 44.1 us  [the longest x1 12.7 us: signal_of(): pl.pallas_call(signal_kernel, grid_spec=pltpu.PrefetchScalarGridSpec(num_...]
    all_to_all x0 -> x1, starting transfers between devices: none -> 5.5 us  [body(): stats = lax.all_to_all(stats, VOCAB, 0, 0, tiled=True)]
    ppermute x9, starting transfers between devices: 12.1 us -> 14.4 us  [trade(): return lax.ppermute(x, ALL, LARGE_PAIRS[(g + step) % 3])]
  transfers between devices with their start and end apart: 24 -> 25, of which waited for: 7 -> 8; matrix products, arithmetic and copies ran while one was open for 6% -> 6% of each run, Pallas kernels for 29% -> 33%
where the time goes in v3:
time: 201 us; the launch traced here: 199 us
  Pallas kernels  91 us (45%)
  starting transfers between devices  47.5 us (24%)
  waiting for transfers between devices  31.2 us (16%)
  blocking collectives  16.2 us (8%)
  matrix products  5.96 us (3%)
  other arithmetic  4.75 us (2%)
    ppermute x12, starting transfers between devices, get(): return lax.ppermute(x, ALL, LARGE_PAIRS[(g + step) % 3])  23.7 us
    pallas_call x2, Pallas kernels, half_logits(): pl.pallas_call(late_kernel if late else early_kernel, grid=(vocab_rows //...  21.4 us
    ppermute x9, waiting for transfers between devices, trade(): return lax.ppermute(x, ALL, LARGE_PAIRS[(g + step) % 3])  16.9 us
    all_to_all x1, blocking collectives, small_stage(): lax.all_to_all(x, ALL, 0, 0, axis_index_groups=SMALL_CUBES, tiled=True)  16.2 us
    ppermute x9, starting transfers between devices, trade(): return lax.ppermute(x, ALL, LARGE_PAIRS[(g + step) % 3])  14.4 us
    pallas_call x1, Pallas kernels, signal_of(): pl.pallas_call(signal_kernel, grid_spec=pltpu.PrefetchScalarGridSpec(num_...  12.7 us
    pallas_call x6, Pallas kernels, add_up(): pl.pallas_call(add_kernel, grid=(count,), in_specs=[block(first) for _, f...  12.6 us
    pallas_call x1, Pallas kernels, columns_turned(): pl.pallas_call(columns_kernel, grid_spec=pltpu.PrefetchScalarGridSpec(num...  12.1 us
  transfers between devices with their start and end apart: 25, of which 8 were waited for; matrix products, arithmetic and copies ran while one was open for 6% of the time, Pallas kernels for 33%

profile of v3, /device:TPU:0, one launch (start us, length us, event | category | flops | bytes accessed | tf_op | source)
XLA Modules:
  0.0 199.3 jit_solution(12411267984536371225)
XLA Ops:
  0.6 1.0 broadcast_in_dim.12
  1.7 16.2 %all_to_all.15 = bf16[8,64,1024]{2,1,0:T(8,128)(2,1)S(1)} all-to-all(bf16[8,64,1024]{2,1,0:T(8,128)(2,1)S(1)} %broadcast_in_dim.12), channel_id=1, replica_groups={{0,2,8,10,32,34,40,42},{4,6,12,14,36,38,44,46},{16,18,24,26,48,50,56,58..., dimensions={0} | all-to-all | bytes 2097152 | tf_op jit(solution)/shard_map/all_to_all | solution.py:82
  17.9 2.1 %collective-permute-start = (bf16[176,1024]{1,0:T(8,128)(2,1)S(1)}, bf16[176,1024]{1,0:T(8,128)(2,1)S(1)}, u32[]{:S(2)}, u32[]{:S(2)}) collective-permute-start(bf16[176,1024]{1,0:T(8,128)(2,1)S(1)} %get-tuple-element.25), channel_id=1, source_target_pairs={{0,96},{1,33},{2,98},{3,35},{4,100},{5,37},{6,102},{7,39},{8,104},... | collective-permute-start | bytes 1081352 | tf_op jit(solution)/shard_map/ppermute | solution.py:91
  20.0 2.7 %collective-permute-start.4 = (bf16[176,1024]{1,0:T(8,128)(2,1)S(1)}, bf16[176,1024]{1,0:T(8,128)(2,1)S(1)}, u32[]{:S(2)}, u32[]{:S(2)}) collective-permute-start(bf16[176,1024]{1,0:T(8,128)(2,1)S(1)} %get-tuple-element.24), channel_id=1, source_target_pairs={{0,24},{1,9},{2,26},{3,11},{4,28},{5,13},{6,30},{7,15},{8,16},{9,1... | collective-permute-start | bytes 1081352 | tf_op jit(solution)/shard_map/ppermute | solution.py:91
  22.7 1.9 collective-permute-start.8
  24.6 2.0 %collective-permute-done = bf16[176,1024]{1,0:T(8,128)(2,1)S(1)} collective-permute-done((bf16[176,1024]{1,0:T(8,128)(2,1)S(1)}, bf16[176,1024]{1,0:T(8,128)(2,1)S(1)}, u32[]{:S(2)}, u32[]{:S(2)}) %collective-permute-start) | collective-permute-done | bytes 360480 | tf_op jit(solution)/shard_map/ppermute | solution.py:91
  26.7 0.9 pad_maximum_fusion.refs_0_
  27.6 2.7 %collective-permute-start.2 = (bf16[352,1024]{1,0:T(8,128)(2,1)}, bf16[352,1024]{1,0:T(8,128)(2,1)}, u32[]{:S(2)}, u32[]{:S(2)}) collective-permute-start(bf16[352,1024]{1,0:T(8,128)(2,1)} %pad_maximum_fusion.refs_0_), channel_id=1, source_target_pairs={{0,24},{1,9},{2,26},{3,11},{4,28},{5,13},{6,30},{7,15},{8,16},{9,1... | collective-permute-start | bytes 2162696 | tf_op jit(solution)/shard_map/ppermute | solution.py:91
  30.2 0.9 pad_maximum_fusion.1.refs_2_.refs_4_
  31.2 1.8 collective-permute-start.6
  33.0 2.1 %collective-permute-start.10 = (bf16[320,1024]{1,0:T(8,128)(2,1)S(1)}, bf16[320,1024]{1,0:T(8,128)(2,1)}, u32[]{:S(2)}, u32[]{:S(2)}) collective-permute-start(bf16[320,1024]{1,0:T(8,128)(2,1)S(1)} %pad_maximum_fusion.2.refs_4_.refs_8_), channel_id=1, source_target_pairs={{0,96},{1,33},{2,98},{3,35},{4,100},{5,37},{6,102},{7,39},{8,104},... | collective-permute-start | bytes 1966088 | tf_op jit(solution)/shard_map/ppermute | solution.py:91
  36.4 1.4 collective-permute-start.1
  37.8 7.2 %collective-permute-done.10.refs_5_.refs_9_ = bf16[320,1024]{1,0:T(8,128)(2,1)} collective-permute-done((bf16[320,1024]{1,0:T(8,128)(2,1)S(1)}, bf16[320,1024]{1,0:T(8,128)(2,1)}, u32[]{:S(2)}, u32[]{:S(2)}) %collective-permute-start.10) | collective-permute-done | bytes 655392 | tf_op jit(solution)/shard_map/ppermute | solution.py:91
  45.0 2.0 %collective-permute-start.5 = (bf16[352,1024]{1,0:T(8,128)(2,1)}, bf16[352,1024]{1,0:T(8,128)(2,1)}, u32[]{:S(2)}, u32[]{:S(2)}) collective-permute-start(bf16[352,1024]{1,0:T(8,128)(2,1)} %pad_maximum_fusion.1.refs_2_.refs_4_), channel_id=1, source_target_pairs={{0,96},{1,33},{2,98},{3,35},{4,100},{5,37},{6,102},{7,39},{8,104},... | collective-permute-start | bytes 2162696 | tf_op jit(solution)/shard_map/ppermute | solution.py:91
  47.3 2.7 %collective-permute-start.11 = (bf16[320,1024]{1,0:T(8,128)(2,1)}, bf16[320,1024]{1,0:T(8,128)(2,1)}, u32[]{:S(2)}, u32[]{:S(2)}) collective-permute-start(bf16[320,1024]{1,0:T(8,128)(2,1)} %collective-permute-done.10.refs_5_.refs_9_), channel_id=1, source_target_pairs={{0,24},{1,9},{2,26},{3,11},{4,28},{5,13},{6,30},{7,15},{8,16},{9,1... | collective-permute-start | bytes 1966088 | tf_op jit(solution)/shard_map/ppermute | solution.py:91
  50.0 1.8 collective-permute-start.3
  51.8 2.0 %collective-permute-start.7 = (bf16[352,1024]{1,0:T(8,128)(2,1)}, bf16[352,1024]{1,0:T(8,128)(2,1)}, u32[]{:S(2)}, u32[]{:S(2)}) collective-permute-start(bf16[352,1024]{1,0:T(8,128)(2,1)} %collective-permute-done.6.refs_3_.refs_5_), channel_id=1, source_target_pairs={{0,96},{1,33},{2,98},{3,35},{4,100},{5,37},{6,102},{7,39},{8,104},... | collective-permute-start | bytes 2162696 | tf_op jit(solution)/shard_map/ppermute | solution.py:91
  53.8 12.1 %shard_map.84.refs_6_ = bf16[1024,4096]{1,0:T(8,128)(2,1)} custom-call(s32[192]{0:T(256)S(1)} %bitcast.11, bf16[1024,4096]{1,0:T(8,128)(2,1)} %w.3), custom_call_target="tpu_custom_call" | custom-call | flops 4294967296 | bytes 16777216 | tf_op jit(solution)/shard_map/pallas_call | solution.py:261
  66.5 9.9 %shard_map.85.refs_7_ = f32[1024,1024]{1,0:T(8,128)} custom-call(bf16[352,1024]{1,0:T(8,128)(2,1)} %pad_maximum_fusion.refs_0_, bf16[352,1024]{1,0:T(8,128)(2,1)} %collective-permute-done.2.refs_1_, bf16[352,1024]{1,0:T(8,128)(2,1)} %pad_maximum_fusion.1.refs_2_.refs_4_, bf16[352,1024]{1,0:T(8,128)(2,1)} %collective-permute-done.6.refs_3_.refs_5_, ...), custom_call_target="tpu_custom_call" | custom-call | flops 4294967296 | bytes 12582912 | tf_op jit(solution)/shard_map/pallas_call | solution.py:369
  76.5 11.5 %shard_map.86 = (f32[1024,1024]{1,0:T(8,128)}, f32[64,16,128]{2,1,0:T(8,128)}) custom-call(bf16[352,1024]{1,0:T(8,128)(2,1)} %collective-permute-done.1.refs_0_.refs_2_, bf16[352,1024]{1,0:T(8,128)(2,1)} %collective-permute-done.3.refs_1_.refs_3_, bf16[352,1024]{1,0:T(8,128)(2,1)} %collective-permute-done.5.refs_2_.refs_6_, ...), custom_call_target="tpu_custom_call" | custom-call | flops 4294967296 | bytes 12582912 | tf_op jit(solution)/shard_map/pallas_call | solution.py:369
  88.0 5.5 %all-to-all-start.1 = ((f32[64,16,128]{2,1,0:T(8,128)}), f32[64,16,128]{2,1,0:T(8,128)}, u32[]{:S(2)}, u32[]{:S(2)}) async-start(f32[64,16,128]{2,1,0:T(8,128)} %get-tuple-element.14), calls=%async_computation.1 | async-start | bytes 1048576 | tf_op jit(solution)/shard_map/all_to_all | solution.py:509
  93.5 10.1 %shard_map.87 = bf16[4096,1024]{1,0:T(8,128)(2,1)} custom-call(bf16[1024,4096]{1,0:T(8,128)(2,1)} %w.3), custom_call_target="tpu_custom_call" | custom-call | flops 4294967296 | bytes 16777216 | tf_op jit(solution)/shard_map/pallas_call | solution.py:283
  103.5 1.8 all-to-all-done.1.stats
  105.4 12.7 %shard_map.88 = (bf16[1024,1024]{1,0:T(8,128)(2,1)}, f32[1,1024]{1,0:T(1,128)}, bf16[4,176,1024]{2,1,0:T(8,128)(2,1)}, bf16[4,176,1024]{2,1,0:T(8,128)(2,1)}, bf16[4,160,1024]{2,1,0:T(8,128)(2,1)}) custom-call(s32[192]{0:T(256)} %bitcast.12, f32[64,16,128]{2,1,0:T(8,128)} %all-to-all-done.1.stats, f32[1024,1024]{1,0:T(8,128)} %get-tuple-element.15.logits, ...), custom_call_target="tpu_custom_call" | custom-call | flops 4294967296 | bytes 14680064 | tf_op jit(solution)/shard_map/pallas_call | solution.py:436
  118.0 0.9 collective-permute-start.12
  118.9 3.0 %collective-permute-start.15 = (bf16[4,176,1024]{2,1,0:T(8,128)(2,1)}, bf16[4,176,1024]{2,1,0:T(8,128)(2,1)}, u32[]{:S(2)}, u32[]{:S(2)}) collective-permute-start(bf16[4,176,1024]{2,1,0:T(8,128)(2,1)} %get-tuple-element.21), channel_id=1, source_target_pairs={{0,96},{1,33},{2,98},{3,35},{4,100},{5,37},{6,102},{7,39},{8,104},... | collective-permute-start | bytes 4325384 | tf_op jit(solution)/shard_map/ppermute | solution.py:160
  121.9 2.8 %collective-permute-start.18 = (bf16[4,160,1024]{2,1,0:T(8,128)(2,1)}, bf16[4,160,1024]{2,1,0:T(8,128)(2,1)}, u32[]{:S(2)}, u32[]{:S(2)}) collective-permute-start(bf16[4,160,1024]{2,1,0:T(8,128)(2,1)} %get-tuple-element.23), channel_id=1, source_target_pairs={{0,24},{1,9},{2,26},{3,11},{4,28},{5,13},{6,30},{7,15},{8,16},{9,1... | collective-permute-start | bytes 3932168 | tf_op jit(solution)/shard_map/ppermute | solution.py:160
  124.7 9.3 %shard_map.89 = (bf16[4,176,1024]{2,1,0:T(8,128)(2,1)}, bf16[4,176,1024]{2,1,0:T(8,128)(2,1)}, bf16[4,160,1024]{2,1,0:T(8,128)(2,1)}) custom-call(s32[192]{0:T(256)} %bitcast.13, bf16[64,64,1024]{2,1,0:T(8,128)(2,1)} %bitcast.25, bf16[64,64,1024]{2,1,0:T(8,128)(2,1)} %bitcast.26, bf16[64,64,1024]{2,1,0:T(8,128)(2,1)} %bitcast.27, ...), custom_call_target="tpu_custom_call" | custom-call | flops 4294967296 | bytes 8388608 | tf_op jit(solution)/shard_map/pallas_call | solution.py:477
  134.0 4.7 %collective-permute-done.12.refs_1_ = bf16[4,176,1024]{2,1,0:T(8,128)(2,1)} collective-permute-done((bf16[4,176,1024]{2,1,0:T(8,128)(2,1)}, bf16[4,176,1024]{2,1,0:T(8,128)(2,1)}, u32[]{:S(2)}, u32[]{:S(2)}) %collective-permute-start.12) | collective-permute-done | bytes 1441824 | tf_op jit(solution)/shard_map/ppermute | solution.py:160
  138.7 2.1 %shard_map.90 = bf16[2,176,1024]{2,1,0:T(8,128)(2,1)} custom-call(bf16[4,176,1024]{2,1,0:T(8,128)(2,1)} %get-tuple-element.18.refs_0_, bf16[4,176,1024]{2,1,0:T(8,128)(2,1)} %collective-permute-done.12.refs_1_), custom_call_target="tpu_custom_call" | custom-call | flops 720896 | bytes 2162688 | tf_op jit(solution)/shard_map/pallas_call | solution.py:113
  140.8 0.8 collective-permute-start.13
  141.6 2.1 %shard_map.92 = bf16[2,176,1024]{2,1,0:T(8,128)(2,1)} custom-call(bf16[4,176,1024]{2,1,0:T(8,128)(2,1)} %get-tuple-element.20.refs_0_.refs_4_, bf16[4,176,1024]{2,1,0:T(8,128)(2,1)} %collective-permute-done.15.refs_1_.refs_5_), custom_call_target="tpu_custom_call" | custom-call | flops 720896 | bytes 2162688 | tf_op jit(solution)/shard_map/pallas_call | solution.py:113
  143.8 2.7 %collective-permute-start.16 = (bf16[2,176,1024]{2,1,0:T(8,128)(2,1)}, bf16[2,176,1024]{2,1,0:T(8,128)(2,1)}, u32[]{:S(2)}, u32[]{:S(2)}) collective-permute-start(bf16[2,176,1024]{2,1,0:T(8,128)(2,1)} %shard_map.92), channel_id=1, source_target_pairs={{0,6},{1,3},{2,4},{3,1},{4,2},{5,7},{6,0},{7,5},{8,14},{9,11},{10,... | collective-permute-start | bytes 2162696 | tf_op jit(solution)/shard_map/ppermute | solution.py:160
  146.5 8.7 %shard_map.98 = f32[64,4096]{1,0:T(8,128)} custom-call(s32[192]{0:T(256)} %bitcast.14, bf16[352,1024]{1,0:T(8,128)(2,1)} %pad_maximum_fusion.refs_0_, bf16[352,1024]{1,0:T(8,128)(2,1)} %collective-permute-done.2.refs_1_, bf16[352,1024]{1,0:T(8,128)(2,1)} %collective-permute-done.1.refs_0_.refs_2_, bf16[352,1024]{1,0:T(8,128)(2,1)} %collective-permute-done.3.refs_1_.refs_3_, ...), custom_call_target="tpu_custom_call" | custom-call | flops 536870912 | bytes 8388608 | tf_op jit(solution)/shard_map/pallas_call | solution.py:221
  155.3 2.1 %shard_map.94 = bf16[2,160,1024]{2,1,0:T(8,128)(2,1)} custom-call(bf16[4,160,1024]{2,1,0:T(8,128)(2,1)} %get-tuple-element.22.refs_0_.refs_8_, bf16[4,160,1024]{2,1,0:T(8,128)(2,1)} %collective-permute-done.18.refs_1_.refs_9_), custom_call_target="tpu_custom_call" | custom-call | flops 655360 | bytes 1966080 | tf_op jit(solution)/shard_map/pallas_call | solution.py:113
  157.4 3.0 %collective-permute-start.19 = (bf16[2,160,1024]{2,1,0:T(8,128)(2,1)}, bf16[2,160,1024]{2,1,0:T(8,128)(2,1)}, u32[]{:S(2)}, u32[]{:S(2)}) collective-permute-start(bf16[2,160,1024]{2,1,0:T(8,128)(2,1)} %shard_map.94), channel_id=1, source_target_pairs={{0,96},{1,33},{2,98},{3,35},{4,100},{5,37},{6,102},{7,39},{8,104},... | collective-permute-start | bytes 1966088 | tf_op jit(solution)/shard_map/ppermute | solution.py:160
  160.4 2.1 %shard_map.91 = bf16[1,176,1024]{2,1,0:T(8,128)(2,1)} custom-call(bf16[4,176,1024]{2,1,0:T(8,128)(2,1)} %get-tuple-element.18.refs_0_, bf16[4,176,1024]{2,1,0:T(8,128)(2,1)} %collective-permute-done.12.refs_1_, bf16[2,176,1024]{2,1,0:T(8,128)(2,1)} %collective-permute-done.13.refs_2_), custom_call_target="tpu_custom_call" | custom-call | flops 540672 | bytes 1441792 | tf_op jit(solution)/shard_map/pallas_call | solution.py:113
  162.7 2.1 %shard_map.93 = bf16[1,176,1024]{2,1,0:T(8,128)(2,1)} custom-call(bf16[4,176,1024]{2,1,0:T(8,128)(2,1)} %get-tuple-element.20.refs_0_.refs_4_, bf16[4,176,1024]{2,1,0:T(8,128)(2,1)} %collective-permute-done.15.refs_1_.refs_5_, bf16[2,176,1024]{2,1,0:T(8,128)(2,1)} %collective-permute-done.16.refs_2_.refs_6_), custom_call_target="tpu_custom_call" | custom-call | flops 540672 | bytes 1441792 | tf_op jit(solution)/shard_map/pallas_call | solution.py:113
  165.3 4.2 %collective-permute-done.19.refs_2_.refs_10_ = bf16[2,160,1024]{2,1,0:T(8,128)(2,1)} collective-permute-done((bf16[2,160,1024]{2,1,0:T(8,128)(2,1)}, bf16[2,160,1024]{2,1,0:T(8,128)(2,1)}, u32[]{:S(2)}, u32[]{:S(2)}) %collective-permute-start.19) | collective-permute-done | bytes 655392 | tf_op jit(solution)/shard_map/ppermute | solution.py:160
  169.5 2.0 %shard_map.95 = bf16[1,160,1024]{2,1,0:T(8,128)(2,1)} custom-call(bf16[4,160,1024]{2,1,0:T(8,128)(2,1)} %get-tuple-element.22.refs_0_.refs_8_, bf16[4,160,1024]{2,1,0:T(8,128)(2,1)} %collective-permute-done.18.refs_1_.refs_9_, bf16[2,160,1024]{2,1,0:T(8,128)(2,1)} %collective-permute-done.19.refs_2_.refs_10_), custom_call_target="tpu_custom_call" | custom-call | flops 491520 | bytes 1310720 | tf_op jit(solution)/shard_map/pallas_call | solution.py:113
  172.1 8.1 %collective-permute-done.20.refs_11_ = bf16[1,160,1024]{2,1,0:T(8,128)(2,1)} collective-permute-done((bf16[1,160,1024]{2,1,0:T(8,128)(2,1)}, bf16[1,160,1024]{2,1,0:T(8,128)(2,1)}, u32[]{:S(2)}, u32[]{:S(2)}) %collective-permute-start.20) | collective-permute-done | bytes 327712 | tf_op jit(solution)/shard_map/ppermute | solution.py:160
  180.2 3.4 %shard_map.96 = bf16[512,1024]{1,0:T(8,128)(2,1)} custom-call(bf16[4,176,1024]{2,1,0:T(8,128)(2,1)} %get-tuple-element.18.refs_0_, bf16[4,176,1024]{2,1,0:T(8,128)(2,1)} %collective-permute-done.12.refs_1_, bf16[2,176,1024]{2,1,0:T(8,128)(2,1)} %collective-permute-done.13.refs_2_, bf16[1,176,1024]{2,1,0:T(8,128)(2,1)} %collective-permute-done.14.refs_3_, ...), custom_call_target="tpu_custom_call" | custom-call | flops 2097152 | bytes 5242880 | tf_op jit(solution)/shard_map/pallas_call | solution.py:141
  183.5 3.7 %all-to-all-start.2 = ((bf16[8,64,1024]{2,1,0:T(8,128)(2,1)}), bf16[8,64,1024]{2,1,0:T(8,128)(2,1)S(1)}, u32[]{:S(2)}, u32[]{:S(2)}) async-start(bf16[8,64,1024]{2,1,0:T(8,128)(2,1)} %bitcast.35), calls=%async_computation.2 | async-start | bytes 2097152 | tf_op jit(solution)/shard_map/all_to_all | solution.py:82
  187.3 2.3 %add_multiply_fusion.1 = f32[64,4096]{1,0:T(8,128)} fusion(f32[64,4096]{1,0:T(8,128)S(1)} %copy-done.2, f32[64,4096]{1,0:T(8,128)} %collective-permute-done.22), kind=kLoop, calls=%fused_computation.1 | loop fusion | flops 524288 | bytes 3145728 | tf_op jit(solution)/shard_map/div | solution.py:523
  189.6 3.3 %fusion = f32[512,1024]{1,0:T(8,128)S(1)} fusion(bf16[1024,1024]{1,0:T(8,128)(2,1)} %collective-permute-done.21, s32[]{:T(128)S(6)} %select_n.9), kind=kOutput, calls=%fused_computation.2 | convolution fusion | flops 1073741824 | bytes 5242884 | tf_op jit(solution)/shard_map/dot_general | solution.py:520
  192.9 2.6 %add_multiply_fusion = f32[512,1024]{1,0:T(8,128)} fusion(f32[512,1024]{1,0:T(8,128)S(1)} %fusion, bf16[1024,1024]{1,0:T(8,128)(2,1)S(1)} %copy-done.4, s32[]{:T(128)S(6)} %select_n.9), kind=kOutput, calls=%fused_computation | convolution fusion | flops 1074790400 | bytes 7340036 | tf_op jit(solution)/shard_map/dot_general | solution.py:520
  195.5 2.9 %all-to-all-done.2.pieces = bf16[8,64,1024]{2,1,0:T(8,128)(2,1)S(1)} async-done(((bf16[8,64,1024]{2,1,0:T(8,128)(2,1)}), bf16[8,64,1024]{2,1,0:T(8,128)(2,1)S(1)}, u32[]{:S(2)}, u32[]{:S(2)}) %all-to-all-start.2) | async-done | bytes 1048608 | tf_op jit(solution)/shard_map/all_to_all | solution.py:82
  198.4 0.9 shard_map.97
  (41 shorter events, 3.7 us)
Async XLA Ops:
  17.9 8.7 %collective-permute-start = (bf16[176,1024]{1,0:T(8,128)(2,1)S(1)}, bf16[176,1024]{1,0:T(8,128)(2,1)S(1)}, u32[]{:S(2)}, u32[]{:S(2)}) collective-permute-start(bf16[176,1024]{1,0:T(8,128)(2,1)S(1)} %get-tuple-element.25), channel_id=1, source_target_pairs={{0,96},{1,33},{2,98},{3,35},{4,100},{5,37},{6,102},{7,39},{8,104},... | collective-permute-start | bytes 1081352 | tf_op jit(solution)/shard_map/ppermute | solution.py:91
  20.0 10.2 %collective-permute-start.4 = (bf16[176,1024]{1,0:T(8,128)(2,1)S(1)}, bf16[176,1024]{1,0:T(8,128)(2,1)S(1)}, u32[]{:S(2)}, u32[]{:S(2)}) collective-permute-start(bf16[176,1024]{1,0:T(8,128)(2,1)S(1)} %get-tuple-element.24), channel_id=1, source_target_pairs={{0,24},{1,9},{2,26},{3,11},{4,28},{5,13},{6,30},{7,15},{8,16},{9,1... | collective-permute-start | bytes 1081352 | tf_op jit(solution)/shard_map/ppermute | solution.py:91
  22.7 10.3 %collective-permute-start.8 = (bf16[160,1024]{1,0:T(8,128)(2,1)S(1)}, bf16[160,1024]{1,0:T(8,128)(2,1)S(1)}, u32[]{:S(2)}, u32[]{:S(2)}) collective-permute-start(bf16[160,1024]{1,0:T(8,128)(2,1)S(1)} %slice.14), channel_id=1, source_target_pairs={{0,6},{1,3},{2,4},{3,1},{4,2},{5,7},{6,0},{7,5},{8,14},{9,11},{10,... | collective-permute-start | bytes 983048 | tf_op jit(solution)/shard_map/ppermute | solution.py:91
  27.6 22.4 %collective-permute-start.2 = (bf16[352,1024]{1,0:T(8,128)(2,1)}, bf16[352,1024]{1,0:T(8,128)(2,1)}, u32[]{:S(2)}, u32[]{:S(2)}) collective-permute-start(bf16[352,1024]{1,0:T(8,128)(2,1)} %pad_maximum_fusion.refs_0_), channel_id=1, source_target_pairs={{0,24},{1,9},{2,26},{3,11},{4,28},{5,13},{6,30},{7,15},{8,16},{9,1... | collective-permute-start | bytes 2162696 | tf_op jit(solution)/shard_map/ppermute | solution.py:91
  31.2 20.7 %collective-permute-start.6 = (bf16[352,1024]{1,0:T(8,128)(2,1)}, bf16[352,1024]{1,0:T(8,128)(2,1)}, u32[]{:S(2)}, u32[]{:S(2)}) collective-permute-start(bf16[352,1024]{1,0:T(8,128)(2,1)} %pad_maximum_fusion.1.refs_2_.refs_4_), channel_id=1, source_target_pairs={{0,6},{1,3},{2,4},{3,1},{4,2},{5,7},{6,0},{7,5},{8,14},{9,11},{10,... | collective-permute-start | bytes 2162696 | tf_op jit(solution)/shard_map/ppermute | solution.py:91
  33.0 32.9 %copy-start.1 = (bf16[320,1024]{1,0:T(8,128)(2,1)}, bf16[320,1024]{1,0:T(8,128)(2,1)S(1)}, u32[]{:S(2)}) copy-start(bf16[320,1024]{1,0:T(8,128)(2,1)S(1)} %pad_maximum_fusion.2.refs_4_.refs_8_) | copy-start | bytes 1966084
  33.0 12.0 %collective-permute-start.10 = (bf16[320,1024]{1,0:T(8,128)(2,1)S(1)}, bf16[320,1024]{1,0:T(8,128)(2,1)}, u32[]{:S(2)}, u32[]{:S(2)}) collective-permute-start(bf16[320,1024]{1,0:T(8,128)(2,1)S(1)} %pad_maximum_fusion.2.refs_4_.refs_8_), channel_id=1, source_target_pairs={{0,96},{1,33},{2,98},{3,35},{4,100},{5,37},{6,102},{7,39},{8,104},... | collective-permute-start | bytes 1966088 | tf_op jit(solution)/shard_map/ppermute | solution.py:91
  35.1 12.2 %collective-permute-start.9 = (bf16[320,1024]{1,0:T(8,128)(2,1)S(1)}, bf16[320,1024]{1,0:T(8,128)(2,1)S(1)}, u32[]{:S(2)}, u32[]{:S(2)}) collective-permute-start(bf16[320,1024]{1,0:T(8,128)(2,1)S(1)} %pad_maximum_fusion.2.refs_4_.refs_8_), channel_id=1, source_target_pairs={{0,24},{1,9},{2,26},{3,11},{4,28},{5,13},{6,30},{7,15},{8,16},{9,1... | collective-permute-start | bytes 1966088 | tf_op jit(solution)/shard_map/ppermute | solution.py:91
  36.4 29.5 %copy-start = (s32[1,192]{1,0:T(1,128)}, s32[1,192]{1,0:T(1,128)S(1)}, u32[]{:S(2)}) copy-start(s32[1,192]{1,0:T(1,128)S(1)} %constant_dynamic-slice_fusion) | copy-start | bytes 2308
  36.4 40.0 %collective-permute-start.1 = (bf16[352,1024]{1,0:T(8,128)(2,1)}, bf16[352,1024]{1,0:T(8,128)(2,1)}, u32[]{:S(2)}, u32[]{:S(2)}) collective-permute-start(bf16[352,1024]{1,0:T(8,128)(2,1)} %pad_maximum_fusion.refs_0_), channel_id=1, source_target_pairs={{0,6},{1,3},{2,4},{3,1},{4,2},{5,7},{6,0},{7,5},{8,14},{9,11},{10,... | collective-permute-start | bytes 2162696 | tf_op jit(solution)/shard_map/ppermute | solution.py:91
  45.0 31.4 %collective-permute-start.5 = (bf16[352,1024]{1,0:T(8,128)(2,1)}, bf16[352,1024]{1,0:T(8,128)(2,1)}, u32[]{:S(2)}, u32[]{:S(2)}) collective-permute-start(bf16[352,1024]{1,0:T(8,128)(2,1)} %pad_maximum_fusion.1.refs_2_.refs_4_), channel_id=1, source_target_pairs={{0,96},{1,33},{2,98},{3,35},{4,100},{5,37},{6,102},{7,39},{8,104},... | collective-permute-start | bytes 2162696 | tf_op jit(solution)/shard_map/ppermute | solution.py:91
  47.3 18.6 %copy-start.3 = (bf16[320,1024]{1,0:T(8,128)(2,1)}, bf16[320,1024]{1,0:T(8,128)(2,1)S(1)}, u32[]{:S(2)}) copy-start(bf16[320,1024]{1,0:T(8,128)(2,1)S(1)} %collective-permute-done.9.refs_4_.refs_10_) | copy-start | bytes 1966084
  47.3 29.1 %collective-permute-start.11 = (bf16[320,1024]{1,0:T(8,128)(2,1)}, bf16[320,1024]{1,0:T(8,128)(2,1)}, u32[]{:S(2)}, u32[]{:S(2)}) collective-permute-start(bf16[320,1024]{1,0:T(8,128)(2,1)} %collective-permute-done.10.refs_5_.refs_9_), channel_id=1, source_target_pairs={{0,24},{1,9},{2,26},{3,11},{4,28},{5,13},{6,30},{7,15},{8,16},{9,1... | collective-permute-start | bytes 1966088 | tf_op jit(solution)/shard_map/ppermute | solution.py:91
  50.0 26.5 %collective-permute-start.3 = (bf16[352,1024]{1,0:T(8,128)(2,1)}, bf16[352,1024]{1,0:T(8,128)(2,1)}, u32[]{:S(2)}, u32[]{:S(2)}) collective-permute-start(bf16[352,1024]{1,0:T(8,128)(2,1)} %collective-permute-done.2.refs_1_), channel_id=1, source_target_pairs={{0,6},{1,3},{2,4},{3,1},{4,2},{5,7},{6,0},{7,5},{8,14},{9,11},{10,... | collective-permute-start | bytes 2162696 | tf_op jit(solution)/shard_map/ppermute | solution.py:91
  51.8 24.6 %collective-permute-start.7 = (bf16[352,1024]{1,0:T(8,128)(2,1)}, bf16[352,1024]{1,0:T(8,128)(2,1)}, u32[]{:S(2)}, u32[]{:S(2)}) collective-permute-start(bf16[352,1024]{1,0:T(8,128)(2,1)} %collective-permute-done.6.refs_3_.refs_5_), channel_id=1, source_target_pairs={{0,96},{1,33},{2,98},{3,35},{4,100},{5,37},{6,102},{7,39},{8,104},... | collective-permute-start | bytes 2162696 | tf_op jit(solution)/shard_map/ppermute | solution.py:91
  53.8 12.1 %copy-start.5 = (s32[1024]{0:T(1024)S(1)}, s32[1024]{0:T(1024)}, u32[]{:S(2)}) copy-start(s32[1024]{0:T(1024)} %param.7) | copy-start | bytes 12292
  88.0 17.4 %all-to-all-start.1 = ((f32[64,16,128]{2,1,0:T(8,128)}), f32[64,16,128]{2,1,0:T(8,128)}, u32[]{:S(2)}, u32[]{:S(2)}) async-start(f32[64,16,128]{2,1,0:T(8,128)} %get-tuple-element.14), calls=%async_computation.1 | async-start | bytes 1048576 | tf_op jit(solution)/shard_map/all_to_all | solution.py:509
  118.0 20.6 %collective-permute-start.12 = (bf16[4,176,1024]{2,1,0:T(8,128)(2,1)}, bf16[4,176,1024]{2,1,0:T(8,128)(2,1)}, u32[]{:S(2)}, u32[]{:S(2)}) collective-permute-start(bf16[4,176,1024]{2,1,0:T(8,128)(2,1)} %get-tuple-element.19), channel_id=1, source_target_pairs={{0,6},{1,3},{2,4},{3,1},{4,2},{5,7},{6,0},{7,5},{8,14},{9,11},{10,... | collective-permute-start | bytes 4325384 | tf_op jit(solution)/shard_map/ppermute | solution.py:160
  118.9 22.7 %collective-permute-start.15 = (bf16[4,176,1024]{2,1,0:T(8,128)(2,1)}, bf16[4,176,1024]{2,1,0:T(8,128)(2,1)}, u32[]{:S(2)}, u32[]{:S(2)}) collective-permute-start(bf16[4,176,1024]{2,1,0:T(8,128)(2,1)} %get-tuple-element.21), channel_id=1, source_target_pairs={{0,96},{1,33},{2,98},{3,35},{4,100},{5,37},{6,102},{7,39},{8,104},... | collective-permute-start | bytes 4325384 | tf_op jit(solution)/shard_map/ppermute | solution.py:160
  121.9 33.4 %collective-permute-start.18 = (bf16[4,160,1024]{2,1,0:T(8,128)(2,1)}, bf16[4,160,1024]{2,1,0:T(8,128)(2,1)}, u32[]{:S(2)}, u32[]{:S(2)}) collective-permute-start(bf16[4,160,1024]{2,1,0:T(8,128)(2,1)} %get-tuple-element.23), channel_id=1, source_target_pairs={{0,24},{1,9},{2,26},{3,11},{4,28},{5,13},{6,30},{7,15},{8,16},{9,1... | collective-permute-start | bytes 3932168 | tf_op jit(solution)/shard_map/ppermute | solution.py:160
  124.7 64.9 %collective-permute-start.21 = (bf16[1024,1024]{1,0:T(8,128)(2,1)}, bf16[1024,1024]{1,0:T(8,128)(2,1)}, u32[]{:S(2)}, u32[]{:S(2)}) collective-permute-start(bf16[1024,1024]{1,0:T(8,128)(2,1)} %get-tuple-element.17.refs_10_), channel_id=1, source_target_pairs={{0,1},{1,0},{2,3},{3,2},{4,5},{5,4},{6,7},{7,6},{8,9},{9,8},{10,11... | collective-permute-start | bytes 6291464 | tf_op jit(solution)/shard_map/ppermute | solution.py:522
  140.8 19.6 %collective-permute-start.13 = (bf16[2,176,1024]{2,1,0:T(8,128)(2,1)}, bf16[2,176,1024]{2,1,0:T(8,128)(2,1)}, u32[]{:S(2)}, u32[]{:S(2)}) collective-permute-start(bf16[2,176,1024]{2,1,0:T(8,128)(2,1)} %shard_map.90), channel_id=1, source_target_pairs={{0,24},{1,9},{2,26},{3,11},{4,28},{5,13},{6,30},{7,15},{8,16},{9,1... | collective-permute-start | bytes 2162696 | tf_op jit(solution)/shard_map/ppermute | solution.py:160
  143.8 18.9 %collective-permute-start.16 = (bf16[2,176,1024]{2,1,0:T(8,128)(2,1)}, bf16[2,176,1024]{2,1,0:T(8,128)(2,1)}, u32[]{:S(2)}, u32[]{:S(2)}) collective-permute-start(bf16[2,176,1024]{2,1,0:T(8,128)(2,1)} %shard_map.92), channel_id=1, source_target_pairs={{0,6},{1,3},{2,4},{3,1},{4,2},{5,7},{6,0},{7,5},{8,14},{9,11},{10,... | collective-permute-start | bytes 2162696 | tf_op jit(solution)/shard_map/ppermute | solution.py:160
  155.2 32.1 %collective-permute-start.22 = (f32[64,4096]{1,0:T(8,128)}, f32[64,4096]{1,0:T(8,128)}, u32[]{:S(2)}, u32[]{:S(2)}) collective-permute-start(f32[64,4096]{1,0:T(8,128)} %shard_map.98), channel_id=1, source_target_pairs={{0,1},{1,0},{2,3},{3,2},{4,5},{5,4},{6,7},{7,6},{8,9},{9,8},{10,11... | collective-permute-start | bytes 3145736 | tf_op jit(solution)/shard_map/ppermute | solution.py:523
  157.4 12.1 %collective-permute-start.19 = (bf16[2,160,1024]{2,1,0:T(8,128)(2,1)}, bf16[2,160,1024]{2,1,0:T(8,128)(2,1)}, u32[]{:S(2)}, u32[]{:S(2)}) collective-permute-start(bf16[2,160,1024]{2,1,0:T(8,128)(2,1)} %shard_map.94), channel_id=1, source_target_pairs={{0,96},{1,33},{2,98},{3,35},{4,100},{5,37},{6,102},{7,39},{8,104},... | collective-permute-start | bytes 1966088 | tf_op jit(solution)/shard_map/ppermute | solution.py:160
  162.5 17.7 %collective-permute-start.14 = (bf16[1,176,1024]{2,1,0:T(8,128)(2,1)}, bf16[1,176,1024]{2,1,0:T(8,128)(2,1)}, u32[]{:S(2)}, u32[]{:S(2)}) collective-permute-start(bf16[1,176,1024]{2,1,0:T(8,128)(2,1)} %shard_map.91), channel_id=1, source_target_pairs={{0,96},{1,33},{2,98},{3,35},{4,100},{5,37},{6,102},{7,39},{8,104},... | collective-permute-start | bytes 1081352 | tf_op jit(solution)/shard_map/ppermute | solution.py:160
  164.8 15.4 %collective-permute-start.17 = (bf16[1,176,1024]{2,1,0:T(8,128)(2,1)}, bf16[1,176,1024]{2,1,0:T(8,128)(2,1)}, u32[]{:S(2)}, u32[]{:S(2)}) collective-permute-start(bf16[1,176,1024]{2,1,0:T(8,128)(2,1)} %shard_map.93), channel_id=1, source_target_pairs={{0,24},{1,9},{2,26},{3,11},{4,28},{5,13},{6,30},{7,15},{8,16},{9,1... | collective-permute-start | bytes 1081352 | tf_op jit(solution)/shard_map/ppermute | solution.py:160
  171.5 8.6 %collective-permute-start.20 = (bf16[1,160,1024]{2,1,0:T(8,128)(2,1)}, bf16[1,160,1024]{2,1,0:T(8,128)(2,1)}, u32[]{:S(2)}, u32[]{:S(2)}) collective-permute-start(bf16[1,160,1024]{2,1,0:T(8,128)(2,1)} %shard_map.95), channel_id=1, source_target_pairs={{0,6},{1,3},{2,4},{3,1},{4,2},{5,7},{6,0},{7,5},{8,14},{9,11},{10,... | collective-permute-start | bytes 983048 | tf_op jit(solution)/shard_map/ppermute | solution.py:160
  183.5 3.7 %copy-start.2 = (f32[64,4096]{1,0:T(8,128)S(1)}, f32[64,4096]{1,0:T(8,128)}, u32[]{:S(2)}) copy-start(f32[64,4096]{1,0:T(8,128)} %shard_map.98) | copy-start | bytes 3145732
  183.5 14.9 %all-to-all-start.2 = ((bf16[8,64,1024]{2,1,0:T(8,128)(2,1)}), bf16[8,64,1024]{2,1,0:T(8,128)(2,1)S(1)}, u32[]{:S(2)}, u32[]{:S(2)}) async-start(bf16[8,64,1024]{2,1,0:T(8,128)(2,1)} %bitcast.35), calls=%async_computation.2 | async-start | bytes 2097152 | tf_op jit(solution)/shard_map/all_to_all | solution.py:82
  189.6 3.4 %copy-start.4 = (bf16[1024,1024]{1,0:T(8,128)(2,1)S(1)}, bf16[1024,1024]{1,0:T(8,128)(2,1)}, u32[]{:S(2)}) copy-start(bf16[1024,1024]{1,0:T(8,128)(2,1)} %get-tuple-element.17.refs_10_) | copy-start | bytes 6291460

commit v4 on v2

--- a/solution.py
+++ b/solution.py
@@ -117,13 +117,13 @@
         out_specs=block(0),
         out_shape=jax.ShapeDtypeStruct((count, rows, tokens), BF16),
         compiler_params=pltpu.CompilerParams(
-            dimension_semantics=("arbitrary",), vmem_limit_bytes=ALL_VMEM
+            dimension_semantics=("arbitrary",), vmem_limit_bytes=12 << 20
         ),
         cost_estimate=pl.CostEstimate(
             flops=len(terms) * count * rows * tokens,
             bytes_accessed=2 * (len(terms) + 1) * count * rows * tokens, transcendentals=0,
         ),
-    )(*[in_hbm(x) for x, _ in terms])
+    )(*[in_hbm(x) if x.shape[0] == 4 else x for x, _ in terms])
 
 
 def last_kernel(*refs):
@@ -147,12 +147,12 @@
         out_specs=pl.BlockSpec((sum(SIZES), part), lambda i: (0, i)),
         out_shape=jax.ShapeDtypeStruct((sum(SIZES), tokens), BF16),
         compiler_params=pltpu.CompilerParams(
-            dimension_semantics=("arbitrary",), vmem_limit_bytes=ALL_VMEM
+            dimension_semantics=("arbitrary",), vmem_limit_bytes=16 << 20
         ),
         cost_estimate=pl.CostEstimate(
             flops=4 * sum(SIZES) * tokens, bytes_accessed=10 * sum(SIZES) * tokens, transcendentals=0
         ),
-    )(*[in_hbm(x) for x in terms])
+    )(*[in_hbm(x) if x.shape[0] == 4 else x for x in terms])
 
 
 def summed_groups(sends, keeps):
@@ -236,48 +236,80 @@
     )(chips, *[in_hbm(x) for x in got], own)
 
 
-def turn_kernel(chips, w, wide, tall, turned):
+def columns_kernel(chips, w, wide):
+    rows = w.shape[0]
+    lane = lax.broadcasted_iota(jnp.int32, (rows, 128), 1)
+    for l in range(8):
+        for tile in range(4):
+            done = None
+            for g, group in enumerate(GROUPS):
+                for s, count, first in group:
+                    if s // 2 != tile:
+                        continue
+                    chip, side = chips[64 * g + 8 * l + s], s % 2
+                    block = w[:, pl.ds(pl.multiple_of(chip // 2 * 128, 128), 128)].astype(F32)
+                    block = pltpu.roll(block, 64 * (chip % 2 != side).astype(jnp.int32), 1)
+                    done = block if done is None else jnp.where(
+                        lane >= 64 * side + first, block, done
+                    )
+            wide[:, (4 * l + tile) * 128 : (4 * l + tile + 1) * 128] = done.astype(BF16)
+
+
+def columns_turned(chips, w):
+    vocab_rows, width = w.shape
+    block = pl.BlockSpec((128, width), lambda i, t: (i, 0))
+    return pl.pallas_call(
+        columns_kernel,
+        grid_spec=pltpu.PrefetchScalarGridSpec(
+            num_scalar_prefetch=1, grid=(vocab_rows // 128,), in_specs=[block], out_specs=block
+        ),
+        out_shape=pltpu.HBM((vocab_rows, width), BF16),
+        compiler_params=pltpu.CompilerParams(
+            dimension_semantics=("arbitrary",), vmem_limit_bytes=24 << 20
+        ),
+        cost_estimate=pl.CostEstimate(
+            flops=1024 * vocab_rows * width, bytes_accessed=4 * vocab_rows * width, transcendentals=0
+        ),
+    )(chips, in_hbm(w))
+
+
+def rows_kernel(chips, w, tall, turned, sem):
     step = pl.program_id(0)
     size = w.shape[1]
-
-    @pl.when(step < 8)
-    def _():
-        turned[pl.ds(pl.multiple_of(step * size, size), size)] = w[...].T
-
-    @pl.when(step >= 8)
-    def _():
-        pieces = []
+    turned[pl.ds(pl.multiple_of(step * size, size), size)] = w[...].T
+
+    @pl.when(step == pl.num_programs(0) - 1)
+    def _():
         for g, group in enumerate(GROUPS):
-            for s, count, first in group:
-                at = pl.multiple_of(chips[64 * g + 8 * (step - 8) + s] * 64 + first, 16)
-                pieces.append(turned[pl.ds(at, count)])
-        rows = jnp.concatenate(pieces, axis=0)
-        tall[...] = rows
-        wide[...] = rows.T
-
-
-def turned_weights(chips, w):
+            for l in range(8):
+                at = l * sum(SIZES) + STARTS[g]
+                for s, count, first in group:
+                    src = pl.multiple_of(chips[64 * g + 8 * l + s] * 64 + first, 16)
+                    pltpu.make_async_copy(
+                        turned.at[pl.ds(src, count)], tall.at[pl.ds(at, count)], sem
+                    ).start()
+                    at += count
+        pltpu.make_async_copy(tall, tall, sem).wait()
+
+
+def rows_turned(chips, w):
     vocab_rows, width = w.shape
     size = width // 8
-    late = lambda i: jnp.maximum(i - 8, 0)
-    return pl.pallas_call(
-        turn_kernel,
+    return pl.pallas_call(
+        rows_kernel,
         grid_spec=pltpu.PrefetchScalarGridSpec(
             num_scalar_prefetch=1,
-            grid=(16,),
-            in_specs=[pl.BlockSpec((vocab_rows, size), lambda i, t: (0, jnp.minimum(i, 7)))],
-            out_specs=[
-                pl.BlockSpec((vocab_rows, size), lambda i, t: (0, late(i))),
-                pl.BlockSpec((size, vocab_rows), lambda i, t: (late(i), 0)),
-            ],
-            scratch_shapes=[pltpu.VMEM((width, vocab_rows), BF16)],
-        ),
-        out_shape=[pltpu.HBM((vocab_rows, width), BF16), pltpu.HBM((width, vocab_rows), BF16)],
-        compiler_params=pltpu.CompilerParams(
-            dimension_semantics=("arbitrary",), vmem_limit_bytes=32 << 20
-        ),
-        cost_estimate=pl.CostEstimate(
-            flops=2048 * vocab_rows * width, bytes_accessed=6 * vocab_rows * width, transcendentals=0
+            grid=(8,),
+            in_specs=[pl.BlockSpec((vocab_rows, size), lambda i, t: (0, i))],
+            out_specs=pl.BlockSpec(memory_space=pl.ANY),
+            scratch_shapes=[pltpu.VMEM((width, vocab_rows), BF16), pltpu.SemaphoreType.DMA],
+        ),
+        out_shape=pltpu.HBM((width, vocab_rows), BF16),
+        compiler_params=pltpu.CompilerParams(
+            dimension_semantics=("arbitrary",), vmem_limit_bytes=24 << 20
+        ),
+        cost_estimate=pl.CostEstimate(
+            flops=1024 * vocab_rows * width, bytes_accessed=4 * vocab_rows * width, transcendentals=0
         ),
     )(chips, in_hbm(w))
 
@@ -356,7 +388,7 @@
         + [pltpu.VMEM((1, tokens), F32)] * (3 if late else 0)
         + [pltpu.SemaphoreType.DMA],
         compiler_params=pltpu.CompilerParams(
-            dimension_semantics=("arbitrary",), vmem_limit_bytes=ALL_VMEM
+            dimension_semantics=("arbitrary",), vmem_limit_bytes=32 << 20
         ),
         cost_estimate=pl.CostEstimate(
             flops=vocab_rows * width * tokens,
@@ -471,11 +503,12 @@
     chips = lax.dynamic_index_in_dim(jnp.asarray(CHIPS), lax.axis_index(ALL), 0, keepdims=False)
     tgt = (targets - lax.axis_index(VOCAB) * vocab_rows)[None, :]
     some = small_stage(jnp.broadcast_to(own[None], (8, feats, tokens)))
-    wide, tall = turned_weights(chips, head_weight)
+    wide = columns_turned(chips, head_weight)
     got = gathered_groups(some.reshape(8 * feats, tokens))
     part = half_logits(0, [a for group in got for a in group[:2]], wide)
     logits, stats = half_logits(1, [a for group in got for a in group[2:]], wide, part, tgt)
     stats = lax.all_to_all(stats, VOCAB, 0, 0, tiled=True)
+    tall = rows_turned(chips, head_weight)
     a_part = a_part_of(chips, [a for group in got for a in group], own)
     grad, tok_loss, sends = signal_of(stats, logits, loss_cot[None, :], tgt, tall)
     sums = summed_groups(sends, half_grads(0, tall, grad))

time: 202 us -> 198 us (0.980)
  blocking collectives: 33.7 us -> 16.2 us
  starting transfers between devices: 39.6 us -> 47.6 us
  waiting for transfers between devices: 31 us -> 35.6 us
  Pallas kernels: 81.7 us -> 86 us
  other arithmetic: 4.82 us -> 2.44 us
    all_to_all x1 -> x0, blocking collectives: 17.5 us -> none  [body(): stats = lax.all_to_all(stats, VOCAB, 0, 0, tiled=True)]
    pallas_call x1 -> x2, Pallas kernels: 15.2 us -> 22.8 us  [the longest x1 12.1 us: columns_turned(): pl.pallas_call(columns_kernel, grid_spec=pltpu.PrefetchScalarGridSpec(num...]
    all_to_all x0 -> x1, starting transfers between devices: none -> 5.5 us  [body(): stats = lax.all_to_all(stats, VOCAB, 0, 0, tiled=True)]
    ppermute x9, starting transfers between devices: 12.1 us -> 16.4 us  [trade(): return lax.ppermute(x, ALL, LARGE_PAIRS[(g + step) % 3])]
    ppermute x12, waiting for transfers between devices: 9.53 us -> 13.8 us  [get(): return lax.ppermute(x, ALL, LARGE_PAIRS[(g + step) % 3])]
    pallas_call x6, Pallas kernels: 12.6 us -> 9.51 us  [add_up(): pl.pallas_call(add_kernel, grid=(count,), in_specs=[block(first) for _, f...]
  transfers between devices with their start and end apart: 24 -> 25, of which waited for: 7 -> 9; matrix products, arithmetic and copies ran while one was open for 6% -> 5% of each run, Pallas kernels for 29% -> 32%
where the time goes in v4:
time: 198 us; the launch traced here: 197 us
  Pallas kernels  86 us (43%)
  starting transfers between devices  47.6 us (24%)
  waiting for transfers between devices  35.6 us (18%)
  blocking collectives  16.2 us (8%)
  matrix products  5.96 us (3%)
  other arithmetic  2.44 us (1%)
    ppermute x12, starting transfers between devices, get(): return lax.ppermute(x, ALL, LARGE_PAIRS[(g + step) % 3])  21.9 us
    pallas_call x2, Pallas kernels, half_logits(): pl.pallas_call(late_kernel if late else early_kernel, grid=(vocab_rows //...  21.6 us
    ppermute x9, waiting for transfers between devices, trade(): return lax.ppermute(x, ALL, LARGE_PAIRS[(g + step) % 3])  17.8 us
    ppermute x9, starting transfers between devices, trade(): return lax.ppermute(x, ALL, LARGE_PAIRS[(g + step) % 3])  16.4 us
    all_to_all x1, blocking collectives, small_stage(): lax.all_to_all(x, ALL, 0, 0, axis_index_groups=SMALL_CUBES, tiled=True)  16.2 us
    ppermute x12, waiting for transfers between devices, get(): return lax.ppermute(x, ALL, LARGE_PAIRS[(g + step) % 3])  13.8 us
    pallas_call x1, Pallas kernels, columns_turned(): pl.pallas_call(columns_kernel, grid_spec=pltpu.PrefetchScalarGridSpec(num...  12.1 us
    pallas_call x1, Pallas kernels, signal_of(): pl.pallas_call(signal_kernel, grid=(count + 4,), in_specs=[whole(*stats.s...  11.5 us
  transfers between devices with their start and end apart: 25, of which 9 were waited for; matrix products, arithmetic and copies ran while one was open for 5% of the time, Pallas kernels for 32%

profile of v4, /device:TPU:0, one launch (start us, length us, event | category | flops | bytes accessed | tf_op | source)
XLA Modules:
  0.0 196.5 jit_solution(17890869852334409266)
XLA Ops:
  0.6 1.0 broadcast_in_dim.12
  1.7 16.2 %all_to_all.15 = bf16[8,64,1024]{2,1,0:T(8,128)(2,1)S(1)} all-to-all(bf16[8,64,1024]{2,1,0:T(8,128)(2,1)S(1)} %broadcast_in_dim.12), channel_id=1, replica_groups={{0,2,8,10,32,34,40,42},{4,6,12,14,36,38,44,46},{16,18,24,26,48,50,56,58..., dimensions={0} | all-to-all | bytes 2097152 | tf_op jit(solution)/shard_map/all_to_all | solution.py:82
  17.9 2.4 %collective-permute-start.4 = (bf16[176,1024]{1,0:T(8,128)(2,1)S(1)}, bf16[176,1024]{1,0:T(8,128)(2,1)S(1)}, u32[]{:S(2)}, u32[]{:S(2)}) collective-permute-start(bf16[176,1024]{1,0:T(8,128)(2,1)S(1)} %get-tuple-element.24), channel_id=1, source_target_pairs={{0,24},{1,9},{2,26},{3,11},{4,28},{5,13},{6,30},{7,15},{8,16},{9,1... | collective-permute-start | bytes 1081352 | tf_op jit(solution)/shard_map/ppermute | solution.py:91
  20.3 2.4 %collective-permute-start = (bf16[176,1024]{1,0:T(8,128)(2,1)S(1)}, bf16[176,1024]{1,0:T(8,128)(2,1)S(1)}, u32[]{:S(2)}, u32[]{:S(2)}) collective-permute-start(bf16[176,1024]{1,0:T(8,128)(2,1)S(1)} %get-tuple-element.25), channel_id=1, source_target_pairs={{0,96},{1,33},{2,98},{3,35},{4,100},{5,37},{6,102},{7,39},{8,104},... | collective-permute-start | bytes 1081352 | tf_op jit(solution)/shard_map/ppermute | solution.py:91
  22.7 1.9 collective-permute-start.8
  24.6 2.7 %collective-permute-done.4 = bf16[176,1024]{1,0:T(8,128)(2,1)S(1)} collective-permute-done((bf16[176,1024]{1,0:T(8,128)(2,1)S(1)}, bf16[176,1024]{1,0:T(8,128)(2,1)S(1)}, u32[]{:S(2)}, u32[]{:S(2)}) %collective-permute-start.4) | collective-permute-done | bytes 360480 | tf_op jit(solution)/shard_map/ppermute | solution.py:91
  27.4 1.4 collective-permute-start.6
  29.0 2.4 %collective-permute-start.2 = (bf16[352,1024]{1,0:T(8,128)(2,1)S(1)}, bf16[352,1024]{1,0:T(8,128)(2,1)S(1)}, u32[]{:S(2)}, u32[]{:S(2)}) collective-permute-start(bf16[352,1024]{1,0:T(8,128)(2,1)S(1)} %pad_maximum_fusion.refs_0_), channel_id=1, source_target_pairs={{0,24},{1,9},{2,26},{3,11},{4,28},{5,13},{6,30},{7,15},{8,16},{9,1... | collective-permute-start | bytes 2162696 | tf_op jit(solution)/shard_map/ppermute | solution.py:91
  31.5 2.1 %collective-permute-start.10 = (bf16[320,1024]{1,0:T(8,128)(2,1)S(1)}, bf16[320,1024]{1,0:T(8,128)(2,1)}, u32[]{:S(2)}, u32[]{:S(2)}) collective-permute-start(bf16[320,1024]{1,0:T(8,128)(2,1)S(1)} %pad_maximum_fusion.2.refs_4_.refs_8_), channel_id=1, source_target_pairs={{0,96},{1,33},{2,98},{3,35},{4,100},{5,37},{6,102},{7,39},{8,104},... | collective-permute-start | bytes 1966088 | tf_op jit(solution)/shard_map/ppermute | solution.py:91
  33.6 1.3 collective-permute-start.9
  35.6 0.9 collective-permute-start.5
  36.4 7.1 %collective-permute-done.10.refs_5_.refs_9_ = bf16[320,1024]{1,0:T(8,128)(2,1)} collective-permute-done((bf16[320,1024]{1,0:T(8,128)(2,1)S(1)}, bf16[320,1024]{1,0:T(8,128)(2,1)}, u32[]{:S(2)}, u32[]{:S(2)}) %collective-permute-start.10) | collective-permute-done | bytes 655392 | tf_op jit(solution)/shard_map/ppermute | solution.py:91
  43.5 1.5 collective-permute-start.1
  45.0 3.8 %collective-permute-done.9.refs_4_.refs_10_ = bf16[320,1024]{1,0:T(8,128)(2,1)} collective-permute-done((bf16[320,1024]{1,0:T(8,128)(2,1)S(1)}, bf16[320,1024]{1,0:T(8,128)(2,1)}, u32[]{:S(2)}, u32[]{:S(2)}) %collective-permute-start.9) | collective-permute-done | bytes 655392 | tf_op jit(solution)/shard_map/ppermute | solution.py:91
  48.8 2.3 %collective-permute-start.11 = (bf16[320,1024]{1,0:T(8,128)(2,1)}, bf16[320,1024]{1,0:T(8,128)(2,1)}, u32[]{:S(2)}, u32[]{:S(2)}) collective-permute-start(bf16[320,1024]{1,0:T(8,128)(2,1)} %collective-permute-done.10.refs_5_.refs_9_), channel_id=1, source_target_pairs={{0,24},{1,9},{2,26},{3,11},{4,28},{5,13},{6,30},{7,15},{8,16},{9,1... | collective-permute-start | bytes 1966088 | tf_op jit(solution)/shard_map/ppermute | solution.py:91
  51.1 2.0 %collective-permute-start.7 = (bf16[352,1024]{1,0:T(8,128)(2,1)S(1)}, bf16[352,1024]{1,0:T(8,128)(2,1)}, u32[]{:S(2)}, u32[]{:S(2)}) collective-permute-start(bf16[352,1024]{1,0:T(8,128)(2,1)S(1)} %collective-permute-done.6.refs_3_.refs_5_), channel_id=1, source_target_pairs={{0,96},{1,33},{2,98},{3,35},{4,100},{5,37},{6,102},{7,39},{8,104},... | collective-permute-start | bytes 2162696 | tf_op jit(solution)/shard_map/ppermute | solution.py:91
  53.1 1.4 collective-permute-start.3
  54.5 12.1 %shard_map.84.refs_6_ = bf16[1024,4096]{1,0:T(8,128)(2,1)} custom-call(s32[192]{0:T(256)S(1)} %bitcast.10, bf16[1024,4096]{1,0:T(8,128)(2,1)} %w.3), custom_call_target="tpu_custom_call" | custom-call | flops 4294967296 | bytes 16777216 | tf_op jit(solution)/shard_map/pallas_call | solution.py:261
  66.6 10.1 %shard_map.85.refs_7_ = f32[1024,1024]{1,0:T(8,128)} custom-call(bf16[352,1024]{1,0:T(8,128)(2,1)S(1)} %pad_maximum_fusion.refs_0_, bf16[352,1024]{1,0:T(8,128)(2,1)S(1)} %collective-permute-done.2.refs_1_, bf16[352,1024]{1,0:T(8,128)(2,1)S(1)} %pad_maximum_fusion.1.refs_2_.refs_4_, bf16[352,1024]{1,0:T(8,128)(2,1)S(1)} %collective-permute-done.6.refs_3_.refs_5_, ...), custom_call_target="tpu_custom_call" | custom-call | flops 4294967296 | bytes 12582912 | tf_op jit(solution)/shard_map/pallas_call | solution.py:377
  76.8 11.5 %shard_map.86 = (f32[1024,1024]{1,0:T(8,128)}, f32[64,16,128]{2,1,0:T(8,128)}) custom-call(bf16[352,1024]{1,0:T(8,128)(2,1)} %collective-permute-done.1.refs_0_.refs_2_, bf16[352,1024]{1,0:T(8,128)(2,1)} %collective-permute-done.3.refs_1_.refs_3_, bf16[352,1024]{1,0:T(8,128)(2,1)} %collective-permute-done.5.refs_2_.refs_6_, ...), custom_call_target="tpu_custom_call" | custom-call | flops 4294967296 | bytes 12582912 | tf_op jit(solution)/shard_map/pallas_call | solution.py:377
  88.3 5.5 %all-to-all-start.1 = ((f32[64,16,128]{2,1,0:T(8,128)}), f32[64,16,128]{2,1,0:T(8,128)}, u32[]{:S(2)}, u32[]{:S(2)}) async-start(f32[64,16,128]{2,1,0:T(8,128)} %get-tuple-element.14), calls=%async_computation.1 | async-start | bytes 1048576 | tf_op jit(solution)/shard_map/all_to_all | solution.py:510
  93.8 10.7 %shard_map.87.tall = bf16[4096,1024]{1,0:T(8,128)(2,1)} custom-call(s32[192]{0:T(256)S(1)} %bitcast.11, bf16[1024,4096]{1,0:T(8,128)(2,1)} %w.3), custom_call_target="tpu_custom_call" | custom-call | flops 4294967296 | bytes 16777216 | tf_op jit(solution)/shard_map/pallas_call | solution.py:298
  104.5 1.2 all-to-all-done.1.stats
  105.7 11.5 %shard_map.88 = (bf16[1024,1024]{1,0:T(8,128)(2,1)}, f32[1,1024]{1,0:T(1,128)}, bf16[4,176,1024]{2,1,0:T(8,128)(2,1)}, bf16[4,176,1024]{2,1,0:T(8,128)(2,1)}, bf16[4,160,1024]{2,1,0:T(8,128)(2,1)}) custom-call(f32[64,16,128]{2,1,0:T(8,128)} %all-to-all-done.1.stats, f32[1024,1024]{1,0:T(8,128)} %get-tuple-element.15.logits, f32[1,1024]{1,0:T(1,128)} %bitcast.20, ...), custom_call_target="tpu_custom_call" | custom-call | flops 4294967296 | bytes 14680064 | tf_op jit(solution)/shard_map/pallas_call | solution.py:441
  117.2 1.8 collective-permute-start.15
  119.0 2.7 %collective-permute-start.12 = (bf16[4,176,1024]{2,1,0:T(8,128)(2,1)}, bf16[4,176,1024]{2,1,0:T(8,128)(2,1)}, u32[]{:S(2)}, u32[]{:S(2)}) collective-permute-start(bf16[4,176,1024]{2,1,0:T(8,128)(2,1)} %get-tuple-element.19), channel_id=1, source_target_pairs={{0,6},{1,3},{2,4},{3,1},{4,2},{5,7},{6,0},{7,5},{8,14},{9,11},{10,... | collective-permute-start | bytes 4325384 | tf_op jit(solution)/shard_map/ppermute | solution.py:160
  121.7 2.8 %collective-permute-start.18 = (bf16[4,160,1024]{2,1,0:T(8,128)(2,1)}, bf16[4,160,1024]{2,1,0:T(8,128)(2,1)}, u32[]{:S(2)}, u32[]{:S(2)}) collective-permute-start(bf16[4,160,1024]{2,1,0:T(8,128)(2,1)} %get-tuple-element.23), channel_id=1, source_target_pairs={{0,24},{1,9},{2,26},{3,11},{4,28},{5,13},{6,30},{7,15},{8,16},{9,1... | collective-permute-start | bytes 3932168 | tf_op jit(solution)/shard_map/ppermute | solution.py:160
  124.4 8.2 %shard_map.89 = (bf16[4,176,1024]{2,1,0:T(8,128)(2,1)}, bf16[4,176,1024]{2,1,0:T(8,128)(2,1)}, bf16[4,160,1024]{2,1,0:T(8,128)(2,1)}) custom-call(bf16[4096,1024]{1,0:T(8,128)(2,1)} %shard_map.87.tall, bf16[1024,1024]{1,0:T(8,128)(2,1)} %get-tuple-element.17.grad), custom_call_target="tpu_custom_call" | custom-call | flops 4294967296 | bytes 8388608 | tf_op jit(solution)/shard_map/pallas_call | solution.py:479
  132.6 5.1 %collective-permute-done.15.refs_1_.refs_5_ = bf16[4,176,1024]{2,1,0:T(8,128)(2,1)} collective-permute-done((bf16[4,176,1024]{2,1,0:T(8,128)(2,1)}, bf16[4,176,1024]{2,1,0:T(8,128)(2,1)}, u32[]{:S(2)}, u32[]{:S(2)}) %collective-permute-start.15) | collective-permute-done | bytes 1441824 | tf_op jit(solution)/shard_map/ppermute | solution.py:160
  137.7 2.1 %shard_map.92 = bf16[2,176,1024]{2,1,0:T(8,128)(2,1)} custom-call(bf16[4,176,1024]{2,1,0:T(8,128)(2,1)} %get-tuple-element.20.refs_0_.refs_4_, bf16[4,176,1024]{2,1,0:T(8,128)(2,1)} %collective-permute-done.15.refs_1_.refs_5_), custom_call_target="tpu_custom_call" | custom-call | flops 720896 | bytes 2162688 | tf_op jit(solution)/shard_map/pallas_call | solution.py:113
  139.8 1.5 collective-permute-start.16
  141.3 2.1 %shard_map.90 = bf16[2,176,1024]{2,1,0:T(8,128)(2,1)} custom-call(bf16[4,176,1024]{2,1,0:T(8,128)(2,1)} %get-tuple-element.18.refs_0_, bf16[4,176,1024]{2,1,0:T(8,128)(2,1)} %collective-permute-done.12.refs_1_), custom_call_target="tpu_custom_call" | custom-call | flops 720896 | bytes 2162688 | tf_op jit(solution)/shard_map/pallas_call | solution.py:113
  143.5 2.8 %collective-permute-start.13 = (bf16[2,176,1024]{2,1,0:T(8,128)(2,1)}, bf16[2,176,1024]{2,1,0:T(8,128)(2,1)}, u32[]{:S(2)}, u32[]{:S(2)}) collective-permute-start(bf16[2,176,1024]{2,1,0:T(8,128)(2,1)} %shard_map.90), channel_id=1, source_target_pairs={{0,24},{1,9},{2,26},{3,11},{4,28},{5,13},{6,30},{7,15},{8,16},{9,1... | collective-permute-start | bytes 2162696 | tf_op jit(solution)/shard_map/ppermute | solution.py:160
  146.2 8.7 %shard_map.98 = f32[64,4096]{1,0:T(8,128)} custom-call(s32[192]{0:T(256)} %bitcast.12, bf16[352,1024]{1,0:T(8,128)(2,1)} %copy-done.1, bf16[352,1024]{1,0:T(8,128)(2,1)} %copy-done.4, bf16[352,1024]{1,0:T(8,128)(2,1)} %collective-permute-done.1.refs_0_.refs_2_, bf16[352,1024]{1,0:T(8,128)(2,1)} %collective-permute-done.3.refs_1_.refs_3_, ...), custom_call_target="tpu_custom_call" | custom-call | flops 536870912 | bytes 8388608 | tf_op jit(solution)/shard_map/pallas_call | solution.py:221
  155.0 1.4 shard_map.94
  156.4 3.1 %collective-permute-start.19 = (bf16[2,160,1024]{2,1,0:T(8,128)(2,1)S(1)}, bf16[2,160,1024]{2,1,0:T(8,128)(2,1)S(1)}, u32[]{:S(2)}, u32[]{:S(2)}) collective-permute-start(bf16[2,160,1024]{2,1,0:T(8,128)(2,1)S(1)} %shard_map.94), channel_id=1, source_target_pairs={{0,96},{1,33},{2,98},{3,35},{4,100},{5,37},{6,102},{7,39},{8,104},... | collective-permute-start | bytes 1966088 | tf_op jit(solution)/shard_map/ppermute | solution.py:160
  159.5 1.3 shard_map.93
  161.4 1.3 shard_map.91
  163.0 5.2 %collective-permute-done.19.refs_2_.refs_10_ = bf16[2,160,1024]{2,1,0:T(8,128)(2,1)S(1)} collective-permute-done((bf16[2,160,1024]{2,1,0:T(8,128)(2,1)S(1)}, bf16[2,160,1024]{2,1,0:T(8,128)(2,1)S(1)}, u32[]{:S(2)}, u32[]{:S(2)}) %collective-permute-start.19) | collective-permute-done | bytes 655392 | tf_op jit(solution)/shard_map/ppermute | solution.py:160
  168.3 1.2 shard_map.95
  169.5 0.9 collective-permute-start.20
  170.4 7.4 %collective-permute-done.20.refs_11_ = bf16[1,160,1024]{2,1,0:T(8,128)(2,1)S(1)} collective-permute-done((bf16[1,160,1024]{2,1,0:T(8,128)(2,1)S(1)}, bf16[1,160,1024]{2,1,0:T(8,128)(2,1)S(1)}, u32[]{:S(2)}, u32[]{:S(2)}) %collective-permute-start.20) | collective-permute-done | bytes 327712 | tf_op jit(solution)/shard_map/ppermute | solution.py:160
  177.8 2.9 %shard_map.96 = bf16[512,1024]{1,0:T(8,128)(2,1)} custom-call(bf16[4,176,1024]{2,1,0:T(8,128)(2,1)} %get-tuple-element.18.refs_0_, bf16[4,176,1024]{2,1,0:T(8,128)(2,1)} %collective-permute-done.12.refs_1_, bf16[2,176,1024]{2,1,0:T(8,128)(2,1)} %collective-permute-done.13.refs_2_, bf16[1,176,1024]{2,1,0:T(8,128)(2,1)S(1)} %collective-permute-done.14.refs_3_, ...), custom_call_target="tpu_custom_call" | custom-call | flops 2097152 | bytes 5242880 | tf_op jit(solution)/shard_map/pallas_call | solution.py:141
  180.8 3.7 %all-to-all-start.2 = ((bf16[8,64,1024]{2,1,0:T(8,128)(2,1)}), bf16[8,64,1024]{2,1,0:T(8,128)(2,1)S(1)}, u32[]{:S(2)}, u32[]{:S(2)}) async-start(bf16[8,64,1024]{2,1,0:T(8,128)(2,1)} %bitcast.6), calls=%async_computation.2 | async-start | bytes 2097152 | tf_op jit(solution)/shard_map/all_to_all | solution.py:82
  184.5 2.3 %add_multiply_fusion.1 = f32[64,4096]{1,0:T(8,128)} fusion(f32[64,4096]{1,0:T(8,128)S(1)} %copy-done.7, f32[64,4096]{1,0:T(8,128)} %collective-permute-done.22), kind=kLoop, calls=%fused_computation.1 | loop fusion | flops 524288 | bytes 3145728 | tf_op jit(solution)/shard_map/div | solution.py:524
  186.8 3.3 %fusion = f32[512,1024]{1,0:T(8,128)S(1)} fusion(bf16[1024,1024]{1,0:T(8,128)(2,1)} %collective-permute-done.21, s32[]{:T(128)S(6)} %select_n.9), kind=kOutput, calls=%fused_computation.2 | convolution fusion | flops 1073741824 | bytes 5242884 | tf_op jit(solution)/shard_map/dot_general | solution.py:521
  190.2 2.6 %add_multiply_fusion = f32[512,1024]{1,0:T(8,128)} fusion(f32[512,1024]{1,0:T(8,128)S(1)} %fusion, bf16[1024,1024]{1,0:T(8,128)(2,1)S(1)} %copy-done.9, s32[]{:T(128)S(6)} %select_n.9), kind=kOutput, calls=%fused_computation | convolution fusion | flops 1074790400 | bytes 7340036 | tf_op jit(solution)/shard_map/dot_general | solution.py:521
  192.8 2.9 %all-to-all-done.2.pieces = bf16[8,64,1024]{2,1,0:T(8,128)(2,1)S(1)} async-done(((bf16[8,64,1024]{2,1,0:T(8,128)(2,1)}), bf16[8,64,1024]{2,1,0:T(8,128)(2,1)S(1)}, u32[]{:S(2)}, u32[]{:S(2)}) %all-to-all-start.2) | async-done | bytes 1048608 | tf_op jit(solution)/shard_map/all_to_all | solution.py:82
  (49 shorter events, 3.0 us)
Async XLA Ops:
  17.9 9.4 %collective-permute-start.4 = (bf16[176,1024]{1,0:T(8,128)(2,1)S(1)}, bf16[176,1024]{1,0:T(8,128)(2,1)S(1)}, u32[]{:S(2)}, u32[]{:S(2)}) collective-permute-start(bf16[176,1024]{1,0:T(8,128)(2,1)S(1)} %get-tuple-element.24), channel_id=1, source_target_pairs={{0,24},{1,9},{2,26},{3,11},{4,28},{5,13},{6,30},{7,15},{8,16},{9,1... | collective-permute-start | bytes 1081352 | tf_op jit(solution)/shard_map/ppermute | solution.py:91
  20.3 8.6 %collective-permute-start = (bf16[176,1024]{1,0:T(8,128)(2,1)S(1)}, bf16[176,1024]{1,0:T(8,128)(2,1)S(1)}, u32[]{:S(2)}, u32[]{:S(2)}) collective-permute-start(bf16[176,1024]{1,0:T(8,128)(2,1)S(1)} %get-tuple-element.25), channel_id=1, source_target_pairs={{0,96},{1,33},{2,98},{3,35},{4,100},{5,37},{6,102},{7,39},{8,104},... | collective-permute-start | bytes 1081352 | tf_op jit(solution)/shard_map/ppermute | solution.py:91
  22.7 8.7 %collective-permute-start.8 = (bf16[160,1024]{1,0:T(8,128)(2,1)S(1)}, bf16[160,1024]{1,0:T(8,128)(2,1)S(1)}, u32[]{:S(2)}, u32[]{:S(2)}) collective-permute-start(bf16[160,1024]{1,0:T(8,128)(2,1)S(1)} %slice.14), channel_id=1, source_target_pairs={{0,6},{1,3},{2,4},{3,1},{4,2},{5,7},{6,0},{7,5},{8,14},{9,11},{10,... | collective-permute-start | bytes 983048 | tf_op jit(solution)/shard_map/ppermute | solution.py:91
  27.4 39.2 %copy-start = (bf16[352,1024]{1,0:T(8,128)(2,1)}, bf16[352,1024]{1,0:T(8,128)(2,1)S(1)}, u32[]{:S(2)}) copy-start(bf16[352,1024]{1,0:T(8,128)(2,1)S(1)} %pad_maximum_fusion.1.refs_2_.refs_4_) | copy-start | bytes 2162692
  27.4 23.7 %collective-permute-start.6 = (bf16[352,1024]{1,0:T(8,128)(2,1)S(1)}, bf16[352,1024]{1,0:T(8,128)(2,1)S(1)}, u32[]{:S(2)}, u32[]{:S(2)}) collective-permute-start(bf16[352,1024]{1,0:T(8,128)(2,1)S(1)} %pad_maximum_fusion.1.refs_2_.refs_4_), channel_id=1, source_target_pairs={{0,6},{1,3},{2,4},{3,1},{4,2},{5,7},{6,0},{7,5},{8,14},{9,11},{10,... | collective-permute-start | bytes 2162696 | tf_op jit(solution)/shard_map/ppermute | solution.py:91
  29.0 37.5 %copy-start.1 = (bf16[352,1024]{1,0:T(8,128)(2,1)}, bf16[352,1024]{1,0:T(8,128)(2,1)S(1)}, u32[]{:S(2)}) copy-start(bf16[352,1024]{1,0:T(8,128)(2,1)S(1)} %pad_maximum_fusion.refs_0_) | copy-start | bytes 2162692
  29.0 24.0 %collective-permute-start.2 = (bf16[352,1024]{1,0:T(8,128)(2,1)S(1)}, bf16[352,1024]{1,0:T(8,128)(2,1)S(1)}, u32[]{:S(2)}, u32[]{:S(2)}) collective-permute-start(bf16[352,1024]{1,0:T(8,128)(2,1)S(1)} %pad_maximum_fusion.refs_0_), channel_id=1, source_target_pairs={{0,24},{1,9},{2,26},{3,11},{4,28},{5,13},{6,30},{7,15},{8,16},{9,1... | collective-permute-start | bytes 2162696 | tf_op jit(solution)/shard_map/ppermute | solution.py:91
  31.5 35.1 %copy-start.2 = (bf16[320,1024]{1,0:T(8,128)(2,1)}, bf16[320,1024]{1,0:T(8,128)(2,1)S(1)}, u32[]{:S(2)}) copy-start(bf16[320,1024]{1,0:T(8,128)(2,1)S(1)} %pad_maximum_fusion.2.refs_4_.refs_8_) | copy-start | bytes 1966084
  31.5 12.0 %collective-permute-start.10 = (bf16[320,1024]{1,0:T(8,128)(2,1)S(1)}, bf16[320,1024]{1,0:T(8,128)(2,1)}, u32[]{:S(2)}, u32[]{:S(2)}) collective-permute-start(bf16[320,1024]{1,0:T(8,128)(2,1)S(1)} %pad_maximum_fusion.2.refs_4_.refs_8_), channel_id=1, source_target_pairs={{0,96},{1,33},{2,98},{3,35},{4,100},{5,37},{6,102},{7,39},{8,104},... | collective-permute-start | bytes 1966088 | tf_op jit(solution)/shard_map/ppermute | solution.py:91
  33.6 15.2 %collective-permute-start.9 = (bf16[320,1024]{1,0:T(8,128)(2,1)S(1)}, bf16[320,1024]{1,0:T(8,128)(2,1)}, u32[]{:S(2)}, u32[]{:S(2)}) collective-permute-start(bf16[320,1024]{1,0:T(8,128)(2,1)S(1)} %pad_maximum_fusion.2.refs_4_.refs_8_), channel_id=1, source_target_pairs={{0,24},{1,9},{2,26},{3,11},{4,28},{5,13},{6,30},{7,15},{8,16},{9,1... | collective-permute-start | bytes 1966088 | tf_op jit(solution)/shard_map/ppermute | solution.py:91
  35.6 58.2 %copy-start.5 = (s32[1,192]{1,0:T(1,128)}, s32[1,192]{1,0:T(1,128)S(1)}, u32[]{:S(2)}) copy-start(s32[1,192]{1,0:T(1,128)S(1)} %constant_dynamic-slice_fusion) | copy-start | bytes 2308
  35.6 41.2 %collective-permute-start.5 = (bf16[352,1024]{1,0:T(8,128)(2,1)S(1)}, bf16[352,1024]{1,0:T(8,128)(2,1)}, u32[]{:S(2)}, u32[]{:S(2)}) collective-permute-start(bf16[352,1024]{1,0:T(8,128)(2,1)S(1)} %pad_maximum_fusion.1.refs_2_.refs_4_), channel_id=1, source_target_pairs={{0,96},{1,33},{2,98},{3,35},{4,100},{5,37},{6,102},{7,39},{8,104},... | collective-permute-start | bytes 2162696 | tf_op jit(solution)/shard_map/ppermute | solution.py:91
  43.5 33.3 %collective-permute-start.1 = (bf16[352,1024]{1,0:T(8,128)(2,1)S(1)}, bf16[352,1024]{1,0:T(8,128)(2,1)}, u32[]{:S(2)}, u32[]{:S(2)}) collective-permute-start(bf16[352,1024]{1,0:T(8,128)(2,1)S(1)} %pad_maximum_fusion.refs_0_), channel_id=1, source_target_pairs={{0,6},{1,3},{2,4},{3,1},{4,2},{5,7},{6,0},{7,5},{8,14},{9,11},{10,... | collective-permute-start | bytes 2162696 | tf_op jit(solution)/shard_map/ppermute | solution.py:91
  48.8 28.0 %collective-permute-start.11 = (bf16[320,1024]{1,0:T(8,128)(2,1)}, bf16[320,1024]{1,0:T(8,128)(2,1)}, u32[]{:S(2)}, u32[]{:S(2)}) collective-permute-start(bf16[320,1024]{1,0:T(8,128)(2,1)} %collective-permute-done.10.refs_5_.refs_9_), channel_id=1, source_target_pairs={{0,24},{1,9},{2,26},{3,11},{4,28},{5,13},{6,30},{7,15},{8,16},{9,1... | collective-permute-start | bytes 1966088 | tf_op jit(solution)/shard_map/ppermute | solution.py:91
  51.1 15.5 %copy-start.3 = (bf16[352,1024]{1,0:T(8,128)(2,1)}, bf16[352,1024]{1,0:T(8,128)(2,1)S(1)}, u32[]{:S(2)}) copy-start(bf16[352,1024]{1,0:T(8,128)(2,1)S(1)} %collective-permute-done.6.refs_3_.refs_5_) | copy-start | bytes 2162692
  51.1 25.7 %collective-permute-start.7 = (bf16[352,1024]{1,0:T(8,128)(2,1)S(1)}, bf16[352,1024]{1,0:T(8,128)(2,1)}, u32[]{:S(2)}, u32[]{:S(2)}) collective-permute-start(bf16[352,1024]{1,0:T(8,128)(2,1)S(1)} %collective-permute-done.6.refs_3_.refs_5_), channel_id=1, source_target_pairs={{0,96},{1,33},{2,98},{3,35},{4,100},{5,37},{6,102},{7,39},{8,104},... | collective-permute-start | bytes 2162696 | tf_op jit(solution)/shard_map/ppermute | solution.py:91
  53.1 13.5 %copy-start.4 = (bf16[352,1024]{1,0:T(8,128)(2,1)}, bf16[352,1024]{1,0:T(8,128)(2,1)S(1)}, u32[]{:S(2)}) copy-start(bf16[352,1024]{1,0:T(8,128)(2,1)S(1)} %collective-permute-done.2.refs_1_) | copy-start | bytes 2162692
  53.1 23.7 %collective-permute-start.3 = (bf16[352,1024]{1,0:T(8,128)(2,1)S(1)}, bf16[352,1024]{1,0:T(8,128)(2,1)}, u32[]{:S(2)}, u32[]{:S(2)}) collective-permute-start(bf16[352,1024]{1,0:T(8,128)(2,1)S(1)} %collective-permute-done.2.refs_1_), channel_id=1, source_target_pairs={{0,6},{1,3},{2,4},{3,1},{4,2},{5,7},{6,0},{7,5},{8,14},{9,11},{10,... | collective-permute-start | bytes 2162696 | tf_op jit(solution)/shard_map/ppermute | solution.py:91
  54.5 12.1 %copy-start.8 = (s32[1024]{0:T(1024)S(1)}, s32[1024]{0:T(1024)}, u32[]{:S(2)}) copy-start(s32[1024]{0:T(1024)} %param.7) | copy-start | bytes 12292
  66.6 10.2 %copy-start.6 = (s32[1024]{0:T(1024)}, s32[1024]{0:T(1024)S(1)}, u32[]{:S(2)}) copy-start(s32[1024]{0:T(1024)S(1)} %broadcast_subtract_fusion) | copy-start | bytes 12292
  88.3 17.4 %all-to-all-start.1 = ((f32[64,16,128]{2,1,0:T(8,128)}), f32[64,16,128]{2,1,0:T(8,128)}, u32[]{:S(2)}, u32[]{:S(2)}) async-start(f32[64,16,128]{2,1,0:T(8,128)} %get-tuple-element.14), calls=%async_computation.1 | async-start | bytes 1048576 | tf_op jit(solution)/shard_map/all_to_all | solution.py:510
  117.2 20.5 %collective-permute-start.15 = (bf16[4,176,1024]{2,1,0:T(8,128)(2,1)}, bf16[4,176,1024]{2,1,0:T(8,128)(2,1)}, u32[]{:S(2)}, u32[]{:S(2)}) collective-permute-start(bf16[4,176,1024]{2,1,0:T(8,128)(2,1)} %get-tuple-element.21), channel_id=1, source_target_pairs={{0,96},{1,33},{2,98},{3,35},{4,100},{5,37},{6,102},{7,39},{8,104},... | collective-permute-start | bytes 4325384 | tf_op jit(solution)/shard_map/ppermute | solution.py:160
  119.0 22.4 %collective-permute-start.12 = (bf16[4,176,1024]{2,1,0:T(8,128)(2,1)}, bf16[4,176,1024]{2,1,0:T(8,128)(2,1)}, u32[]{:S(2)}, u32[]{:S(2)}) collective-permute-start(bf16[4,176,1024]{2,1,0:T(8,128)(2,1)} %get-tuple-element.19), channel_id=1, source_target_pairs={{0,6},{1,3},{2,4},{3,1},{4,2},{5,7},{6,0},{7,5},{8,14},{9,11},{10,... | collective-permute-start | bytes 4325384 | tf_op jit(solution)/shard_map/ppermute | solution.py:160
  121.7 33.3 %collective-permute-start.18 = (bf16[4,160,1024]{2,1,0:T(8,128)(2,1)}, bf16[4,160,1024]{2,1,0:T(8,128)(2,1)}, u32[]{:S(2)}, u32[]{:S(2)}) collective-permute-start(bf16[4,160,1024]{2,1,0:T(8,128)(2,1)} %get-tuple-element.23), channel_id=1, source_target_pairs={{0,24},{1,9},{2,26},{3,11},{4,28},{5,13},{6,30},{7,15},{8,16},{9,1... | collective-permute-start | bytes 3932168 | tf_op jit(solution)/shard_map/ppermute | solution.py:160
  124.4 62.4 %collective-permute-start.21 = (bf16[1024,1024]{1,0:T(8,128)(2,1)}, bf16[1024,1024]{1,0:T(8,128)(2,1)}, u32[]{:S(2)}, u32[]{:S(2)}) collective-permute-start(bf16[1024,1024]{1,0:T(8,128)(2,1)} %get-tuple-element.17.grad), channel_id=1, source_target_pairs={{0,1},{1,0},{2,3},{3,2},{4,5},{5,4},{6,7},{7,6},{8,9},{9,8},{10,11... | collective-permute-start | bytes 6291464 | tf_op jit(solution)/shard_map/ppermute | solution.py:523
  139.8 19.7 %collective-permute-start.16 = (bf16[2,176,1024]{2,1,0:T(8,128)(2,1)}, bf16[2,176,1024]{2,1,0:T(8,128)(2,1)}, u32[]{:S(2)}, u32[]{:S(2)}) collective-permute-start(bf16[2,176,1024]{2,1,0:T(8,128)(2,1)} %shard_map.92), channel_id=1, source_target_pairs={{0,6},{1,3},{2,4},{3,1},{4,2},{5,7},{6,0},{7,5},{8,14},{9,11},{10,... | collective-permute-start | bytes 2162696 | tf_op jit(solution)/shard_map/ppermute | solution.py:160
  143.5 17.9 %collective-permute-start.13 = (bf16[2,176,1024]{2,1,0:T(8,128)(2,1)}, bf16[2,176,1024]{2,1,0:T(8,128)(2,1)}, u32[]{:S(2)}, u32[]{:S(2)}) collective-permute-start(bf16[2,176,1024]{2,1,0:T(8,128)(2,1)} %shard_map.90), channel_id=1, source_target_pairs={{0,24},{1,9},{2,26},{3,11},{4,28},{5,13},{6,30},{7,15},{8,16},{9,1... | collective-permute-start | bytes 2162696 | tf_op jit(solution)/shard_map/ppermute | solution.py:160
  154.9 29.6 %collective-permute-start.22 = (f32[64,4096]{1,0:T(8,128)}, f32[64,4096]{1,0:T(8,128)}, u32[]{:S(2)}, u32[]{:S(2)}) collective-permute-start(f32[64,4096]{1,0:T(8,128)} %shard_map.98), channel_id=1, source_target_pairs={{0,1},{1,0},{2,3},{3,2},{4,5},{5,4},{6,7},{7,6},{8,9},{9,8},{10,11... | collective-permute-start | bytes 3145736 | tf_op jit(solution)/shard_map/ppermute | solution.py:524
  156.4 11.9 %collective-permute-start.19 = (bf16[2,160,1024]{2,1,0:T(8,128)(2,1)S(1)}, bf16[2,160,1024]{2,1,0:T(8,128)(2,1)S(1)}, u32[]{:S(2)}, u32[]{:S(2)}) collective-permute-start(bf16[2,160,1024]{2,1,0:T(8,128)(2,1)S(1)} %shard_map.94), channel_id=1, source_target_pairs={{0,96},{1,33},{2,98},{3,35},{4,100},{5,37},{6,102},{7,39},{8,104},... | collective-permute-start | bytes 1966088 | tf_op jit(solution)/shard_map/ppermute | solution.py:160
  160.8 17.0 %collective-permute-start.17 = (bf16[1,176,1024]{2,1,0:T(8,128)(2,1)S(1)}, bf16[1,176,1024]{2,1,0:T(8,128)(2,1)S(1)}, u32[]{:S(2)}, u32[]{:S(2)}) collective-permute-start(bf16[1,176,1024]{2,1,0:T(8,128)(2,1)S(1)} %shard_map.93), channel_id=1, source_target_pairs={{0,24},{1,9},{2,26},{3,11},{4,28},{5,13},{6,30},{7,15},{8,16},{9,1... | collective-permute-start | bytes 1081352 | tf_op jit(solution)/shard_map/ppermute | solution.py:160
  162.7 15.1 %collective-permute-start.14 = (bf16[1,176,1024]{2,1,0:T(8,128)(2,1)S(1)}, bf16[1,176,1024]{2,1,0:T(8,128)(2,1)S(1)}, u32[]{:S(2)}, u32[]{:S(2)}) collective-permute-start(bf16[1,176,1024]{2,1,0:T(8,128)(2,1)S(1)} %shard_map.91), channel_id=1, source_target_pairs={{0,96},{1,33},{2,98},{3,35},{4,100},{5,37},{6,102},{7,39},{8,104},... | collective-permute-start | bytes 1081352 | tf_op jit(solution)/shard_map/ppermute | solution.py:160
  169.5 8.4 %collective-permute-start.20 = (bf16[1,160,1024]{2,1,0:T(8,128)(2,1)S(1)}, bf16[1,160,1024]{2,1,0:T(8,128)(2,1)S(1)}, u32[]{:S(2)}, u32[]{:S(2)}) collective-permute-start(bf16[1,160,1024]{2,1,0:T(8,128)(2,1)S(1)} %shard_map.95), channel_id=1, source_target_pairs={{0,6},{1,3},{2,4},{3,1},{4,2},{5,7},{6,0},{7,5},{8,14},{9,11},{10,... | collective-permute-start | bytes 983048 | tf_op jit(solution)/shard_map/ppermute | solution.py:160
  180.8 3.7 %copy-start.7 = (f32[64,4096]{1,0:T(8,128)S(1)}, f32[64,4096]{1,0:T(8,128)}, u32[]{:S(2)}) copy-start(f32[64,4096]{1,0:T(8,128)} %shard_map.98) | copy-start | bytes 3145732
  180.8 14.9 %all-to-all-start.2 = ((bf16[8,64,1024]{2,1,0:T(8,128)(2,1)}), bf16[8,64,1024]{2,1,0:T(8,128)(2,1)S(1)}, u32[]{:S(2)}, u32[]{:S(2)}) async-start(bf16[8,64,1024]{2,1,0:T(8,128)(2,1)} %bitcast.6), calls=%async_computation.2 | async-start | bytes 2097152 | tf_op jit(solution)/shard_map/all_to_all | solution.py:82
  186.8 3.4 %copy-start.9 = (bf16[1024,1024]{1,0:T(8,128)(2,1)S(1)}, bf16[1024,1024]{1,0:T(8,128)(2,1)}, u32[]{:S(2)}) copy-start(bf16[1024,1024]{1,0:T(8,128)(2,1)} %get-tuple-element.17.grad) | copy-start | bytes 6291460

commit v5 on v4

--- a/solution.py
+++ b/solution.py
@@ -247,12 +247,12 @@
                     if s // 2 != tile:
                         continue
                     chip, side = chips[64 * g + 8 * l + s], s % 2
-                    block = w[:, pl.ds(pl.multiple_of(chip // 2 * 128, 128), 128)].astype(F32)
+                    block = w[:, pl.ds(pl.multiple_of(chip // 2 * 128, 128), 128)]
                     block = pltpu.roll(block, 64 * (chip % 2 != side).astype(jnp.int32), 1)
                     done = block if done is None else jnp.where(
                         lane >= 64 * side + first, block, done
                     )
-            wide[:, (4 * l + tile) * 128 : (4 * l + tile + 1) * 128] = done.astype(BF16)
+            wide[:, (4 * l + tile) * 128 : (4 * l + tile + 1) * 128] = done
 
 
 def columns_turned(chips, w):
@@ -316,8 +316,8 @@
 
 def half_copies(got, h):
     size = sum(SIZES)
-    for g in range(3):
-        for l in range(4):
+    for l in range(4):
+        for g in range(3):
             src = got[2 * g + l // 2].at[pl.ds((l % 2) * SIZES[g], SIZES[g])]
             yield src, h.at[pl.ds(l * size + STARTS[g], SIZES[g])]
 
@@ -341,15 +341,22 @@
 
     @pl.when(step == 0)
     def _():
-        for src, dst in half_copies(got, h):
-            pltpu.make_async_copy(src, dst, sem).start()
+        for k, (src, dst) in enumerate(half_copies(got, h)):
+            pltpu.make_async_copy(src, dst, sem.at[k // 3]).start()
         top[...] = jnp.full(top.shape, -jnp.inf, F32)
         total[...] = jnp.zeros(total.shape, F32)
         hit[...] = jnp.zeros(hit.shape, F32)
-        pltpu.make_async_copy(h, h, sem).wait()
-
-    block = part[...] + jnp.dot(w[...], h[...], preferred_element_type=F32)
-    logits[...] = block
+        logits[...] = part[...]
+        for l in range(4):
+            some = pl.ds(l * sum(SIZES), sum(SIZES))
+            pltpu.make_async_copy(h.at[some], h.at[some], sem.at[l]).wait()
+            logits[...] += jnp.dot(w[:, some], h[some, :], preferred_element_type=F32)
+
+    @pl.when(step > 0)
+    def _():
+        logits[...] = part[...] + jnp.dot(w[...], h[...], preferred_element_type=F32)
+
+    block = logits[...]
     at = lax.broadcasted_iota(jnp.int32, block.shape, 0) + step * rows
     hit[...] += jnp.sum(jnp.where(at == tgt[...], block, F32(0.0)), axis=0, keepdims=True)
     now = jnp.maximum(top[...], jnp.max(block, axis=0, keepdims=True))
@@ -386,7 +393,7 @@
         ] if late else pltpu.HBM((vocab_rows, tokens), F32),
         scratch_shapes=[pltpu.VMEM((width // 2, tokens), BF16)]
         + [pltpu.VMEM((1, tokens), F32)] * (3 if late else 0)
-        + [pltpu.SemaphoreType.DMA],
+        + [pltpu.SemaphoreType.DMA((4,)) if late else pltpu.SemaphoreType.DMA],
         compiler_params=pltpu.CompilerParams(
             dimension_semantics=("arbitrary",), vmem_limit_bytes=32 << 20
         ),

time: 198 us -> 197 us (level)
  no operation moved by 1% of the time
where the time goes in v5:
time: 197 us; the launch traced here: 196 us
  Pallas kernels  85.6 us (43%)
  starting transfers between devices  47.6 us (24%)
  waiting for transfers between devices  35.5 us (18%)
  blocking collectives  16.2 us (8%)
  matrix products  5.96 us (3%)
  other arithmetic  2.44 us (1%)
    ppermute x12, starting transfers between devices, get(): return lax.ppermute(x, ALL, LARGE_PAIRS[(g + step) % 3])  21.9 us
    pallas_call x2, Pallas kernels, half_logits(): pl.pallas_call(late_kernel if late else early_kernel, grid=(vocab_rows //...  21.2 us
    ppermute x9, waiting for transfers between devices, trade(): return lax.ppermute(x, ALL, LARGE_PAIRS[(g + step) % 3])  17.7 us
    ppermute x9, starting transfers between devices, trade(): return lax.ppermute(x, ALL, LARGE_PAIRS[(g + step) % 3])  16.4 us
    all_to_all x1, blocking collectives, small_stage(): lax.all_to_all(x, ALL, 0, 0, axis_index_groups=SMALL_CUBES, tiled=True)  16.2 us
    ppermute x12, waiting for transfers between devices, get(): return lax.ppermute(x, ALL, LARGE_PAIRS[(g + step) % 3])  13.8 us
    pallas_call x1, Pallas kernels, columns_turned(): pl.pallas_call(columns_kernel, grid_spec=pltpu.PrefetchScalarGridSpec(num...  12 us
    pallas_call x1, Pallas kernels, signal_of(): pl.pallas_call(signal_kernel, grid=(count + 4,), in_specs=[whole(*stats.s...  11.5 us
  transfers between devices with their start and end apart: 25, of which 9 were waited for; matrix products, arithmetic and copies ran while one was open for 5% of the time, Pallas kernels for 32%

profile of v5, /device:TPU:0, one launch (start us, length us, event | category | flops | bytes accessed | tf_op | source)
XLA Modules:
  0.0 196.1 jit_solution(16208078822764061630)
XLA Ops:
  0.6 1.0 broadcast_in_dim.12
  1.7 16.2 %all_to_all.15 = bf16[8,64,1024]{2,1,0:T(8,128)(2,1)S(1)} all-to-all(bf16[8,64,1024]{2,1,0:T(8,128)(2,1)S(1)} %broadcast_in_dim.12), channel_id=1, replica_groups={{0,2,8,10,32,34,40,42},{4,6,12,14,36,38,44,46},{16,18,24,26,48,50,56,58..., dimensions={0} | all-to-all | bytes 2097152 | tf_op jit(solution)/shard_map/all_to_all | solution.py:82
  17.9 2.4 %collective-permute-start.4 = (bf16[176,1024]{1,0:T(8,128)(2,1)S(1)}, bf16[176,1024]{1,0:T(8,128)(2,1)S(1)}, u32[]{:S(2)}, u32[]{:S(2)}) collective-permute-start(bf16[176,1024]{1,0:T(8,128)(2,1)S(1)} %get-tuple-element.24), channel_id=1, source_target_pairs={{0,24},{1,9},{2,26},{3,11},{4,28},{5,13},{6,30},{7,15},{8,16},{9,1... | collective-permute-start | bytes 1081352 | tf_op jit(solution)/shard_map/ppermute | solution.py:91
  20.3 2.4 %collective-permute-start = (bf16[176,1024]{1,0:T(8,128)(2,1)S(1)}, bf16[176,1024]{1,0:T(8,128)(2,1)S(1)}, u32[]{:S(2)}, u32[]{:S(2)}) collective-permute-start(bf16[176,1024]{1,0:T(8,128)(2,1)S(1)} %get-tuple-element.25), channel_id=1, source_target_pairs={{0,96},{1,33},{2,98},{3,35},{4,100},{5,37},{6,102},{7,39},{8,104},... | collective-permute-start | bytes 1081352 | tf_op jit(solution)/shard_map/ppermute | solution.py:91
  22.7 1.9 collective-permute-start.8
  24.6 2.7 %collective-permute-done.4 = bf16[176,1024]{1,0:T(8,128)(2,1)S(1)} collective-permute-done((bf16[176,1024]{1,0:T(8,128)(2,1)S(1)}, bf16[176,1024]{1,0:T(8,128)(2,1)S(1)}, u32[]{:S(2)}, u32[]{:S(2)}) %collective-permute-start.4) | collective-permute-done | bytes 360480 | tf_op jit(solution)/shard_map/ppermute | solution.py:91
  27.4 1.4 collective-permute-start.6
  29.0 2.4 %collective-permute-start.2 = (bf16[352,1024]{1,0:T(8,128)(2,1)S(1)}, bf16[352,1024]{1,0:T(8,128)(2,1)S(1)}, u32[]{:S(2)}, u32[]{:S(2)}) collective-permute-start(bf16[352,1024]{1,0:T(8,128)(2,1)S(1)} %pad_maximum_fusion.refs_0_), channel_id=1, source_target_pairs={{0,24},{1,9},{2,26},{3,11},{4,28},{5,13},{6,30},{7,15},{8,16},{9,1... | collective-permute-start | bytes 2162696 | tf_op jit(solution)/shard_map/ppermute | solution.py:91
  31.5 2.1 %collective-permute-start.10 = (bf16[320,1024]{1,0:T(8,128)(2,1)S(1)}, bf16[320,1024]{1,0:T(8,128)(2,1)}, u32[]{:S(2)}, u32[]{:S(2)}) collective-permute-start(bf16[320,1024]{1,0:T(8,128)(2,1)S(1)} %pad_maximum_fusion.2.refs_4_.refs_8_), channel_id=1, source_target_pairs={{0,96},{1,33},{2,98},{3,35},{4,100},{5,37},{6,102},{7,39},{8,104},... | collective-permute-start | bytes 1966088 | tf_op jit(solution)/shard_map/ppermute | solution.py:91
  33.6 1.3 collective-permute-start.9
  35.6 0.9 collective-permute-start.5
  36.4 7.1 %collective-permute-done.10.refs_5_.refs_9_ = bf16[320,1024]{1,0:T(8,128)(2,1)} collective-permute-done((bf16[320,1024]{1,0:T(8,128)(2,1)S(1)}, bf16[320,1024]{1,0:T(8,128)(2,1)}, u32[]{:S(2)}, u32[]{:S(2)}) %collective-permute-start.10) | collective-permute-done | bytes 655392 | tf_op jit(solution)/shard_map/ppermute | solution.py:91
  43.5 1.5 collective-permute-start.1
  45.0 3.8 %collective-permute-done.9.refs_4_.refs_10_ = bf16[320,1024]{1,0:T(8,128)(2,1)} collective-permute-done((bf16[320,1024]{1,0:T(8,128)(2,1)S(1)}, bf16[320,1024]{1,0:T(8,128)(2,1)}, u32[]{:S(2)}, u32[]{:S(2)}) %collective-permute-start.9) | collective-permute-done | bytes 655392 | tf_op jit(solution)/shard_map/ppermute | solution.py:91
  48.8 2.3 %collective-permute-start.11 = (bf16[320,1024]{1,0:T(8,128)(2,1)}, bf16[320,1024]{1,0:T(8,128)(2,1)}, u32[]{:S(2)}, u32[]{:S(2)}) collective-permute-start(bf16[320,1024]{1,0:T(8,128)(2,1)} %collective-permute-done.10.refs_5_.refs_9_), channel_id=1, source_target_pairs={{0,24},{1,9},{2,26},{3,11},{4,28},{5,13},{6,30},{7,15},{8,16},{9,1... | collective-permute-start | bytes 1966088 | tf_op jit(solution)/shard_map/ppermute | solution.py:91
  51.1 2.0 %collective-permute-start.7 = (bf16[352,1024]{1,0:T(8,128)(2,1)S(1)}, bf16[352,1024]{1,0:T(8,128)(2,1)}, u32[]{:S(2)}, u32[]{:S(2)}) collective-permute-start(bf16[352,1024]{1,0:T(8,128)(2,1)S(1)} %collective-permute-done.6.refs_3_.refs_5_), channel_id=1, source_target_pairs={{0,96},{1,33},{2,98},{3,35},{4,100},{5,37},{6,102},{7,39},{8,104},... | collective-permute-start | bytes 2162696 | tf_op jit(solution)/shard_map/ppermute | solution.py:91
  53.1 1.4 collective-permute-start.3
  54.5 12.0 %shard_map.84.refs_6_ = bf16[1024,4096]{1,0:T(8,128)(2,1)} custom-call(s32[192]{0:T(256)S(1)} %bitcast.10, bf16[1024,4096]{1,0:T(8,128)(2,1)} %w.3), custom_call_target="tpu_custom_call" | custom-call | flops 4294967296 | bytes 16777216 | tf_op jit(solution)/shard_map/pallas_call | solution.py:261
  66.6 10.0 %shard_map.85.refs_7_ = f32[1024,1024]{1,0:T(8,128)} custom-call(bf16[352,1024]{1,0:T(8,128)(2,1)S(1)} %pad_maximum_fusion.refs_0_, bf16[352,1024]{1,0:T(8,128)(2,1)S(1)} %collective-permute-done.2.refs_1_, bf16[352,1024]{1,0:T(8,128)(2,1)S(1)} %pad_maximum_fusion.1.refs_2_.refs_4_, bf16[352,1024]{1,0:T(8,128)(2,1)S(1)} %collective-permute-done.6.refs_3_.refs_5_, ...), custom_call_target="tpu_custom_call" | custom-call | flops 4294967296 | bytes 12582912 | tf_op jit(solution)/shard_map/pallas_call | solution.py:384
  76.7 11.2 %shard_map.86 = (f32[1024,1024]{1,0:T(8,128)}, f32[64,16,128]{2,1,0:T(8,128)}) custom-call(bf16[352,1024]{1,0:T(8,128)(2,1)} %collective-permute-done.1.refs_0_.refs_2_, bf16[352,1024]{1,0:T(8,128)(2,1)} %collective-permute-done.3.refs_1_.refs_3_, bf16[352,1024]{1,0:T(8,128)(2,1)} %collective-permute-done.5.refs_2_.refs_6_, ...), custom_call_target="tpu_custom_call" | custom-call | flops 4294967296 | bytes 12582912 | tf_op jit(solution)/shard_map/pallas_call | solution.py:384
  87.8 5.5 %all-to-all-start.1 = ((f32[64,16,128]{2,1,0:T(8,128)}), f32[64,16,128]{2,1,0:T(8,128)}, u32[]{:S(2)}, u32[]{:S(2)}) async-start(f32[64,16,128]{2,1,0:T(8,128)} %get-tuple-element.14), calls=%async_computation.1 | async-start | bytes 1048576 | tf_op jit(solution)/shard_map/all_to_all | solution.py:517
  93.3 10.7 %shard_map.87.tall = bf16[4096,1024]{1,0:T(8,128)(2,1)} custom-call(s32[192]{0:T(256)S(1)} %bitcast.11, bf16[1024,4096]{1,0:T(8,128)(2,1)} %w.3), custom_call_target="tpu_custom_call" | custom-call | flops 4294967296 | bytes 16777216 | tf_op jit(solution)/shard_map/pallas_call | solution.py:298
  104.1 1.2 all-to-all-done.1.stats
  105.2 11.5 %shard_map.88 = (bf16[1024,1024]{1,0:T(8,128)(2,1)}, f32[1,1024]{1,0:T(1,128)}, bf16[4,176,1024]{2,1,0:T(8,128)(2,1)}, bf16[4,176,1024]{2,1,0:T(8,128)(2,1)}, bf16[4,160,1024]{2,1,0:T(8,128)(2,1)}) custom-call(f32[64,16,128]{2,1,0:T(8,128)} %all-to-all-done.1.stats, f32[1024,1024]{1,0:T(8,128)} %get-tuple-element.15.logits, f32[1,1024]{1,0:T(1,128)} %bitcast.20, ...), custom_call_target="tpu_custom_call" | custom-call | flops 4294967296 | bytes 14680064 | tf_op jit(solution)/shard_map/pallas_call | solution.py:448
  116.7 1.8 collective-permute-start.15
  118.5 2.7 %collective-permute-start.12 = (bf16[4,176,1024]{2,1,0:T(8,128)(2,1)}, bf16[4,176,1024]{2,1,0:T(8,128)(2,1)}, u32[]{:S(2)}, u32[]{:S(2)}) collective-permute-start(bf16[4,176,1024]{2,1,0:T(8,128)(2,1)} %get-tuple-element.19), channel_id=1, source_target_pairs={{0,6},{1,3},{2,4},{3,1},{4,2},{5,7},{6,0},{7,5},{8,14},{9,11},{10,... | collective-permute-start | bytes 4325384 | tf_op jit(solution)/shard_map/ppermute | solution.py:160
  121.2 2.8 %collective-permute-start.18 = (bf16[4,160,1024]{2,1,0:T(8,128)(2,1)}, bf16[4,160,1024]{2,1,0:T(8,128)(2,1)}, u32[]{:S(2)}, u32[]{:S(2)}) collective-permute-start(bf16[4,160,1024]{2,1,0:T(8,128)(2,1)} %get-tuple-element.23), channel_id=1, source_target_pairs={{0,24},{1,9},{2,26},{3,11},{4,28},{5,13},{6,30},{7,15},{8,16},{9,1... | collective-permute-start | bytes 3932168 | tf_op jit(solution)/shard_map/ppermute | solution.py:160
  123.9 8.2 %shard_map.89 = (bf16[4,176,1024]{2,1,0:T(8,128)(2,1)}, bf16[4,176,1024]{2,1,0:T(8,128)(2,1)}, bf16[4,160,1024]{2,1,0:T(8,128)(2,1)}) custom-call(bf16[4096,1024]{1,0:T(8,128)(2,1)} %shard_map.87.tall, bf16[1024,1024]{1,0:T(8,128)(2,1)} %get-tuple-element.17.grad), custom_call_target="tpu_custom_call" | custom-call | flops 4294967296 | bytes 8388608 | tf_op jit(solution)/shard_map/pallas_call | solution.py:486
  132.1 5.1 %collective-permute-done.15.refs_1_.refs_5_ = bf16[4,176,1024]{2,1,0:T(8,128)(2,1)} collective-permute-done((bf16[4,176,1024]{2,1,0:T(8,128)(2,1)}, bf16[4,176,1024]{2,1,0:T(8,128)(2,1)}, u32[]{:S(2)}, u32[]{:S(2)}) %collective-permute-start.15) | collective-permute-done | bytes 1441824 | tf_op jit(solution)/shard_map/ppermute | solution.py:160
  137.2 2.1 %shard_map.92 = bf16[2,176,1024]{2,1,0:T(8,128)(2,1)} custom-call(bf16[4,176,1024]{2,1,0:T(8,128)(2,1)} %get-tuple-element.20.refs_0_.refs_4_, bf16[4,176,1024]{2,1,0:T(8,128)(2,1)} %collective-permute-done.15.refs_1_.refs_5_), custom_call_target="tpu_custom_call" | custom-call | flops 720896 | bytes 2162688 | tf_op jit(solution)/shard_map/pallas_call | solution.py:113
  139.4 1.5 collective-permute-start.16
  140.9 2.1 %shard_map.90 = bf16[2,176,1024]{2,1,0:T(8,128)(2,1)} custom-call(bf16[4,176,1024]{2,1,0:T(8,128)(2,1)} %get-tuple-element.18.refs_0_, bf16[4,176,1024]{2,1,0:T(8,128)(2,1)} %collective-permute-done.12.refs_1_), custom_call_target="tpu_custom_call" | custom-call | flops 720896 | bytes 2162688 | tf_op jit(solution)/shard_map/pallas_call | solution.py:113
  143.0 2.7 %collective-permute-start.13 = (bf16[2,176,1024]{2,1,0:T(8,128)(2,1)}, bf16[2,176,1024]{2,1,0:T(8,128)(2,1)}, u32[]{:S(2)}, u32[]{:S(2)}) collective-permute-start(bf16[2,176,1024]{2,1,0:T(8,128)(2,1)} %shard_map.90), channel_id=1, source_target_pairs={{0,24},{1,9},{2,26},{3,11},{4,28},{5,13},{6,30},{7,15},{8,16},{9,1... | collective-permute-start | bytes 2162696 | tf_op jit(solution)/shard_map/ppermute | solution.py:160
  145.8 8.7 %shard_map.98 = f32[64,4096]{1,0:T(8,128)} custom-call(s32[192]{0:T(256)} %bitcast.12, bf16[352,1024]{1,0:T(8,128)(2,1)} %copy-done.1, bf16[352,1024]{1,0:T(8,128)(2,1)} %copy-done.4, bf16[352,1024]{1,0:T(8,128)(2,1)} %collective-permute-done.1.refs_0_.refs_2_, bf16[352,1024]{1,0:T(8,128)(2,1)} %collective-permute-done.3.refs_1_.refs_3_, ...), custom_call_target="tpu_custom_call" | custom-call | flops 536870912 | bytes 8388608 | tf_op jit(solution)/shard_map/pallas_call | solution.py:221
  154.5 1.4 shard_map.94
  155.9 3.1 %collective-permute-start.19 = (bf16[2,160,1024]{2,1,0:T(8,128)(2,1)S(1)}, bf16[2,160,1024]{2,1,0:T(8,128)(2,1)S(1)}, u32[]{:S(2)}, u32[]{:S(2)}) collective-permute-start(bf16[2,160,1024]{2,1,0:T(8,128)(2,1)S(1)} %shard_map.94), channel_id=1, source_target_pairs={{0,96},{1,33},{2,98},{3,35},{4,100},{5,37},{6,102},{7,39},{8,104},... | collective-permute-start | bytes 1966088 | tf_op jit(solution)/shard_map/ppermute | solution.py:160
  159.0 1.3 shard_map.93
  160.9 1.3 shard_map.91
  162.6 5.2 %collective-permute-done.19.refs_2_.refs_10_ = bf16[2,160,1024]{2,1,0:T(8,128)(2,1)S(1)} collective-permute-done((bf16[2,160,1024]{2,1,0:T(8,128)(2,1)S(1)}, bf16[2,160,1024]{2,1,0:T(8,128)(2,1)S(1)}, u32[]{:S(2)}, u32[]{:S(2)}) %collective-permute-start.19) | collective-permute-done | bytes 655392 | tf_op jit(solution)/shard_map/ppermute | solution.py:160
  167.8 1.2 shard_map.95
  169.0 0.9 collective-permute-start.20
  169.9 7.4 %collective-permute-done.20.refs_11_ = bf16[1,160,1024]{2,1,0:T(8,128)(2,1)S(1)} collective-permute-done((bf16[1,160,1024]{2,1,0:T(8,128)(2,1)S(1)}, bf16[1,160,1024]{2,1,0:T(8,128)(2,1)S(1)}, u32[]{:S(2)}, u32[]{:S(2)}) %collective-permute-start.20) | collective-permute-done | bytes 327712 | tf_op jit(solution)/shard_map/ppermute | solution.py:160
  177.4 2.9 %shard_map.96 = bf16[512,1024]{1,0:T(8,128)(2,1)} custom-call(bf16[4,176,1024]{2,1,0:T(8,128)(2,1)} %get-tuple-element.18.refs_0_, bf16[4,176,1024]{2,1,0:T(8,128)(2,1)} %collective-permute-done.12.refs_1_, bf16[2,176,1024]{2,1,0:T(8,128)(2,1)} %collective-permute-done.13.refs_2_, bf16[1,176,1024]{2,1,0:T(8,128)(2,1)S(1)} %collective-permute-done.14.refs_3_, ...), custom_call_target="tpu_custom_call" | custom-call | flops 2097152 | bytes 5242880 | tf_op jit(solution)/shard_map/pallas_call | solution.py:141
  180.3 3.7 %all-to-all-start.2 = ((bf16[8,64,1024]{2,1,0:T(8,128)(2,1)}), bf16[8,64,1024]{2,1,0:T(8,128)(2,1)S(1)}, u32[]{:S(2)}, u32[]{:S(2)}) async-start(bf16[8,64,1024]{2,1,0:T(8,128)(2,1)} %bitcast.6), calls=%async_computation.2 | async-start | bytes 2097152 | tf_op jit(solution)/shard_map/all_to_all | solution.py:82
  184.0 2.3 %add_multiply_fusion.1 = f32[64,4096]{1,0:T(8,128)} fusion(f32[64,4096]{1,0:T(8,128)S(1)} %copy-done.7, f32[64,4096]{1,0:T(8,128)} %collective-permute-done.22), kind=kLoop, calls=%fused_computation.1 | loop fusion | flops 524288 | bytes 3145728 | tf_op jit(solution)/shard_map/div | solution.py:531
  186.3 3.3 %fusion = f32[512,1024]{1,0:T(8,128)S(1)} fusion(bf16[1024,1024]{1,0:T(8,128)(2,1)} %collective-permute-done.21, s32[]{:T(128)S(6)} %select_n.9), kind=kOutput, calls=%fused_computation.2 | convolution fusion | flops 1073741824 | bytes 5242884 | tf_op jit(solution)/shard_map/dot_general | solution.py:528
  189.7 2.6 %add_multiply_fusion = f32[512,1024]{1,0:T(8,128)} fusion(f32[512,1024]{1,0:T(8,128)S(1)} %fusion, bf16[1024,1024]{1,0:T(8,128)(2,1)S(1)} %copy-done.9, s32[]{:T(128)S(6)} %select_n.9), kind=kOutput, calls=%fused_computation | convolution fusion | flops 1074790400 | bytes 7340036 | tf_op jit(solution)/shard_map/dot_general | solution.py:528
  192.3 2.9 %all-to-all-done.2.pieces = bf16[8,64,1024]{2,1,0:T(8,128)(2,1)S(1)} async-done(((bf16[8,64,1024]{2,1,0:T(8,128)(2,1)}), bf16[8,64,1024]{2,1,0:T(8,128)(2,1)S(1)}, u32[]{:S(2)}, u32[]{:S(2)}) %all-to-all-start.2) | async-done | bytes 1048608 | tf_op jit(solution)/shard_map/all_to_all | solution.py:82
  (49 shorter events, 3.0 us)
Async XLA Ops:
  17.9 9.4 %collective-permute-start.4 = (bf16[176,1024]{1,0:T(8,128)(2,1)S(1)}, bf16[176,1024]{1,0:T(8,128)(2,1)S(1)}, u32[]{:S(2)}, u32[]{:S(2)}) collective-permute-start(bf16[176,1024]{1,0:T(8,128)(2,1)S(1)} %get-tuple-element.24), channel_id=1, source_target_pairs={{0,24},{1,9},{2,26},{3,11},{4,28},{5,13},{6,30},{7,15},{8,16},{9,1... | collective-permute-start | bytes 1081352 | tf_op jit(solution)/shard_map/ppermute | solution.py:91
  20.3 8.6 %collective-permute-start = (bf16[176,1024]{1,0:T(8,128)(2,1)S(1)}, bf16[176,1024]{1,0:T(8,128)(2,1)S(1)}, u32[]{:S(2)}, u32[]{:S(2)}) collective-permute-start(bf16[176,1024]{1,0:T(8,128)(2,1)S(1)} %get-tuple-element.25), channel_id=1, source_target_pairs={{0,96},{1,33},{2,98},{3,35},{4,100},{5,37},{6,102},{7,39},{8,104},... | collective-permute-start | bytes 1081352 | tf_op jit(solution)/shard_map/ppermute | solution.py:91
  22.7 8.7 %collective-permute-start.8 = (bf16[160,1024]{1,0:T(8,128)(2,1)S(1)}, bf16[160,1024]{1,0:T(8,128)(2,1)S(1)}, u32[]{:S(2)}, u32[]{:S(2)}) collective-permute-start(bf16[160,1024]{1,0:T(8,128)(2,1)S(1)} %slice.14), channel_id=1, source_target_pairs={{0,6},{1,3},{2,4},{3,1},{4,2},{5,7},{6,0},{7,5},{8,14},{9,11},{10,... | collective-permute-start | bytes 983048 | tf_op jit(solution)/shard_map/ppermute | solution.py:91
  27.4 39.1 %copy-start = (bf16[352,1024]{1,0:T(8,128)(2,1)}, bf16[352,1024]{1,0:T(8,128)(2,1)S(1)}, u32[]{:S(2)}) copy-start(bf16[352,1024]{1,0:T(8,128)(2,1)S(1)} %pad_maximum_fusion.1.refs_2_.refs_4_) | copy-start | bytes 2162692
  27.4 23.7 %collective-permute-start.6 = (bf16[352,1024]{1,0:T(8,128)(2,1)S(1)}, bf16[352,1024]{1,0:T(8,128)(2,1)S(1)}, u32[]{:S(2)}, u32[]{:S(2)}) collective-permute-start(bf16[352,1024]{1,0:T(8,128)(2,1)S(1)} %pad_maximum_fusion.1.refs_2_.refs_4_), channel_id=1, source_target_pairs={{0,6},{1,3},{2,4},{3,1},{4,2},{5,7},{6,0},{7,5},{8,14},{9,11},{10,... | collective-permute-start | bytes 2162696 | tf_op jit(solution)/shard_map/ppermute | solution.py:91
  29.0 37.5 %copy-start.1 = (bf16[352,1024]{1,0:T(8,128)(2,1)}, bf16[352,1024]{1,0:T(8,128)(2,1)S(1)}, u32[]{:S(2)}) copy-start(bf16[352,1024]{1,0:T(8,128)(2,1)S(1)} %pad_maximum_fusion.refs_0_) | copy-start | bytes 2162692
  29.0 24.0 %collective-permute-start.2 = (bf16[352,1024]{1,0:T(8,128)(2,1)S(1)}, bf16[352,1024]{1,0:T(8,128)(2,1)S(1)}, u32[]{:S(2)}, u32[]{:S(2)}) collective-permute-start(bf16[352,1024]{1,0:T(8,128)(2,1)S(1)} %pad_maximum_fusion.refs_0_), channel_id=1, source_target_pairs={{0,24},{1,9},{2,26},{3,11},{4,28},{5,13},{6,30},{7,15},{8,16},{9,1... | collective-permute-start | bytes 2162696 | tf_op jit(solution)/shard_map/ppermute | solution.py:91
  31.5 35.0 %copy-start.2 = (bf16[320,1024]{1,0:T(8,128)(2,1)}, bf16[320,1024]{1,0:T(8,128)(2,1)S(1)}, u32[]{:S(2)}) copy-start(bf16[320,1024]{1,0:T(8,128)(2,1)S(1)} %pad_maximum_fusion.2.refs_4_.refs_8_) | copy-start | bytes 1966084
  31.5 12.0 %collective-permute-start.10 = (bf16[320,1024]{1,0:T(8,128)(2,1)S(1)}, bf16[320,1024]{1,0:T(8,128)(2,1)}, u32[]{:S(2)}, u32[]{:S(2)}) collective-permute-start(bf16[320,1024]{1,0:T(8,128)(2,1)S(1)} %pad_maximum_fusion.2.refs_4_.refs_8_), channel_id=1, source_target_pairs={{0,96},{1,33},{2,98},{3,35},{4,100},{5,37},{6,102},{7,39},{8,104},... | collective-permute-start | bytes 1966088 | tf_op jit(solution)/shard_map/ppermute | solution.py:91
  33.6 15.2 %collective-permute-start.9 = (bf16[320,1024]{1,0:T(8,128)(2,1)S(1)}, bf16[320,1024]{1,0:T(8,128)(2,1)}, u32[]{:S(2)}, u32[]{:S(2)}) collective-permute-start(bf16[320,1024]{1,0:T(8,128)(2,1)S(1)} %pad_maximum_fusion.2.refs_4_.refs_8_), channel_id=1, source_target_pairs={{0,24},{1,9},{2,26},{3,11},{4,28},{5,13},{6,30},{7,15},{8,16},{9,1... | collective-permute-start | bytes 1966088 | tf_op jit(solution)/shard_map/ppermute | solution.py:91
  35.6 57.8 %copy-start.5 = (s32[1,192]{1,0:T(1,128)}, s32[1,192]{1,0:T(1,128)S(1)}, u32[]{:S(2)}) copy-start(s32[1,192]{1,0:T(1,128)S(1)} %constant_dynamic-slice_fusion) | copy-start | bytes 2308
  35.6 41.0 %collective-permute-start.5 = (bf16[352,1024]{1,0:T(8,128)(2,1)S(1)}, bf16[352,1024]{1,0:T(8,128)(2,1)}, u32[]{:S(2)}, u32[]{:S(2)}) collective-permute-start(bf16[352,1024]{1,0:T(8,128)(2,1)S(1)} %pad_maximum_fusion.1.refs_2_.refs_4_), channel_id=1, source_target_pairs={{0,96},{1,33},{2,98},{3,35},{4,100},{5,37},{6,102},{7,39},{8,104},... | collective-permute-start | bytes 2162696 | tf_op jit(solution)/shard_map/ppermute | solution.py:91
  43.5 33.1 %collective-permute-start.1 = (bf16[352,1024]{1,0:T(8,128)(2,1)S(1)}, bf16[352,1024]{1,0:T(8,128)(2,1)}, u32[]{:S(2)}, u32[]{:S(2)}) collective-permute-start(bf16[352,1024]{1,0:T(8,128)(2,1)S(1)} %pad_maximum_fusion.refs_0_), channel_id=1, source_target_pairs={{0,6},{1,3},{2,4},{3,1},{4,2},{5,7},{6,0},{7,5},{8,14},{9,11},{10,... | collective-permute-start | bytes 2162696 | tf_op jit(solution)/shard_map/ppermute | solution.py:91
  48.8 27.9 %collective-permute-start.11 = (bf16[320,1024]{1,0:T(8,128)(2,1)}, bf16[320,1024]{1,0:T(8,128)(2,1)}, u32[]{:S(2)}, u32[]{:S(2)}) collective-permute-start(bf16[320,1024]{1,0:T(8,128)(2,1)} %collective-permute-done.10.refs_5_.refs_9_), channel_id=1, source_target_pairs={{0,24},{1,9},{2,26},{3,11},{4,28},{5,13},{6,30},{7,15},{8,16},{9,1... | collective-permute-start | bytes 1966088 | tf_op jit(solution)/shard_map/ppermute | solution.py:91
  51.1 15.4 %copy-start.3 = (bf16[352,1024]{1,0:T(8,128)(2,1)}, bf16[352,1024]{1,0:T(8,128)(2,1)S(1)}, u32[]{:S(2)}) copy-start(bf16[352,1024]{1,0:T(8,128)(2,1)S(1)} %collective-permute-done.6.refs_3_.refs_5_) | copy-start | bytes 2162692
  51.1 25.5 %collective-permute-start.7 = (bf16[352,1024]{1,0:T(8,128)(2,1)S(1)}, bf16[352,1024]{1,0:T(8,128)(2,1)}, u32[]{:S(2)}, u32[]{:S(2)}) collective-permute-start(bf16[352,1024]{1,0:T(8,128)(2,1)S(1)} %collective-permute-done.6.refs_3_.refs_5_), channel_id=1, source_target_pairs={{0,96},{1,33},{2,98},{3,35},{4,100},{5,37},{6,102},{7,39},{8,104},... | collective-permute-start | bytes 2162696 | tf_op jit(solution)/shard_map/ppermute | solution.py:91
  53.1 13.4 %copy-start.4 = (bf16[352,1024]{1,0:T(8,128)(2,1)}, bf16[352,1024]{1,0:T(8,128)(2,1)S(1)}, u32[]{:S(2)}) copy-start(bf16[352,1024]{1,0:T(8,128)(2,1)S(1)} %collective-permute-done.2.refs_1_) | copy-start | bytes 2162692
  53.1 23.5 %collective-permute-start.3 = (bf16[352,1024]{1,0:T(8,128)(2,1)S(1)}, bf16[352,1024]{1,0:T(8,128)(2,1)}, u32[]{:S(2)}, u32[]{:S(2)}) collective-permute-start(bf16[352,1024]{1,0:T(8,128)(2,1)S(1)} %collective-permute-done.2.refs_1_), channel_id=1, source_target_pairs={{0,6},{1,3},{2,4},{3,1},{4,2},{5,7},{6,0},{7,5},{8,14},{9,11},{10,... | collective-permute-start | bytes 2162696 | tf_op jit(solution)/shard_map/ppermute | solution.py:91
  54.5 12.0 %copy-start.8 = (s32[1024]{0:T(1024)S(1)}, s32[1024]{0:T(1024)}, u32[]{:S(2)}) copy-start(s32[1024]{0:T(1024)} %param.7) | copy-start | bytes 12292
  66.5 10.1 %copy-start.6 = (s32[1024]{0:T(1024)}, s32[1024]{0:T(1024)S(1)}, u32[]{:S(2)}) copy-start(s32[1024]{0:T(1024)S(1)} %broadcast_subtract_fusion) | copy-start | bytes 12292
  87.8 17.4 %all-to-all-start.1 = ((f32[64,16,128]{2,1,0:T(8,128)}), f32[64,16,128]{2,1,0:T(8,128)}, u32[]{:S(2)}, u32[]{:S(2)}) async-start(f32[64,16,128]{2,1,0:T(8,128)} %get-tuple-element.14), calls=%async_computation.1 | async-start | bytes 1048576 | tf_op jit(solution)/shard_map/all_to_all | solution.py:517
  116.7 20.5 %collective-permute-start.15 = (bf16[4,176,1024]{2,1,0:T(8,128)(2,1)}, bf16[4,176,1024]{2,1,0:T(8,128)(2,1)}, u32[]{:S(2)}, u32[]{:S(2)}) collective-permute-start(bf16[4,176,1024]{2,1,0:T(8,128)(2,1)} %get-tuple-element.21), channel_id=1, source_target_pairs={{0,96},{1,33},{2,98},{3,35},{4,100},{5,37},{6,102},{7,39},{8,104},... | collective-permute-start | bytes 4325384 | tf_op jit(solution)/shard_map/ppermute | solution.py:160
  118.5 22.4 %collective-permute-start.12 = (bf16[4,176,1024]{2,1,0:T(8,128)(2,1)}, bf16[4,176,1024]{2,1,0:T(8,128)(2,1)}, u32[]{:S(2)}, u32[]{:S(2)}) collective-permute-start(bf16[4,176,1024]{2,1,0:T(8,128)(2,1)} %get-tuple-element.19), channel_id=1, source_target_pairs={{0,6},{1,3},{2,4},{3,1},{4,2},{5,7},{6,0},{7,5},{8,14},{9,11},{10,... | collective-permute-start | bytes 4325384 | tf_op jit(solution)/shard_map/ppermute | solution.py:160
  121.2 33.3 %collective-permute-start.18 = (bf16[4,160,1024]{2,1,0:T(8,128)(2,1)}, bf16[4,160,1024]{2,1,0:T(8,128)(2,1)}, u32[]{:S(2)}, u32[]{:S(2)}) collective-permute-start(bf16[4,160,1024]{2,1,0:T(8,128)(2,1)} %get-tuple-element.23), channel_id=1, source_target_pairs={{0,24},{1,9},{2,26},{3,11},{4,28},{5,13},{6,30},{7,15},{8,16},{9,1... | collective-permute-start | bytes 3932168 | tf_op jit(solution)/shard_map/ppermute | solution.py:160
  123.9 62.4 %collective-permute-start.21 = (bf16[1024,1024]{1,0:T(8,128)(2,1)}, bf16[1024,1024]{1,0:T(8,128)(2,1)}, u32[]{:S(2)}, u32[]{:S(2)}) collective-permute-start(bf16[1024,1024]{1,0:T(8,128)(2,1)} %get-tuple-element.17.grad), channel_id=1, source_target_pairs={{0,1},{1,0},{2,3},{3,2},{4,5},{5,4},{6,7},{7,6},{8,9},{9,8},{10,11... | collective-permute-start | bytes 6291464 | tf_op jit(solution)/shard_map/ppermute | solution.py:530
  139.4 19.7 %collective-permute-start.16 = (bf16[2,176,1024]{2,1,0:T(8,128)(2,1)}, bf16[2,176,1024]{2,1,0:T(8,128)(2,1)}, u32[]{:S(2)}, u32[]{:S(2)}) collective-permute-start(bf16[2,176,1024]{2,1,0:T(8,128)(2,1)} %shard_map.92), channel_id=1, source_target_pairs={{0,6},{1,3},{2,4},{3,1},{4,2},{5,7},{6,0},{7,5},{8,14},{9,11},{10,... | collective-permute-start | bytes 2162696 | tf_op jit(solution)/shard_map/ppermute | solution.py:160
  143.0 17.9 %collective-permute-start.13 = (bf16[2,176,1024]{2,1,0:T(8,128)(2,1)}, bf16[2,176,1024]{2,1,0:T(8,128)(2,1)}, u32[]{:S(2)}, u32[]{:S(2)}) collective-permute-start(bf16[2,176,1024]{2,1,0:T(8,128)(2,1)} %shard_map.90), channel_id=1, source_target_pairs={{0,24},{1,9},{2,26},{3,11},{4,28},{5,13},{6,30},{7,15},{8,16},{9,1... | collective-permute-start | bytes 2162696 | tf_op jit(solution)/shard_map/ppermute | solution.py:160
  154.4 29.6 %collective-permute-start.22 = (f32[64,4096]{1,0:T(8,128)}, f32[64,4096]{1,0:T(8,128)}, u32[]{:S(2)}, u32[]{:S(2)}) collective-permute-start(f32[64,4096]{1,0:T(8,128)} %shard_map.98), channel_id=1, source_target_pairs={{0,1},{1,0},{2,3},{3,2},{4,5},{5,4},{6,7},{7,6},{8,9},{9,8},{10,11... | collective-permute-start | bytes 3145736 | tf_op jit(solution)/shard_map/ppermute | solution.py:531
  155.9 11.9 %collective-permute-start.19 = (bf16[2,160,1024]{2,1,0:T(8,128)(2,1)S(1)}, bf16[2,160,1024]{2,1,0:T(8,128)(2,1)S(1)}, u32[]{:S(2)}, u32[]{:S(2)}) collective-permute-start(bf16[2,160,1024]{2,1,0:T(8,128)(2,1)S(1)} %shard_map.94), channel_id=1, source_target_pairs={{0,96},{1,33},{2,98},{3,35},{4,100},{5,37},{6,102},{7,39},{8,104},... | collective-permute-start | bytes 1966088 | tf_op jit(solution)/shard_map/ppermute | solution.py:160
  160.4 17.0 %collective-permute-start.17 = (bf16[1,176,1024]{2,1,0:T(8,128)(2,1)S(1)}, bf16[1,176,1024]{2,1,0:T(8,128)(2,1)S(1)}, u32[]{:S(2)}, u32[]{:S(2)}) collective-permute-start(bf16[1,176,1024]{2,1,0:T(8,128)(2,1)S(1)} %shard_map.93), channel_id=1, source_target_pairs={{0,24},{1,9},{2,26},{3,11},{4,28},{5,13},{6,30},{7,15},{8,16},{9,1... | collective-permute-start | bytes 1081352 | tf_op jit(solution)/shard_map/ppermute | solution.py:160
  162.3 15.1 %collective-permute-start.14 = (bf16[1,176,1024]{2,1,0:T(8,128)(2,1)S(1)}, bf16[1,176,1024]{2,1,0:T(8,128)(2,1)S(1)}, u32[]{:S(2)}, u32[]{:S(2)}) collective-permute-start(bf16[1,176,1024]{2,1,0:T(8,128)(2,1)S(1)} %shard_map.91), channel_id=1, source_target_pairs={{0,96},{1,33},{2,98},{3,35},{4,100},{5,37},{6,102},{7,39},{8,104},... | collective-permute-start | bytes 1081352 | tf_op jit(solution)/shard_map/ppermute | solution.py:160
  169.0 8.4 %collective-permute-start.20 = (bf16[1,160,1024]{2,1,0:T(8,128)(2,1)S(1)}, bf16[1,160,1024]{2,1,0:T(8,128)(2,1)S(1)}, u32[]{:S(2)}, u32[]{:S(2)}) collective-permute-start(bf16[1,160,1024]{2,1,0:T(8,128)(2,1)S(1)} %shard_map.95), channel_id=1, source_target_pairs={{0,6},{1,3},{2,4},{3,1},{4,2},{5,7},{6,0},{7,5},{8,14},{9,11},{10,... | collective-permute-start | bytes 983048 | tf_op jit(solution)/shard_map/ppermute | solution.py:160
  180.3 3.7 %copy-start.7 = (f32[64,4096]{1,0:T(8,128)S(1)}, f32[64,4096]{1,0:T(8,128)}, u32[]{:S(2)}) copy-start(f32[64,4096]{1,0:T(8,128)} %shard_map.98) | copy-start | bytes 3145732
  180.3 14.9 %all-to-all-start.2 = ((bf16[8,64,1024]{2,1,0:T(8,128)(2,1)}), bf16[8,64,1024]{2,1,0:T(8,128)(2,1)S(1)}, u32[]{:S(2)}, u32[]{:S(2)}) async-start(bf16[8,64,1024]{2,1,0:T(8,128)(2,1)} %bitcast.6), calls=%async_computation.2 | async-start | bytes 2097152 | tf_op jit(solution)/shard_map/all_to_all | solution.py:82
  186.3 3.4 %copy-start.9 = (bf16[1024,1024]{1,0:T(8,128)(2,1)S(1)}, bf16[1024,1024]{1,0:T(8,128)(2,1)}, u32[]{:S(2)}) copy-start(bf16[1024,1024]{1,0:T(8,128)(2,1)} %get-tuple-element.17.grad) | copy-start | bytes 6291460

commit v6 on v5

--- a/solution.py
+++ b/solution.py
@@ -206,13 +206,18 @@
 
 def a_kernel(chips, *refs):
     got, (own, out, h, sem) = refs[:12], refs[12:]
-    for _, copies in gather_copies(chips, got, h):
+    quarter = h.shape[0] // 4
+    quarters = gather_copies(chips, got, h)
+    for q, (_, copies) in enumerate(quarters):
         for src, dst in copies:
-            pltpu.make_async_copy(src, dst, sem).start()
-    pltpu.make_async_copy(h, h, sem).wait()
-    out[...] = lax.dot_general(
-        own[...], h[...], (((1,), (1,)), ((), ())), preferred_element_type=F32
-    )
+            pltpu.make_async_copy(src, dst, sem.at[q]).start()
+    for q, (y, _) in enumerate(quarters):
+        some = h.at[pl.ds(0, quarter)]
+        pltpu.make_async_copy(some, some, sem.at[q]).wait()
+        here = pl.ds(pl.multiple_of(y * quarter, quarter), quarter)
+        out[:, here] = lax.dot_general(
+            own[...], h[here, :], (((1,), (1,)), ((), ())), preferred_element_type=F32
+        )
 
 
 def a_part_of(chips, got, own):
@@ -226,7 +231,7 @@
             in_specs=[pl.BlockSpec(memory_space=pltpu.HBM)] * len(got)
             + [pl.BlockSpec(memory_space=pltpu.VMEM)],
             out_specs=pl.BlockSpec(memory_space=pltpu.VMEM),
-            scratch_shapes=[pltpu.VMEM((width, tokens), BF16), pltpu.SemaphoreType.DMA],
+            scratch_shapes=[pltpu.VMEM((width, tokens), BF16), pltpu.SemaphoreType.DMA((4,))],
         ),
         out_shape=jax.ShapeDtypeStruct((feats, width), F32),
         compiler_params=pltpu.CompilerParams(vmem_limit_bytes=ALL_VMEM),
@@ -390,7 +395,7 @@
         out_specs=[block, pl.BlockSpec((64, lines, 128), lambda i: (0, 0, 0))] if late else block,
         out_shape=[
             pltpu.HBM((vocab_rows, tokens), F32), jax.ShapeDtypeStruct((64, lines, 128), F32),
-        ] if late else pltpu.HBM((vocab_rows, tokens), F32),
+        ] if late else jax.ShapeDtypeStruct((vocab_rows, tokens), F32),
         scratch_shapes=[pltpu.VMEM((width // 2, tokens), BF16)]
         + [pltpu.VMEM((1, tokens), F32)] * (3 if late else 0)
         + [pltpu.SemaphoreType.DMA((4,)) if late else pltpu.SemaphoreType.DMA],
@@ -402,7 +407,7 @@
             bytes_accessed=width * (vocab_rows + tokens) + 4 * vocab_rows * tokens,
             transcendentals=vocab_rows * tokens,
         ),
-    )(*got, in_hbm(wide), *([in_hbm(part), tgt] if late else []))
+    )(*got, in_hbm(wide), *([part, tgt] if late else []))
 
 
 def signal_kernel(stats, logits, cot, tgt, tall, grad, loss, *refs):

time: 197 us -> 194 us (0.985)
  Pallas kernels: 85.6 us -> 82 us
    pallas_call x2, Pallas kernels: 21.2 us -> 19.1 us  [half_logits(): pl.pallas_call(late_kernel if late else early_kernel, grid=(vocab_rows //...]
  transfers between devices with their start and end apart: 25 -> 25, of which waited for: 9 -> 9; matrix products, arithmetic and copies ran while one was open for 5% -> 5% of each run, Pallas kernels for 32% -> 31%
where the time goes in v6:
time: 194 us; the launch traced here: 193 us
  Pallas kernels  82 us (42%)
  starting transfers between devices  47.6 us (25%)
  waiting for transfers between devices  35.5 us (18%)
  blocking collectives  16.2 us (8%)
  matrix products  5.96 us (3%)
  other arithmetic  2.44 us (1%)
    ppermute x12, starting transfers between devices, get(): return lax.ppermute(x, ALL, LARGE_PAIRS[(g + step) % 3])  21.9 us
    pallas_call x2, Pallas kernels, half_logits(): pl.pallas_call(late_kernel if late else early_kernel, grid=(vocab_rows //...  19.1 us
    ppermute x9, waiting for transfers between devices, trade(): return lax.ppermute(x, ALL, LARGE_PAIRS[(g + step) % 3])  17.8 us
    ppermute x9, starting transfers between devices, trade(): return lax.ppermute(x, ALL, LARGE_PAIRS[(g + step) % 3])  16.4 us
    all_to_all x1, blocking collectives, small_stage(): lax.all_to_all(x, ALL, 0, 0, axis_index_groups=SMALL_CUBES, tiled=True)  16.2 us
    ppermute x12, waiting for transfers between devices, get(): return lax.ppermute(x, ALL, LARGE_PAIRS[(g + step) % 3])  13.8 us
    pallas_call x1, Pallas kernels, columns_turned(): pl.pallas_call(columns_kernel, grid_spec=pltpu.PrefetchScalarGridSpec(num...  12 us
    pallas_call x1, Pallas kernels, signal_of(): pl.pallas_call(signal_kernel, grid=(count + 4,), in_specs=[whole(*stats.s...  11.5 us
  transfers between devices with their start and end apart: 25, of which 9 were waited for; matrix products, arithmetic and copies ran while one was open for 5% of the time, Pallas kernels for 31%

profile of v6, /device:TPU:0, one launch (start us, length us, event | category | flops | bytes accessed | tf_op | source)
XLA Modules:
  0.0 192.6 jit_solution(7597554295731342695)
XLA Ops:
  0.6 1.0 broadcast_in_dim.12
  1.7 16.2 %all_to_all.15 = bf16[8,64,1024]{2,1,0:T(8,128)(2,1)S(1)} all-to-all(bf16[8,64,1024]{2,1,0:T(8,128)(2,1)S(1)} %broadcast_in_dim.12), channel_id=1, replica_groups={{0,2,8,10,32,34,40,42},{4,6,12,14,36,38,44,46},{16,18,24,26,48,50,56,58..., dimensions={0} | all-to-all | bytes 2097152 | tf_op jit(solution)/shard_map/all_to_all | solution.py:82
  17.9 2.4 %collective-permute-start.4 = (bf16[176,1024]{1,0:T(8,128)(2,1)S(1)}, bf16[176,1024]{1,0:T(8,128)(2,1)S(1)}, u32[]{:S(2)}, u32[]{:S(2)}) collective-permute-start(bf16[176,1024]{1,0:T(8,128)(2,1)S(1)} %get-tuple-element.24), channel_id=1, source_target_pairs={{0,24},{1,9},{2,26},{3,11},{4,28},{5,13},{6,30},{7,15},{8,16},{9,1... | collective-permute-start | bytes 1081352 | tf_op jit(solution)/shard_map/ppermute | solution.py:91
  20.3 2.4 %collective-permute-start = (bf16[176,1024]{1,0:T(8,128)(2,1)S(1)}, bf16[176,1024]{1,0:T(8,128)(2,1)S(1)}, u32[]{:S(2)}, u32[]{:S(2)}) collective-permute-start(bf16[176,1024]{1,0:T(8,128)(2,1)S(1)} %get-tuple-element.25), channel_id=1, source_target_pairs={{0,96},{1,33},{2,98},{3,35},{4,100},{5,37},{6,102},{7,39},{8,104},... | collective-permute-start | bytes 1081352 | tf_op jit(solution)/shard_map/ppermute | solution.py:91
  22.7 1.9 collective-permute-start.8
  24.6 2.7 %collective-permute-done.4 = bf16[176,1024]{1,0:T(8,128)(2,1)S(1)} collective-permute-done((bf16[176,1024]{1,0:T(8,128)(2,1)S(1)}, bf16[176,1024]{1,0:T(8,128)(2,1)S(1)}, u32[]{:S(2)}, u32[]{:S(2)}) %collective-permute-start.4) | collective-permute-done | bytes 360480 | tf_op jit(solution)/shard_map/ppermute | solution.py:91
  27.4 1.4 collective-permute-start.6
  29.0 2.4 %collective-permute-start.2 = (bf16[352,1024]{1,0:T(8,128)(2,1)S(1)}, bf16[352,1024]{1,0:T(8,128)(2,1)S(1)}, u32[]{:S(2)}, u32[]{:S(2)}) collective-permute-start(bf16[352,1024]{1,0:T(8,128)(2,1)S(1)} %pad_maximum_fusion.refs_0_), channel_id=1, source_target_pairs={{0,24},{1,9},{2,26},{3,11},{4,28},{5,13},{6,30},{7,15},{8,16},{9,1... | collective-permute-start | bytes 2162696 | tf_op jit(solution)/shard_map/ppermute | solution.py:91
  31.5 2.1 %collective-permute-start.10 = (bf16[320,1024]{1,0:T(8,128)(2,1)S(1)}, bf16[320,1024]{1,0:T(8,128)(2,1)}, u32[]{:S(2)}, u32[]{:S(2)}) collective-permute-start(bf16[320,1024]{1,0:T(8,128)(2,1)S(1)} %pad_maximum_fusion.2.refs_4_.refs_8_), channel_id=1, source_target_pairs={{0,96},{1,33},{2,98},{3,35},{4,100},{5,37},{6,102},{7,39},{8,104},... | collective-permute-start | bytes 1966088 | tf_op jit(solution)/shard_map/ppermute | solution.py:91
  33.6 1.3 collective-permute-start.9
  35.6 0.9 collective-permute-start.5
  36.4 7.1 %collective-permute-done.10.refs_5_.refs_9_ = bf16[320,1024]{1,0:T(8,128)(2,1)} collective-permute-done((bf16[320,1024]{1,0:T(8,128)(2,1)S(1)}, bf16[320,1024]{1,0:T(8,128)(2,1)}, u32[]{:S(2)}, u32[]{:S(2)}) %collective-permute-start.10) | collective-permute-done | bytes 655392 | tf_op jit(solution)/shard_map/ppermute | solution.py:91
  43.5 1.5 collective-permute-start.1
  45.0 3.8 %collective-permute-done.9.refs_4_.refs_10_ = bf16[320,1024]{1,0:T(8,128)(2,1)} collective-permute-done((bf16[320,1024]{1,0:T(8,128)(2,1)S(1)}, bf16[320,1024]{1,0:T(8,128)(2,1)}, u32[]{:S(2)}, u32[]{:S(2)}) %collective-permute-start.9) | collective-permute-done | bytes 655392 | tf_op jit(solution)/shard_map/ppermute | solution.py:91
  48.8 2.3 %collective-permute-start.11 = (bf16[320,1024]{1,0:T(8,128)(2,1)}, bf16[320,1024]{1,0:T(8,128)(2,1)}, u32[]{:S(2)}, u32[]{:S(2)}) collective-permute-start(bf16[320,1024]{1,0:T(8,128)(2,1)} %collective-permute-done.10.refs_5_.refs_9_), channel_id=1, source_target_pairs={{0,24},{1,9},{2,26},{3,11},{4,28},{5,13},{6,30},{7,15},{8,16},{9,1... | collective-permute-start | bytes 1966088 | tf_op jit(solution)/shard_map/ppermute | solution.py:91
  51.1 2.0 %collective-permute-start.7 = (bf16[352,1024]{1,0:T(8,128)(2,1)S(1)}, bf16[352,1024]{1,0:T(8,128)(2,1)}, u32[]{:S(2)}, u32[]{:S(2)}) collective-permute-start(bf16[352,1024]{1,0:T(8,128)(2,1)S(1)} %collective-permute-done.6.refs_3_.refs_5_), channel_id=1, source_target_pairs={{0,96},{1,33},{2,98},{3,35},{4,100},{5,37},{6,102},{7,39},{8,104},... | collective-permute-start | bytes 2162696 | tf_op jit(solution)/shard_map/ppermute | solution.py:91
  53.1 1.4 collective-permute-start.3
  54.5 12.0 %shard_map.84.refs_6_ = bf16[1024,4096]{1,0:T(8,128)(2,1)} custom-call(s32[192]{0:T(256)S(1)} %bitcast.10, bf16[1024,4096]{1,0:T(8,128)(2,1)} %w.3), custom_call_target="tpu_custom_call" | custom-call | flops 4294967296 | bytes 16777216 | tf_op jit(solution)/shard_map/pallas_call | solution.py:266
  66.6 8.6 %shard_map.85.refs_7_ = f32[1024,1024]{1,0:T(8,128)S(1)} custom-call(bf16[352,1024]{1,0:T(8,128)(2,1)S(1)} %pad_maximum_fusion.refs_0_, bf16[352,1024]{1,0:T(8,128)(2,1)S(1)} %collective-permute-done.2.refs_1_, bf16[352,1024]{1,0:T(8,128)(2,1)S(1)} %pad_maximum_fusion.1.refs_2_.refs_4_, bf16[352,1024]{1,0:T(8,128)(2,1)S(1)} %collective-permute-done.6.refs_3_.refs_5_, ...), custom_call_target="tpu_custom_call" | custom-call | flops 4294967296 | bytes 12582912 | tf_op jit(solution)/shard_map/pallas_call | solution.py:389
  75.3 10.4 %shard_map.86 = (f32[1024,1024]{1,0:T(8,128)}, f32[64,16,128]{2,1,0:T(8,128)}) custom-call(bf16[352,1024]{1,0:T(8,128)(2,1)} %collective-permute-done.1.refs_0_.refs_2_, bf16[352,1024]{1,0:T(8,128)(2,1)} %collective-permute-done.3.refs_1_.refs_3_, bf16[352,1024]{1,0:T(8,128)(2,1)} %collective-permute-done.5.refs_2_.refs_6_, ...), custom_call_target="tpu_custom_call" | custom-call | flops 4294967296 | bytes 12582912 | tf_op jit(solution)/shard_map/pallas_call | solution.py:389
  85.7 5.5 %all-to-all-start.1 = ((f32[64,16,128]{2,1,0:T(8,128)}), f32[64,16,128]{2,1,0:T(8,128)}, u32[]{:S(2)}, u32[]{:S(2)}) async-start(f32[64,16,128]{2,1,0:T(8,128)} %get-tuple-element.14), calls=%async_computation.1 | async-start | bytes 1048576 | tf_op jit(solution)/shard_map/all_to_all | solution.py:522
  91.2 10.7 %shard_map.87.tall = bf16[4096,1024]{1,0:T(8,128)(2,1)} custom-call(s32[192]{0:T(256)S(1)} %bitcast.11, bf16[1024,4096]{1,0:T(8,128)(2,1)} %w.3), custom_call_target="tpu_custom_call" | custom-call | flops 4294967296 | bytes 16777216 | tf_op jit(solution)/shard_map/pallas_call | solution.py:303
  102.0 1.2 all-to-all-done.1.stats
  103.1 11.5 %shard_map.88 = (bf16[1024,1024]{1,0:T(8,128)(2,1)}, f32[1,1024]{1,0:T(1,128)}, bf16[4,176,1024]{2,1,0:T(8,128)(2,1)}, bf16[4,176,1024]{2,1,0:T(8,128)(2,1)}, bf16[4,160,1024]{2,1,0:T(8,128)(2,1)}) custom-call(f32[64,16,128]{2,1,0:T(8,128)} %all-to-all-done.1.stats, f32[1024,1024]{1,0:T(8,128)} %get-tuple-element.15.logits, f32[1,1024]{1,0:T(1,128)} %bitcast.20, ...), custom_call_target="tpu_custom_call" | custom-call | flops 4294967296 | bytes 14680064 | tf_op jit(solution)/shard_map/pallas_call | solution.py:453
  114.6 1.8 collective-permute-start.15
  116.4 2.7 %collective-permute-start.12 = (bf16[4,176,1024]{2,1,0:T(8,128)(2,1)}, bf16[4,176,1024]{2,1,0:T(8,128)(2,1)}, u32[]{:S(2)}, u32[]{:S(2)}) collective-permute-start(bf16[4,176,1024]{2,1,0:T(8,128)(2,1)} %get-tuple-element.19), channel_id=1, source_target_pairs={{0,6},{1,3},{2,4},{3,1},{4,2},{5,7},{6,0},{7,5},{8,14},{9,11},{10,... | collective-permute-start | bytes 4325384 | tf_op jit(solution)/shard_map/ppermute | solution.py:160
  119.1 2.8 %collective-permute-start.18 = (bf16[4,160,1024]{2,1,0:T(8,128)(2,1)}, bf16[4,160,1024]{2,1,0:T(8,128)(2,1)}, u32[]{:S(2)}, u32[]{:S(2)}) collective-permute-start(bf16[4,160,1024]{2,1,0:T(8,128)(2,1)} %get-tuple-element.23), channel_id=1, source_target_pairs={{0,24},{1,9},{2,26},{3,11},{4,28},{5,13},{6,30},{7,15},{8,16},{9,1... | collective-permute-start | bytes 3932168 | tf_op jit(solution)/shard_map/ppermute | solution.py:160
  121.9 8.2 %shard_map.89 = (bf16[4,176,1024]{2,1,0:T(8,128)(2,1)}, bf16[4,176,1024]{2,1,0:T(8,128)(2,1)}, bf16[4,160,1024]{2,1,0:T(8,128)(2,1)}) custom-call(bf16[4096,1024]{1,0:T(8,128)(2,1)} %shard_map.87.tall, bf16[1024,1024]{1,0:T(8,128)(2,1)} %get-tuple-element.17.grad), custom_call_target="tpu_custom_call" | custom-call | flops 4294967296 | bytes 8388608 | tf_op jit(solution)/shard_map/pallas_call | solution.py:491
  130.0 5.1 %collective-permute-done.15.refs_1_.refs_5_ = bf16[4,176,1024]{2,1,0:T(8,128)(2,1)} collective-permute-done((bf16[4,176,1024]{2,1,0:T(8,128)(2,1)}, bf16[4,176,1024]{2,1,0:T(8,128)(2,1)}, u32[]{:S(2)}, u32[]{:S(2)}) %collective-permute-start.15) | collective-permute-done | bytes 1441824 | tf_op jit(solution)/shard_map/ppermute | solution.py:160
  135.1 2.1 %shard_map.92 = bf16[2,176,1024]{2,1,0:T(8,128)(2,1)} custom-call(bf16[4,176,1024]{2,1,0:T(8,128)(2,1)} %get-tuple-element.20.refs_0_.refs_4_, bf16[4,176,1024]{2,1,0:T(8,128)(2,1)} %collective-permute-done.15.refs_1_.refs_5_), custom_call_target="tpu_custom_call" | custom-call | flops 720896 | bytes 2162688 | tf_op jit(solution)/shard_map/pallas_call | solution.py:113
  137.3 1.5 collective-permute-start.16
  138.8 2.1 %shard_map.90 = bf16[2,176,1024]{2,1,0:T(8,128)(2,1)} custom-call(bf16[4,176,1024]{2,1,0:T(8,128)(2,1)} %get-tuple-element.18.refs_0_, bf16[4,176,1024]{2,1,0:T(8,128)(2,1)} %collective-permute-done.12.refs_1_), custom_call_target="tpu_custom_call" | custom-call | flops 720896 | bytes 2162688 | tf_op jit(solution)/shard_map/pallas_call | solution.py:113
  140.9 2.7 %collective-permute-start.13 = (bf16[2,176,1024]{2,1,0:T(8,128)(2,1)}, bf16[2,176,1024]{2,1,0:T(8,128)(2,1)}, u32[]{:S(2)}, u32[]{:S(2)}) collective-permute-start(bf16[2,176,1024]{2,1,0:T(8,128)(2,1)} %shard_map.90), channel_id=1, source_target_pairs={{0,24},{1,9},{2,26},{3,11},{4,28},{5,13},{6,30},{7,15},{8,16},{9,1... | collective-permute-start | bytes 2162696 | tf_op jit(solution)/shard_map/ppermute | solution.py:160
  143.7 7.3 %shard_map.98 = f32[64,4096]{1,0:T(8,128)} custom-call(s32[192]{0:T(256)} %bitcast.12, bf16[352,1024]{1,0:T(8,128)(2,1)} %copy-done.1, bf16[352,1024]{1,0:T(8,128)(2,1)} %copy-done.4, bf16[352,1024]{1,0:T(8,128)(2,1)} %collective-permute-done.1.refs_0_.refs_2_, bf16[352,1024]{1,0:T(8,128)(2,1)} %collective-permute-done.3.refs_1_.refs_3_, ...), custom_call_target="tpu_custom_call" | custom-call | flops 536870912 | bytes 8388608 | tf_op jit(solution)/shard_map/pallas_call | solution.py:226
  151.0 1.4 shard_map.94
  152.4 3.1 %collective-permute-start.19 = (bf16[2,160,1024]{2,1,0:T(8,128)(2,1)S(1)}, bf16[2,160,1024]{2,1,0:T(8,128)(2,1)S(1)}, u32[]{:S(2)}, u32[]{:S(2)}) collective-permute-start(bf16[2,160,1024]{2,1,0:T(8,128)(2,1)S(1)} %shard_map.94), channel_id=1, source_target_pairs={{0,96},{1,33},{2,98},{3,35},{4,100},{5,37},{6,102},{7,39},{8,104},... | collective-permute-start | bytes 1966088 | tf_op jit(solution)/shard_map/ppermute | solution.py:160
  155.5 1.3 shard_map.93
  157.4 1.3 shard_map.91
  159.1 5.2 %collective-permute-done.19.refs_2_.refs_10_ = bf16[2,160,1024]{2,1,0:T(8,128)(2,1)S(1)} collective-permute-done((bf16[2,160,1024]{2,1,0:T(8,128)(2,1)S(1)}, bf16[2,160,1024]{2,1,0:T(8,128)(2,1)S(1)}, u32[]{:S(2)}, u32[]{:S(2)}) %collective-permute-start.19) | collective-permute-done | bytes 655392 | tf_op jit(solution)/shard_map/ppermute | solution.py:160
  164.3 1.2 shard_map.95
  165.5 0.9 collective-permute-start.20
  166.4 7.4 %collective-permute-done.20.refs_11_ = bf16[1,160,1024]{2,1,0:T(8,128)(2,1)S(1)} collective-permute-done((bf16[1,160,1024]{2,1,0:T(8,128)(2,1)S(1)}, bf16[1,160,1024]{2,1,0:T(8,128)(2,1)S(1)}, u32[]{:S(2)}, u32[]{:S(2)}) %collective-permute-start.20) | collective-permute-done | bytes 327712 | tf_op jit(solution)/shard_map/ppermute | solution.py:160
  173.9 2.9 %shard_map.96 = bf16[512,1024]{1,0:T(8,128)(2,1)} custom-call(bf16[4,176,1024]{2,1,0:T(8,128)(2,1)} %get-tuple-element.18.refs_0_, bf16[4,176,1024]{2,1,0:T(8,128)(2,1)} %collective-permute-done.12.refs_1_, bf16[2,176,1024]{2,1,0:T(8,128)(2,1)} %collective-permute-done.13.refs_2_, bf16[1,176,1024]{2,1,0:T(8,128)(2,1)S(1)} %collective-permute-done.14.refs_3_, ...), custom_call_target="tpu_custom_call" | custom-call | flops 2097152 | bytes 5242880 | tf_op jit(solution)/shard_map/pallas_call | solution.py:141
  176.8 3.7 %all-to-all-start.2 = ((bf16[8,64,1024]{2,1,0:T(8,128)(2,1)}), bf16[8,64,1024]{2,1,0:T(8,128)(2,1)S(1)}, u32[]{:S(2)}, u32[]{:S(2)}) async-start(bf16[8,64,1024]{2,1,0:T(8,128)(2,1)} %bitcast.6), calls=%async_computation.2 | async-start | bytes 2097152 | tf_op jit(solution)/shard_map/all_to_all | solution.py:82
  180.5 2.3 %add_multiply_fusion.1 = f32[64,4096]{1,0:T(8,128)} fusion(f32[64,4096]{1,0:T(8,128)S(1)} %copy-done.7, f32[64,4096]{1,0:T(8,128)} %collective-permute-done.22), kind=kLoop, calls=%fused_computation.1 | loop fusion | flops 524288 | bytes 3145728 | tf_op jit(solution)/shard_map/div | solution.py:536
  182.8 3.3 %fusion = f32[512,1024]{1,0:T(8,128)S(1)} fusion(bf16[1024,1024]{1,0:T(8,128)(2,1)} %collective-permute-done.21, s32[]{:T(128)S(6)} %select_n.9), kind=kOutput, calls=%fused_computation.2 | convolution fusion | flops 1073741824 | bytes 5242884 | tf_op jit(solution)/shard_map/dot_general | solution.py:533
  186.2 2.6 %add_multiply_fusion = f32[512,1024]{1,0:T(8,128)} fusion(f32[512,1024]{1,0:T(8,128)S(1)} %fusion, bf16[1024,1024]{1,0:T(8,128)(2,1)S(1)} %copy-done.9, s32[]{:T(128)S(6)} %select_n.9), kind=kOutput, calls=%fused_computation | convolution fusion | flops 1074790400 | bytes 7340036 | tf_op jit(solution)/shard_map/dot_general | solution.py:533
  188.8 2.9 %all-to-all-done.2.pieces = bf16[8,64,1024]{2,1,0:T(8,128)(2,1)S(1)} async-done(((bf16[8,64,1024]{2,1,0:T(8,128)(2,1)}), bf16[8,64,1024]{2,1,0:T(8,128)(2,1)S(1)}, u32[]{:S(2)}, u32[]{:S(2)}) %all-to-all-start.2) | async-done | bytes 1048608 | tf_op jit(solution)/shard_map/all_to_all | solution.py:82
  (49 shorter events, 3.0 us)
Async XLA Ops:
  17.9 9.4 %collective-permute-start.4 = (bf16[176,1024]{1,0:T(8,128)(2,1)S(1)}, bf16[176,1024]{1,0:T(8,128)(2,1)S(1)}, u32[]{:S(2)}, u32[]{:S(2)}) collective-permute-start(bf16[176,1024]{1,0:T(8,128)(2,1)S(1)} %get-tuple-element.24), channel_id=1, source_target_pairs={{0,24},{1,9},{2,26},{3,11},{4,28},{5,13},{6,30},{7,15},{8,16},{9,1... | collective-permute-start | bytes 1081352 | tf_op jit(solution)/shard_map/ppermute | solution.py:91
  20.3 8.6 %collective-permute-start = (bf16[176,1024]{1,0:T(8,128)(2,1)S(1)}, bf16[176,1024]{1,0:T(8,128)(2,1)S(1)}, u32[]{:S(2)}, u32[]{:S(2)}) collective-permute-start(bf16[176,1024]{1,0:T(8,128)(2,1)S(1)} %get-tuple-element.25), channel_id=1, source_target_pairs={{0,96},{1,33},{2,98},{3,35},{4,100},{5,37},{6,102},{7,39},{8,104},... | collective-permute-start | bytes 1081352 | tf_op jit(solution)/shard_map/ppermute | solution.py:91
  22.7 8.7 %collective-permute-start.8 = (bf16[160,1024]{1,0:T(8,128)(2,1)S(1)}, bf16[160,1024]{1,0:T(8,128)(2,1)S(1)}, u32[]{:S(2)}, u32[]{:S(2)}) collective-permute-start(bf16[160,1024]{1,0:T(8,128)(2,1)S(1)} %slice.14), channel_id=1, source_target_pairs={{0,6},{1,3},{2,4},{3,1},{4,2},{5,7},{6,0},{7,5},{8,14},{9,11},{10,... | collective-permute-start | bytes 983048 | tf_op jit(solution)/shard_map/ppermute | solution.py:91
  27.4 39.1 %copy-start = (bf16[352,1024]{1,0:T(8,128)(2,1)}, bf16[352,1024]{1,0:T(8,128)(2,1)S(1)}, u32[]{:S(2)}) copy-start(bf16[352,1024]{1,0:T(8,128)(2,1)S(1)} %pad_maximum_fusion.1.refs_2_.refs_4_) | copy-start | bytes 2162692
  27.4 23.7 %collective-permute-start.6 = (bf16[352,1024]{1,0:T(8,128)(2,1)S(1)}, bf16[352,1024]{1,0:T(8,128)(2,1)S(1)}, u32[]{:S(2)}, u32[]{:S(2)}) collective-permute-start(bf16[352,1024]{1,0:T(8,128)(2,1)S(1)} %pad_maximum_fusion.1.refs_2_.refs_4_), channel_id=1, source_target_pairs={{0,6},{1,3},{2,4},{3,1},{4,2},{5,7},{6,0},{7,5},{8,14},{9,11},{10,... | collective-permute-start | bytes 2162696 | tf_op jit(solution)/shard_map/ppermute | solution.py:91
  29.0 37.5 %copy-start.1 = (bf16[352,1024]{1,0:T(8,128)(2,1)}, bf16[352,1024]{1,0:T(8,128)(2,1)S(1)}, u32[]{:S(2)}) copy-start(bf16[352,1024]{1,0:T(8,128)(2,1)S(1)} %pad_maximum_fusion.refs_0_) | copy-start | bytes 2162692
  29.0 24.0 %collective-permute-start.2 = (bf16[352,1024]{1,0:T(8,128)(2,1)S(1)}, bf16[352,1024]{1,0:T(8,128)(2,1)S(1)}, u32[]{:S(2)}, u32[]{:S(2)}) collective-permute-start(bf16[352,1024]{1,0:T(8,128)(2,1)S(1)} %pad_maximum_fusion.refs_0_), channel_id=1, source_target_pairs={{0,24},{1,9},{2,26},{3,11},{4,28},{5,13},{6,30},{7,15},{8,16},{9,1... | collective-permute-start | bytes 2162696 | tf_op jit(solution)/shard_map/ppermute | solution.py:91
  31.5 35.0 %copy-start.2 = (bf16[320,1024]{1,0:T(8,128)(2,1)}, bf16[320,1024]{1,0:T(8,128)(2,1)S(1)}, u32[]{:S(2)}) copy-start(bf16[320,1024]{1,0:T(8,128)(2,1)S(1)} %pad_maximum_fusion.2.refs_4_.refs_8_) | copy-start | bytes 1966084
  31.5 12.0 %collective-permute-start.10 = (bf16[320,1024]{1,0:T(8,128)(2,1)S(1)}, bf16[320,1024]{1,0:T(8,128)(2,1)}, u32[]{:S(2)}, u32[]{:S(2)}) collective-permute-start(bf16[320,1024]{1,0:T(8,128)(2,1)S(1)} %pad_maximum_fusion.2.refs_4_.refs_8_), channel_id=1, source_target_pairs={{0,96},{1,33},{2,98},{3,35},{4,100},{5,37},{6,102},{7,39},{8,104},... | collective-permute-start | bytes 1966088 | tf_op jit(solution)/shard_map/ppermute | solution.py:91
  33.6 15.2 %collective-permute-start.9 = (bf16[320,1024]{1,0:T(8,128)(2,1)S(1)}, bf16[320,1024]{1,0:T(8,128)(2,1)}, u32[]{:S(2)}, u32[]{:S(2)}) collective-permute-start(bf16[320,1024]{1,0:T(8,128)(2,1)S(1)} %pad_maximum_fusion.2.refs_4_.refs_8_), channel_id=1, source_target_pairs={{0,24},{1,9},{2,26},{3,11},{4,28},{5,13},{6,30},{7,15},{8,16},{9,1... | collective-permute-start | bytes 1966088 | tf_op jit(solution)/shard_map/ppermute | solution.py:91
  35.6 55.7 %copy-start.5 = (s32[1,192]{1,0:T(1,128)}, s32[1,192]{1,0:T(1,128)S(1)}, u32[]{:S(2)}) copy-start(s32[1,192]{1,0:T(1,128)S(1)} %constant_dynamic-slice_fusion) | copy-start | bytes 2308
  35.6 39.6 %collective-permute-start.5 = (bf16[352,1024]{1,0:T(8,128)(2,1)S(1)}, bf16[352,1024]{1,0:T(8,128)(2,1)}, u32[]{:S(2)}, u32[]{:S(2)}) collective-permute-start(bf16[352,1024]{1,0:T(8,128)(2,1)S(1)} %pad_maximum_fusion.1.refs_2_.refs_4_), channel_id=1, source_target_pairs={{0,96},{1,33},{2,98},{3,35},{4,100},{5,37},{6,102},{7,39},{8,104},... | collective-permute-start | bytes 2162696 | tf_op jit(solution)/shard_map/ppermute | solution.py:91
  43.5 31.7 %collective-permute-start.1 = (bf16[352,1024]{1,0:T(8,128)(2,1)S(1)}, bf16[352,1024]{1,0:T(8,128)(2,1)}, u32[]{:S(2)}, u32[]{:S(2)}) collective-permute-start(bf16[352,1024]{1,0:T(8,128)(2,1)S(1)} %pad_maximum_fusion.refs_0_), channel_id=1, source_target_pairs={{0,6},{1,3},{2,4},{3,1},{4,2},{5,7},{6,0},{7,5},{8,14},{9,11},{10,... | collective-permute-start | bytes 2162696 | tf_op jit(solution)/shard_map/ppermute | solution.py:91
  48.8 26.5 %collective-permute-start.11 = (bf16[320,1024]{1,0:T(8,128)(2,1)}, bf16[320,1024]{1,0:T(8,128)(2,1)}, u32[]{:S(2)}, u32[]{:S(2)}) collective-permute-start(bf16[320,1024]{1,0:T(8,128)(2,1)} %collective-permute-done.10.refs_5_.refs_9_), channel_id=1, source_target_pairs={{0,24},{1,9},{2,26},{3,11},{4,28},{5,13},{6,30},{7,15},{8,16},{9,1... | collective-permute-start | bytes 1966088 | tf_op jit(solution)/shard_map/ppermute | solution.py:91
  51.1 15.4 %copy-start.3 = (bf16[352,1024]{1,0:T(8,128)(2,1)}, bf16[352,1024]{1,0:T(8,128)(2,1)S(1)}, u32[]{:S(2)}) copy-start(bf16[352,1024]{1,0:T(8,128)(2,1)S(1)} %collective-permute-done.6.refs_3_.refs_5_) | copy-start | bytes 2162692
  51.1 24.1 %collective-permute-start.7 = (bf16[352,1024]{1,0:T(8,128)(2,1)S(1)}, bf16[352,1024]{1,0:T(8,128)(2,1)}, u32[]{:S(2)}, u32[]{:S(2)}) collective-permute-start(bf16[352,1024]{1,0:T(8,128)(2,1)S(1)} %collective-permute-done.6.refs_3_.refs_5_), channel_id=1, source_target_pairs={{0,96},{1,33},{2,98},{3,35},{4,100},{5,37},{6,102},{7,39},{8,104},... | collective-permute-start | bytes 2162696 | tf_op jit(solution)/shard_map/ppermute | solution.py:91
  53.1 13.4 %copy-start.4 = (bf16[352,1024]{1,0:T(8,128)(2,1)}, bf16[352,1024]{1,0:T(8,128)(2,1)S(1)}, u32[]{:S(2)}) copy-start(bf16[352,1024]{1,0:T(8,128)(2,1)S(1)} %collective-permute-done.2.refs_1_) | copy-start | bytes 2162692
  53.1 22.2 %collective-permute-start.3 = (bf16[352,1024]{1,0:T(8,128)(2,1)S(1)}, bf16[352,1024]{1,0:T(8,128)(2,1)}, u32[]{:S(2)}, u32[]{:S(2)}) collective-permute-start(bf16[352,1024]{1,0:T(8,128)(2,1)S(1)} %collective-permute-done.2.refs_1_), channel_id=1, source_target_pairs={{0,6},{1,3},{2,4},{3,1},{4,2},{5,7},{6,0},{7,5},{8,14},{9,11},{10,... | collective-permute-start | bytes 2162696 | tf_op jit(solution)/shard_map/ppermute | solution.py:91
  54.5 12.0 %copy-start.8 = (s32[1024]{0:T(1024)S(1)}, s32[1024]{0:T(1024)}, u32[]{:S(2)}) copy-start(s32[1024]{0:T(1024)} %param.7) | copy-start | bytes 12292
  66.5 8.7 %copy-start.6 = (s32[1024]{0:T(1024)}, s32[1024]{0:T(1024)S(1)}, u32[]{:S(2)}) copy-start(s32[1024]{0:T(1024)S(1)} %broadcast_subtract_fusion) | copy-start | bytes 12292
  85.7 17.4 %all-to-all-start.1 = ((f32[64,16,128]{2,1,0:T(8,128)}), f32[64,16,128]{2,1,0:T(8,128)}, u32[]{:S(2)}, u32[]{:S(2)}) async-start(f32[64,16,128]{2,1,0:T(8,128)} %get-tuple-element.14), calls=%async_computation.1 | async-start | bytes 1048576 | tf_op jit(solution)/shard_map/all_to_all | solution.py:522
  114.6 20.5 %collective-permute-start.15 = (bf16[4,176,1024]{2,1,0:T(8,128)(2,1)}, bf16[4,176,1024]{2,1,0:T(8,128)(2,1)}, u32[]{:S(2)}, u32[]{:S(2)}) collective-permute-start(bf16[4,176,1024]{2,1,0:T(8,128)(2,1)} %get-tuple-element.21), channel_id=1, source_target_pairs={{0,96},{1,33},{2,98},{3,35},{4,100},{5,37},{6,102},{7,39},{8,104},... | collective-permute-start | bytes 4325384 | tf_op jit(solution)/shard_map/ppermute | solution.py:160
  116.4 22.4 %collective-permute-start.12 = (bf16[4,176,1024]{2,1,0:T(8,128)(2,1)}, bf16[4,176,1024]{2,1,0:T(8,128)(2,1)}, u32[]{:S(2)}, u32[]{:S(2)}) collective-permute-start(bf16[4,176,1024]{2,1,0:T(8,128)(2,1)} %get-tuple-element.19), channel_id=1, source_target_pairs={{0,6},{1,3},{2,4},{3,1},{4,2},{5,7},{6,0},{7,5},{8,14},{9,11},{10,... | collective-permute-start | bytes 4325384 | tf_op jit(solution)/shard_map/ppermute | solution.py:160
  119.1 31.9 %collective-permute-start.18 = (bf16[4,160,1024]{2,1,0:T(8,128)(2,1)}, bf16[4,160,1024]{2,1,0:T(8,128)(2,1)}, u32[]{:S(2)}, u32[]{:S(2)}) collective-permute-start(bf16[4,160,1024]{2,1,0:T(8,128)(2,1)} %get-tuple-element.23), channel_id=1, source_target_pairs={{0,24},{1,9},{2,26},{3,11},{4,28},{5,13},{6,30},{7,15},{8,16},{9,1... | collective-permute-start | bytes 3932168 | tf_op jit(solution)/shard_map/ppermute | solution.py:160
  121.8 61.0 %collective-permute-start.21 = (bf16[1024,1024]{1,0:T(8,128)(2,1)}, bf16[1024,1024]{1,0:T(8,128)(2,1)}, u32[]{:S(2)}, u32[]{:S(2)}) collective-permute-start(bf16[1024,1024]{1,0:T(8,128)(2,1)} %get-tuple-element.17.grad), channel_id=1, source_target_pairs={{0,1},{1,0},{2,3},{3,2},{4,5},{5,4},{6,7},{7,6},{8,9},{9,8},{10,11... | collective-permute-start | bytes 6291464 | tf_op jit(solution)/shard_map/ppermute | solution.py:535
  137.3 18.2 %collective-permute-start.16 = (bf16[2,176,1024]{2,1,0:T(8,128)(2,1)}, bf16[2,176,1024]{2,1,0:T(8,128)(2,1)}, u32[]{:S(2)}, u32[]{:S(2)}) collective-permute-start(bf16[2,176,1024]{2,1,0:T(8,128)(2,1)} %shard_map.92), channel_id=1, source_target_pairs={{0,6},{1,3},{2,4},{3,1},{4,2},{5,7},{6,0},{7,5},{8,14},{9,11},{10,... | collective-permute-start | bytes 2162696 | tf_op jit(solution)/shard_map/ppermute | solution.py:160
  140.9 16.5 %collective-permute-start.13 = (bf16[2,176,1024]{2,1,0:T(8,128)(2,1)}, bf16[2,176,1024]{2,1,0:T(8,128)(2,1)}, u32[]{:S(2)}, u32[]{:S(2)}) collective-permute-start(bf16[2,176,1024]{2,1,0:T(8,128)(2,1)} %shard_map.90), channel_id=1, source_target_pairs={{0,24},{1,9},{2,26},{3,11},{4,28},{5,13},{6,30},{7,15},{8,16},{9,1... | collective-permute-start | bytes 2162696 | tf_op jit(solution)/shard_map/ppermute | solution.py:160
  150.9 29.6 %collective-permute-start.22 = (f32[64,4096]{1,0:T(8,128)}, f32[64,4096]{1,0:T(8,128)}, u32[]{:S(2)}, u32[]{:S(2)}) collective-permute-start(f32[64,4096]{1,0:T(8,128)} %shard_map.98), channel_id=1, source_target_pairs={{0,1},{1,0},{2,3},{3,2},{4,5},{5,4},{6,7},{7,6},{8,9},{9,8},{10,11... | collective-permute-start | bytes 3145736 | tf_op jit(solution)/shard_map/ppermute | solution.py:536
  152.4 11.9 %collective-permute-start.19 = (bf16[2,160,1024]{2,1,0:T(8,128)(2,1)S(1)}, bf16[2,160,1024]{2,1,0:T(8,128)(2,1)S(1)}, u32[]{:S(2)}, u32[]{:S(2)}) collective-permute-start(bf16[2,160,1024]{2,1,0:T(8,128)(2,1)S(1)} %shard_map.94), channel_id=1, source_target_pairs={{0,96},{1,33},{2,98},{3,35},{4,100},{5,37},{6,102},{7,39},{8,104},... | collective-permute-start | bytes 1966088 | tf_op jit(solution)/shard_map/ppermute | solution.py:160
  156.8 17.0 %collective-permute-start.17 = (bf16[1,176,1024]{2,1,0:T(8,128)(2,1)S(1)}, bf16[1,176,1024]{2,1,0:T(8,128)(2,1)S(1)}, u32[]{:S(2)}, u32[]{:S(2)}) collective-permute-start(bf16[1,176,1024]{2,1,0:T(8,128)(2,1)S(1)} %shard_map.93), channel_id=1, source_target_pairs={{0,24},{1,9},{2,26},{3,11},{4,28},{5,13},{6,30},{7,15},{8,16},{9,1... | collective-permute-start | bytes 1081352 | tf_op jit(solution)/shard_map/ppermute | solution.py:160
  158.7 15.1 %collective-permute-start.14 = (bf16[1,176,1024]{2,1,0:T(8,128)(2,1)S(1)}, bf16[1,176,1024]{2,1,0:T(8,128)(2,1)S(1)}, u32[]{:S(2)}, u32[]{:S(2)}) collective-permute-start(bf16[1,176,1024]{2,1,0:T(8,128)(2,1)S(1)} %shard_map.91), channel_id=1, source_target_pairs={{0,96},{1,33},{2,98},{3,35},{4,100},{5,37},{6,102},{7,39},{8,104},... | collective-permute-start | bytes 1081352 | tf_op jit(solution)/shard_map/ppermute | solution.py:160
  165.5 8.4 %collective-permute-start.20 = (bf16[1,160,1024]{2,1,0:T(8,128)(2,1)S(1)}, bf16[1,160,1024]{2,1,0:T(8,128)(2,1)S(1)}, u32[]{:S(2)}, u32[]{:S(2)}) collective-permute-start(bf16[1,160,1024]{2,1,0:T(8,128)(2,1)S(1)} %shard_map.95), channel_id=1, source_target_pairs={{0,6},{1,3},{2,4},{3,1},{4,2},{5,7},{6,0},{7,5},{8,14},{9,11},{10,... | collective-permute-start | bytes 983048 | tf_op jit(solution)/shard_map/ppermute | solution.py:160
  176.8 3.7 %copy-start.7 = (f32[64,4096]{1,0:T(8,128)S(1)}, f32[64,4096]{1,0:T(8,128)}, u32[]{:S(2)}) copy-start(f32[64,4096]{1,0:T(8,128)} %shard_map.98) | copy-start | bytes 3145732
  176.8 14.9 %all-to-all-start.2 = ((bf16[8,64,1024]{2,1,0:T(8,128)(2,1)}), bf16[8,64,1024]{2,1,0:T(8,128)(2,1)S(1)}, u32[]{:S(2)}, u32[]{:S(2)}) async-start(bf16[8,64,1024]{2,1,0:T(8,128)(2,1)} %bitcast.6), calls=%async_computation.2 | async-start | bytes 2097152 | tf_op jit(solution)/shard_map/all_to_all | solution.py:82
  182.8 3.4 %copy-start.9 = (bf16[1024,1024]{1,0:T(8,128)(2,1)S(1)}, bf16[1024,1024]{1,0:T(8,128)(2,1)}, u32[]{:S(2)}) copy-start(bf16[1024,1024]{1,0:T(8,128)(2,1)} %get-tuple-element.17.grad) | copy-start | bytes 6291460

commit v7 on v6

--- a/solution.py
+++ b/solution.py
@@ -126,33 +126,40 @@
     )(*[in_hbm(x) if x.shape[0] == 4 else x for x, _ in terms])
 
 
-def last_kernel(*refs):
+def early_sum_kernel(*refs):
     *terms, out = refs
     for g in range(3):
-        total = terms[4 * g][...].astype(F32)
-        for term in terms[4 * g + 1 : 4 * g + 4]:
+        total = terms[3 * g][...].astype(F32)
+        for term in terms[3 * g + 1 : 3 * g + 3]:
             total = total + term[...].astype(F32)
-        out[STARTS[g] : STARTS[g] + SIZES[g]] = total.astype(BF16)
-
-
-def add_last(terms):
+        out[STARTS[g] : STARTS[g] + SIZES[g]] = total
+
+
+def last_sum_kernel(*refs):
+    *terms, early, out = refs
+    for g in range(3):
+        here = slice(STARTS[g], STARTS[g] + SIZES[g])
+        out[here] = (early[here] + terms[g][...].astype(F32)).astype(BF16)
+
+
+def stacked_sum(kernel, terms, kind, *more):
     tokens = terms[0].shape[2]
     part = tokens // 2
-    return pl.pallas_call(
-        last_kernel,
+    rows = pl.BlockSpec((sum(SIZES), part), lambda i: (0, i))
+    return pl.pallas_call(
+        kernel,
         grid=(2,),
-        in_specs=[
-            pl.BlockSpec((None, x.shape[1], part), lambda i: (0, 0, i)) for x in terms
-        ],
-        out_specs=pl.BlockSpec((sum(SIZES), part), lambda i: (0, i)),
-        out_shape=jax.ShapeDtypeStruct((sum(SIZES), tokens), BF16),
+        in_specs=[pl.BlockSpec((None, x.shape[1], part), lambda i: (0, 0, i)) for x in terms]
+        + [rows] * len(more),
+        out_specs=rows,
+        out_shape=jax.ShapeDtypeStruct((sum(SIZES), tokens), kind),
         compiler_params=pltpu.CompilerParams(
             dimension_semantics=("arbitrary",), vmem_limit_bytes=16 << 20
         ),
         cost_estimate=pl.CostEstimate(
             flops=4 * sum(SIZES) * tokens, bytes_accessed=10 * sum(SIZES) * tokens, transcendentals=0
         ),
-    )(*[in_hbm(x) if x.shape[0] == 4 else x for x in terms])
+    )(*[in_hbm(x) if x.shape[0] == 4 else x for x in terms], *more)
 
 
 def summed_groups(sends, keeps):
@@ -164,7 +171,10 @@
     near = [
         trade(add_up(1, (keeps[g], 1), (far[g], 1), (mid[g], 1)), g, 0) for g in range(3)
     ]
-    return add_last([x for g in range(3) for x in (keeps[g], far[g], mid[g], near[g])])
+    early = stacked_sum(
+        early_sum_kernel, [x for g in range(3) for x in (keeps[g], far[g], mid[g])], F32
+    )
+    return stacked_sum(last_sum_kernel, near, BF16, early)
 
 
 def sum_kernel(pieces, out):
@@ -376,7 +386,7 @@
         stats[...] = jnp.broadcast_to(jnp.concatenate(both, axis=0)[None], stats.shape)
 
 
-LOGIT_ROWS = 256
+LOGIT_ROWS = 512
 
 
 def half_logits(half, got, wide, part=None, tgt=None):

time: 194 us -> 193 us (level)
  waiting for transfers between devices: 35.5 us -> 33.3 us
    ppermute x9, waiting for transfers between devices: 17.8 us -> 15.7 us  [trade(): return lax.ppermute(x, ALL, LARGE_PAIRS[(g + step) % 3])]
where the time goes in v7:
time: 193 us; the launch traced here: 191 us
  Pallas kernels  82.9 us (43%)
  starting transfers between devices  47.8 us (25%)
  waiting for transfers between devices  33.3 us (17%)
  blocking collectives  16.2 us (8%)
  matrix products  5.95 us (3%)
  other arithmetic  2.44 us (1%)
    ppermute x12, starting transfers between devices, get(): return lax.ppermute(x, ALL, LARGE_PAIRS[(g + step) % 3])  21.9 us
    pallas_call x2, Pallas kernels, half_logits(): pl.pallas_call(late_kernel if late else early_kernel, grid=(vocab_rows //...  19.5 us
    ppermute x9, starting transfers between devices, trade(): return lax.ppermute(x, ALL, LARGE_PAIRS[(g + step) % 3])  16.4 us
    all_to_all x1, blocking collectives, small_stage(): lax.all_to_all(x, ALL, 0, 0, axis_index_groups=SMALL_CUBES, tiled=True)  16.2 us
    ppermute x9, waiting for transfers between devices, trade(): return lax.ppermute(x, ALL, LARGE_PAIRS[(g + step) % 3])  15.7 us
    ppermute x12, waiting for transfers between devices, get(): return lax.ppermute(x, ALL, LARGE_PAIRS[(g + step) % 3])  13.8 us
    pallas_call x1, Pallas kernels, columns_turned(): pl.pallas_call(columns_kernel, grid_spec=pltpu.PrefetchScalarGridSpec(num...  12 us
    pallas_call x1, Pallas kernels, signal_of(): pl.pallas_call(signal_kernel, grid=(count + 4,), in_specs=[whole(*stats.s...  11.4 us
  transfers between devices with their start and end apart: 25, of which 9 were waited for; matrix products, arithmetic and copies ran while one was open for 5% of the time, Pallas kernels for 31%

profile of v7, /device:TPU:0, one launch (start us, length us, event | category | flops | bytes accessed | tf_op | source)
XLA Modules:
  0.0 191.3 jit_solution(1844520046620578816)
XLA Ops:
  0.6 1.0 broadcast_in_dim.12
  1.7 16.2 %all_to_all.15 = bf16[8,64,1024]{2,1,0:T(8,128)(2,1)S(1)} all-to-all(bf16[8,64,1024]{2,1,0:T(8,128)(2,1)S(1)} %broadcast_in_dim.12), channel_id=1, replica_groups={{0,2,8,10,32,34,40,42},{4,6,12,14,36,38,44,46},{16,18,24,26,48,50,56,58..., dimensions={0} | all-to-all | bytes 2097152 | tf_op jit(solution)/shard_map/all_to_all | solution.py:82
  17.9 2.4 %collective-permute-start.4 = (bf16[176,1024]{1,0:T(8,128)(2,1)S(1)}, bf16[176,1024]{1,0:T(8,128)(2,1)S(1)}, u32[]{:S(2)}, u32[]{:S(2)}) collective-permute-start(bf16[176,1024]{1,0:T(8,128)(2,1)S(1)} %get-tuple-element.24), channel_id=1, source_target_pairs={{0,24},{1,9},{2,26},{3,11},{4,28},{5,13},{6,30},{7,15},{8,16},{9,1... | collective-permute-start | bytes 1081352 | tf_op jit(solution)/shard_map/ppermute | solution.py:91
  20.3 2.4 %collective-permute-start = (bf16[176,1024]{1,0:T(8,128)(2,1)S(1)}, bf16[176,1024]{1,0:T(8,128)(2,1)S(1)}, u32[]{:S(2)}, u32[]{:S(2)}) collective-permute-start(bf16[176,1024]{1,0:T(8,128)(2,1)S(1)} %get-tuple-element.25), channel_id=1, source_target_pairs={{0,96},{1,33},{2,98},{3,35},{4,100},{5,37},{6,102},{7,39},{8,104},... | collective-permute-start | bytes 1081352 | tf_op jit(solution)/shard_map/ppermute | solution.py:91
  22.7 1.9 collective-permute-start.8
  24.6 2.7 %collective-permute-done.4 = bf16[176,1024]{1,0:T(8,128)(2,1)S(1)} collective-permute-done((bf16[176,1024]{1,0:T(8,128)(2,1)S(1)}, bf16[176,1024]{1,0:T(8,128)(2,1)S(1)}, u32[]{:S(2)}, u32[]{:S(2)}) %collective-permute-start.4) | collective-permute-done | bytes 360480 | tf_op jit(solution)/shard_map/ppermute | solution.py:91
  27.4 1.4 collective-permute-start.6
  29.0 2.4 %collective-permute-start.2 = (bf16[352,1024]{1,0:T(8,128)(2,1)S(1)}, bf16[352,1024]{1,0:T(8,128)(2,1)S(1)}, u32[]{:S(2)}, u32[]{:S(2)}) collective-permute-start(bf16[352,1024]{1,0:T(8,128)(2,1)S(1)} %pad_maximum_fusion.refs_0_), channel_id=1, source_target_pairs={{0,24},{1,9},{2,26},{3,11},{4,28},{5,13},{6,30},{7,15},{8,16},{9,1... | collective-permute-start | bytes 2162696 | tf_op jit(solution)/shard_map/ppermute | solution.py:91
  31.5 2.1 %collective-permute-start.10 = (bf16[320,1024]{1,0:T(8,128)(2,1)S(1)}, bf16[320,1024]{1,0:T(8,128)(2,1)}, u32[]{:S(2)}, u32[]{:S(2)}) collective-permute-start(bf16[320,1024]{1,0:T(8,128)(2,1)S(1)} %pad_maximum_fusion.2.refs_4_.refs_8_), channel_id=1, source_target_pairs={{0,96},{1,33},{2,98},{3,35},{4,100},{5,37},{6,102},{7,39},{8,104},... | collective-permute-start | bytes 1966088 | tf_op jit(solution)/shard_map/ppermute | solution.py:91
  33.6 1.3 collective-permute-start.9
  36.4 7.1 %collective-permute-done.10.refs_5_.refs_9_ = bf16[320,1024]{1,0:T(8,128)(2,1)} collective-permute-done((bf16[320,1024]{1,0:T(8,128)(2,1)S(1)}, bf16[320,1024]{1,0:T(8,128)(2,1)}, u32[]{:S(2)}, u32[]{:S(2)}) %collective-permute-start.10) | collective-permute-done | bytes 655392 | tf_op jit(solution)/shard_map/ppermute | solution.py:91
  43.5 1.5 collective-permute-start.1
  45.0 3.8 %collective-permute-done.9.refs_4_.refs_10_ = bf16[320,1024]{1,0:T(8,128)(2,1)} collective-permute-done((bf16[320,1024]{1,0:T(8,128)(2,1)S(1)}, bf16[320,1024]{1,0:T(8,128)(2,1)}, u32[]{:S(2)}, u32[]{:S(2)}) %collective-permute-start.9) | collective-permute-done | bytes 655392 | tf_op jit(solution)/shard_map/ppermute | solution.py:91
  48.8 2.3 %collective-permute-start.11 = (bf16[320,1024]{1,0:T(8,128)(2,1)}, bf16[320,1024]{1,0:T(8,128)(2,1)}, u32[]{:S(2)}, u32[]{:S(2)}) collective-permute-start(bf16[320,1024]{1,0:T(8,128)(2,1)} %collective-permute-done.10.refs_5_.refs_9_), channel_id=1, source_target_pairs={{0,24},{1,9},{2,26},{3,11},{4,28},{5,13},{6,30},{7,15},{8,16},{9,1... | collective-permute-start | bytes 1966088 | tf_op jit(solution)/shard_map/ppermute | solution.py:91
  51.1 2.0 %collective-permute-start.7 = (bf16[352,1024]{1,0:T(8,128)(2,1)S(1)}, bf16[352,1024]{1,0:T(8,128)(2,1)}, u32[]{:S(2)}, u32[]{:S(2)}) collective-permute-start(bf16[352,1024]{1,0:T(8,128)(2,1)S(1)} %collective-permute-done.6.refs_3_.refs_5_), channel_id=1, source_target_pairs={{0,96},{1,33},{2,98},{3,35},{4,100},{5,37},{6,102},{7,39},{8,104},... | collective-permute-start | bytes 2162696 | tf_op jit(solution)/shard_map/ppermute | solution.py:91
  53.1 1.4 collective-permute-start.3
  54.5 12.0 %shard_map.84.refs_6_ = bf16[1024,4096]{1,0:T(8,128)(2,1)} custom-call(s32[192]{0:T(256)S(1)} %bitcast.10, bf16[1024,4096]{1,0:T(8,128)(2,1)} %w.3), custom_call_target="tpu_custom_call" | custom-call | flops 4294967296 | bytes 16777216 | tf_op jit(solution)/shard_map/pallas_call | solution.py:276
  66.6 8.6 %shard_map.85.refs_7_ = f32[1024,1024]{1,0:T(8,128)S(1)} custom-call(bf16[352,1024]{1,0:T(8,128)(2,1)S(1)} %pad_maximum_fusion.refs_0_, bf16[352,1024]{1,0:T(8,128)(2,1)S(1)} %collective-permute-done.2.refs_1_, bf16[352,1024]{1,0:T(8,128)(2,1)S(1)} %pad_maximum_fusion.1.refs_2_.refs_4_, bf16[352,1024]{1,0:T(8,128)(2,1)S(1)} %collective-permute-done.6.refs_3_.refs_5_, ...), custom_call_target="tpu_custom_call" | custom-call | flops 4294967296 | bytes 12582912 | tf_op jit(solution)/shard_map/pallas_call | solution.py:399
  75.3 10.8 %shard_map.86 = (f32[1024,1024]{1,0:T(8,128)}, f32[64,16,128]{2,1,0:T(8,128)}) custom-call(bf16[352,1024]{1,0:T(8,128)(2,1)} %collective-permute-done.1.refs_0_.refs_2_, bf16[352,1024]{1,0:T(8,128)(2,1)} %collective-permute-done.3.refs_1_.refs_3_, bf16[352,1024]{1,0:T(8,128)(2,1)} %collective-permute-done.5.refs_2_.refs_6_, ...), custom_call_target="tpu_custom_call" | custom-call | flops 4294967296 | bytes 12582912 | tf_op jit(solution)/shard_map/pallas_call | solution.py:399
  86.1 5.7 %all-to-all-start.1 = ((f32[64,16,128]{2,1,0:T(8,128)}), f32[64,16,128]{2,1,0:T(8,128)}, u32[]{:S(2)}, u32[]{:S(2)}) async-start(f32[64,16,128]{2,1,0:T(8,128)} %get-tuple-element.14), calls=%async_computation.1 | async-start | bytes 1048576 | tf_op jit(solution)/shard_map/all_to_all | solution.py:532
  91.8 10.7 %shard_map.87.tall = bf16[4096,1024]{1,0:T(8,128)(2,1)} custom-call(s32[192]{0:T(256)S(1)} %bitcast.11, bf16[1024,4096]{1,0:T(8,128)(2,1)} %w.3), custom_call_target="tpu_custom_call" | custom-call | flops 4294967296 | bytes 16777216 | tf_op jit(solution)/shard_map/pallas_call | solution.py:313
  102.5 1.0 all-to-all-done.1.stats
  103.5 11.4 %shard_map.88 = (bf16[1024,1024]{1,0:T(8,128)(2,1)}, f32[1,1024]{1,0:T(1,128)}, bf16[4,176,1024]{2,1,0:T(8,128)(2,1)}, bf16[4,176,1024]{2,1,0:T(8,128)(2,1)}, bf16[4,160,1024]{2,1,0:T(8,128)(2,1)}) custom-call(f32[64,16,128]{2,1,0:T(8,128)} %all-to-all-done.1.stats, f32[1024,1024]{1,0:T(8,128)} %get-tuple-element.15.logits, f32[1,1024]{1,0:T(1,128)} %bitcast.20, ...), custom_call_target="tpu_custom_call" | custom-call | flops 4294967296 | bytes 14680064 | tf_op jit(solution)/shard_map/pallas_call | solution.py:463
  114.9 1.8 collective-permute-start.15
  116.8 2.7 %collective-permute-start.12 = (bf16[4,176,1024]{2,1,0:T(8,128)(2,1)}, bf16[4,176,1024]{2,1,0:T(8,128)(2,1)}, u32[]{:S(2)}, u32[]{:S(2)}) collective-permute-start(bf16[4,176,1024]{2,1,0:T(8,128)(2,1)} %get-tuple-element.19), channel_id=1, source_target_pairs={{0,6},{1,3},{2,4},{3,1},{4,2},{5,7},{6,0},{7,5},{8,14},{9,11},{10,... | collective-permute-start | bytes 4325384 | tf_op jit(solution)/shard_map/ppermute | solution.py:167
  119.5 2.8 %collective-permute-start.18 = (bf16[4,160,1024]{2,1,0:T(8,128)(2,1)}, bf16[4,160,1024]{2,1,0:T(8,128)(2,1)}, u32[]{:S(2)}, u32[]{:S(2)}) collective-permute-start(bf16[4,160,1024]{2,1,0:T(8,128)(2,1)} %get-tuple-element.23), channel_id=1, source_target_pairs={{0,24},{1,9},{2,26},{3,11},{4,28},{5,13},{6,30},{7,15},{8,16},{9,1... | collective-permute-start | bytes 3932168 | tf_op jit(solution)/shard_map/ppermute | solution.py:167
  122.2 8.2 %shard_map.89 = (bf16[4,176,1024]{2,1,0:T(8,128)(2,1)}, bf16[4,176,1024]{2,1,0:T(8,128)(2,1)}, bf16[4,160,1024]{2,1,0:T(8,128)(2,1)}) custom-call(bf16[4096,1024]{1,0:T(8,128)(2,1)} %shard_map.87.tall, bf16[1024,1024]{1,0:T(8,128)(2,1)} %get-tuple-element.17.grad), custom_call_target="tpu_custom_call" | custom-call | flops 4294967296 | bytes 8388608 | tf_op jit(solution)/shard_map/pallas_call | solution.py:501
  130.4 5.1 %collective-permute-done.15.refs_1_.refs_4_ = bf16[4,176,1024]{2,1,0:T(8,128)(2,1)} collective-permute-done((bf16[4,176,1024]{2,1,0:T(8,128)(2,1)}, bf16[4,176,1024]{2,1,0:T(8,128)(2,1)}, u32[]{:S(2)}, u32[]{:S(2)}) %collective-permute-start.15) | collective-permute-done | bytes 1441824 | tf_op jit(solution)/shard_map/ppermute | solution.py:167
  135.5 2.1 %shard_map.92 = bf16[2,176,1024]{2,1,0:T(8,128)(2,1)} custom-call(bf16[4,176,1024]{2,1,0:T(8,128)(2,1)} %get-tuple-element.20.refs_0_.refs_3_, bf16[4,176,1024]{2,1,0:T(8,128)(2,1)} %collective-permute-done.15.refs_1_.refs_4_), custom_call_target="tpu_custom_call" | custom-call | flops 720896 | bytes 2162688 | tf_op jit(solution)/shard_map/pallas_call | solution.py:113
  137.6 1.5 collective-permute-start.16
  139.1 2.1 %shard_map.90 = bf16[2,176,1024]{2,1,0:T(8,128)(2,1)} custom-call(bf16[4,176,1024]{2,1,0:T(8,128)(2,1)} %get-tuple-element.18.refs_0_, bf16[4,176,1024]{2,1,0:T(8,128)(2,1)} %collective-permute-done.12.refs_1_), custom_call_target="tpu_custom_call" | custom-call | flops 720896 | bytes 2162688 | tf_op jit(solution)/shard_map/pallas_call | solution.py:113
  141.3 2.7 %collective-permute-start.13 = (bf16[2,176,1024]{2,1,0:T(8,128)(2,1)}, bf16[2,176,1024]{2,1,0:T(8,128)(2,1)}, u32[]{:S(2)}, u32[]{:S(2)}) collective-permute-start(bf16[2,176,1024]{2,1,0:T(8,128)(2,1)} %shard_map.90), channel_id=1, source_target_pairs={{0,24},{1,9},{2,26},{3,11},{4,28},{5,13},{6,30},{7,15},{8,16},{9,1... | collective-permute-start | bytes 2162696 | tf_op jit(solution)/shard_map/ppermute | solution.py:167
  144.0 7.3 %shard_map.99 = f32[64,4096]{1,0:T(8,128)} custom-call(s32[192]{0:T(256)} %bitcast.12, bf16[352,1024]{1,0:T(8,128)(2,1)} %copy-done.1, bf16[352,1024]{1,0:T(8,128)(2,1)} %copy-done.4, bf16[352,1024]{1,0:T(8,128)(2,1)} %collective-permute-done.1.refs_0_.refs_2_, bf16[352,1024]{1,0:T(8,128)(2,1)} %collective-permute-done.3.refs_1_.refs_3_, ...), custom_call_target="tpu_custom_call" | custom-call | flops 536870912 | bytes 8388608 | tf_op jit(solution)/shard_map/pallas_call | solution.py:236
  151.4 1.4 shard_map.94
  152.8 3.1 %collective-permute-start.19 = (bf16[2,160,1024]{2,1,0:T(8,128)(2,1)S(1)}, bf16[2,160,1024]{2,1,0:T(8,128)(2,1)S(1)}, u32[]{:S(2)}, u32[]{:S(2)}) collective-permute-start(bf16[2,160,1024]{2,1,0:T(8,128)(2,1)S(1)} %shard_map.94), channel_id=1, source_target_pairs={{0,96},{1,33},{2,98},{3,35},{4,100},{5,37},{6,102},{7,39},{8,104},... | collective-permute-start | bytes 1966088 | tf_op jit(solution)/shard_map/ppermute | solution.py:167
  155.9 1.3 shard_map.93
  157.8 1.3 shard_map.91
  159.4 5.2 %collective-permute-done.19.refs_2_.refs_8_ = bf16[2,160,1024]{2,1,0:T(8,128)(2,1)S(1)} collective-permute-done((bf16[2,160,1024]{2,1,0:T(8,128)(2,1)S(1)}, bf16[2,160,1024]{2,1,0:T(8,128)(2,1)S(1)}, u32[]{:S(2)}, u32[]{:S(2)}) %collective-permute-start.19) | collective-permute-done | bytes 655392 | tf_op jit(solution)/shard_map/ppermute | solution.py:167
  164.7 1.2 shard_map.95
  165.9 0.9 collective-permute-start.20
  166.8 2.1 %shard_map.96.refs_3_ = f32[512,1024]{1,0:T(8,128)S(1)} custom-call(bf16[4,176,1024]{2,1,0:T(8,128)(2,1)} %get-tuple-element.18.refs_0_, bf16[4,176,1024]{2,1,0:T(8,128)(2,1)} %collective-permute-done.12.refs_1_, bf16[2,176,1024]{2,1,0:T(8,128)(2,1)} %collective-permute-done.13.refs_2_, bf16[4,176,1024]{2,1,0:T(8,128)(2,1)} %get-tuple-element.20.refs_0_.refs_3_, ...), custom_call_target="tpu_custom_call" | custom-call | flops 2097152 | bytes 5242880 | tf_op jit(solution)/shard_map/pallas_call | solution.py:149
  168.9 5.3 %collective-permute-done.20.refs_2_ = bf16[1,160,1024]{2,1,0:T(8,128)(2,1)S(1)} collective-permute-done((bf16[1,160,1024]{2,1,0:T(8,128)(2,1)S(1)}, bf16[1,160,1024]{2,1,0:T(8,128)(2,1)S(1)}, u32[]{:S(2)}, u32[]{:S(2)}) %collective-permute-start.20) | collective-permute-done | bytes 327712 | tf_op jit(solution)/shard_map/ppermute | solution.py:167
  174.2 1.3 shard_map.97
  175.6 3.7 %all-to-all-start.2 = ((bf16[8,64,1024]{2,1,0:T(8,128)(2,1)}), bf16[8,64,1024]{2,1,0:T(8,128)(2,1)S(1)}, u32[]{:S(2)}, u32[]{:S(2)}) async-start(bf16[8,64,1024]{2,1,0:T(8,128)(2,1)} %bitcast.6), calls=%async_computation.2 | async-start | bytes 2097152 | tf_op jit(solution)/shard_map/all_to_all | solution.py:82
  179.3 2.3 %add_multiply_fusion.1 = f32[64,4096]{1,0:T(8,128)} fusion(f32[64,4096]{1,0:T(8,128)S(1)} %copy-done.7, f32[64,4096]{1,0:T(8,128)} %collective-permute-done.22), kind=kLoop, calls=%fused_computation.1 | loop fusion | flops 524288 | bytes 3145728 | tf_op jit(solution)/shard_map/div | solution.py:546
  181.6 3.3 %fusion = f32[512,1024]{1,0:T(8,128)S(1)} fusion(bf16[1024,1024]{1,0:T(8,128)(2,1)} %collective-permute-done.21, s32[]{:T(128)S(6)} %select_n.9), kind=kOutput, calls=%fused_computation.2 | convolution fusion | flops 1073741824 | bytes 5242884 | tf_op jit(solution)/shard_map/dot_general | solution.py:543
  184.9 2.6 %add_multiply_fusion = f32[512,1024]{1,0:T(8,128)} fusion(f32[512,1024]{1,0:T(8,128)S(1)} %fusion, bf16[1024,1024]{1,0:T(8,128)(2,1)S(1)} %copy-done.9, s32[]{:T(128)S(6)} %select_n.9), kind=kOutput, calls=%fused_computation | convolution fusion | flops 1074790400 | bytes 7340036 | tf_op jit(solution)/shard_map/dot_general | solution.py:543
  187.6 2.9 %all-to-all-done.2.pieces = bf16[8,64,1024]{2,1,0:T(8,128)(2,1)S(1)} async-done(((bf16[8,64,1024]{2,1,0:T(8,128)(2,1)}), bf16[8,64,1024]{2,1,0:T(8,128)(2,1)S(1)}, u32[]{:S(2)}, u32[]{:S(2)}) %all-to-all-start.2) | async-done | bytes 1048608 | tf_op jit(solution)/shard_map/all_to_all | solution.py:82
  (50 shorter events, 3.9 us)
Async XLA Ops:
  17.9 9.4 %collective-permute-start.4 = (bf16[176,1024]{1,0:T(8,128)(2,1)S(1)}, bf16[176,1024]{1,0:T(8,128)(2,1)S(1)}, u32[]{:S(2)}, u32[]{:S(2)}) collective-permute-start(bf16[176,1024]{1,0:T(8,128)(2,1)S(1)} %get-tuple-element.24), channel_id=1, source_target_pairs={{0,24},{1,9},{2,26},{3,11},{4,28},{5,13},{6,30},{7,15},{8,16},{9,1... | collective-permute-start | bytes 1081352 | tf_op jit(solution)/shard_map/ppermute | solution.py:91
  20.3 8.6 %collective-permute-start = (bf16[176,1024]{1,0:T(8,128)(2,1)S(1)}, bf16[176,1024]{1,0:T(8,128)(2,1)S(1)}, u32[]{:S(2)}, u32[]{:S(2)}) collective-permute-start(bf16[176,1024]{1,0:T(8,128)(2,1)S(1)} %get-tuple-element.25), channel_id=1, source_target_pairs={{0,96},{1,33},{2,98},{3,35},{4,100},{5,37},{6,102},{7,39},{8,104},... | collective-permute-start | bytes 1081352 | tf_op jit(solution)/shard_map/ppermute | solution.py:91
  22.7 8.7 %collective-permute-start.8 = (bf16[160,1024]{1,0:T(8,128)(2,1)S(1)}, bf16[160,1024]{1,0:T(8,128)(2,1)S(1)}, u32[]{:S(2)}, u32[]{:S(2)}) collective-permute-start(bf16[160,1024]{1,0:T(8,128)(2,1)S(1)} %slice.14), channel_id=1, source_target_pairs={{0,6},{1,3},{2,4},{3,1},{4,2},{5,7},{6,0},{7,5},{8,14},{9,11},{10,... | collective-permute-start | bytes 983048 | tf_op jit(solution)/shard_map/ppermute | solution.py:91
  27.4 39.1 %copy-start = (bf16[352,1024]{1,0:T(8,128)(2,1)}, bf16[352,1024]{1,0:T(8,128)(2,1)S(1)}, u32[]{:S(2)}) copy-start(bf16[352,1024]{1,0:T(8,128)(2,1)S(1)} %pad_maximum_fusion.1.refs_2_.refs_4_) | copy-start | bytes 2162692
  27.4 23.7 %collective-permute-start.6 = (bf16[352,1024]{1,0:T(8,128)(2,1)S(1)}, bf16[352,1024]{1,0:T(8,128)(2,1)S(1)}, u32[]{:S(2)}, u32[]{:S(2)}) collective-permute-start(bf16[352,1024]{1,0:T(8,128)(2,1)S(1)} %pad_maximum_fusion.1.refs_2_.refs_4_), channel_id=1, source_target_pairs={{0,6},{1,3},{2,4},{3,1},{4,2},{5,7},{6,0},{7,5},{8,14},{9,11},{10,... | collective-permute-start | bytes 2162696 | tf_op jit(solution)/shard_map/ppermute | solution.py:91
  29.0 37.5 %copy-start.1 = (bf16[352,1024]{1,0:T(8,128)(2,1)}, bf16[352,1024]{1,0:T(8,128)(2,1)S(1)}, u32[]{:S(2)}) copy-start(bf16[352,1024]{1,0:T(8,128)(2,1)S(1)} %pad_maximum_fusion.refs_0_) | copy-start | bytes 2162692
  29.0 24.0 %collective-permute-start.2 = (bf16[352,1024]{1,0:T(8,128)(2,1)S(1)}, bf16[352,1024]{1,0:T(8,128)(2,1)S(1)}, u32[]{:S(2)}, u32[]{:S(2)}) collective-permute-start(bf16[352,1024]{1,0:T(8,128)(2,1)S(1)} %pad_maximum_fusion.refs_0_), channel_id=1, source_target_pairs={{0,24},{1,9},{2,26},{3,11},{4,28},{5,13},{6,30},{7,15},{8,16},{9,1... | collective-permute-start | bytes 2162696 | tf_op jit(solution)/shard_map/ppermute | solution.py:91
  31.5 35.0 %copy-start.2 = (bf16[320,1024]{1,0:T(8,128)(2,1)}, bf16[320,1024]{1,0:T(8,128)(2,1)S(1)}, u32[]{:S(2)}) copy-start(bf16[320,1024]{1,0:T(8,128)(2,1)S(1)} %pad_maximum_fusion.2.refs_4_.refs_8_) | copy-start | bytes 1966084
  31.5 12.0 %collective-permute-start.10 = (bf16[320,1024]{1,0:T(8,128)(2,1)S(1)}, bf16[320,1024]{1,0:T(8,128)(2,1)}, u32[]{:S(2)}, u32[]{:S(2)}) collective-permute-start(bf16[320,1024]{1,0:T(8,128)(2,1)S(1)} %pad_maximum_fusion.2.refs_4_.refs_8_), channel_id=1, source_target_pairs={{0,96},{1,33},{2,98},{3,35},{4,100},{5,37},{6,102},{7,39},{8,104},... | collective-permute-start | bytes 1966088 | tf_op jit(solution)/shard_map/ppermute | solution.py:91
  33.6 15.2 %collective-permute-start.9 = (bf16[320,1024]{1,0:T(8,128)(2,1)S(1)}, bf16[320,1024]{1,0:T(8,128)(2,1)}, u32[]{:S(2)}, u32[]{:S(2)}) collective-permute-start(bf16[320,1024]{1,0:T(8,128)(2,1)S(1)} %pad_maximum_fusion.2.refs_4_.refs_8_), channel_id=1, source_target_pairs={{0,24},{1,9},{2,26},{3,11},{4,28},{5,13},{6,30},{7,15},{8,16},{9,1... | collective-permute-start | bytes 1966088 | tf_op jit(solution)/shard_map/ppermute | solution.py:91
  35.6 56.2 %copy-start.5 = (s32[1,192]{1,0:T(1,128)}, s32[1,192]{1,0:T(1,128)S(1)}, u32[]{:S(2)}) copy-start(s32[1,192]{1,0:T(1,128)S(1)} %constant_dynamic-slice_fusion) | copy-start | bytes 2308
  35.6 39.7 %collective-permute-start.5 = (bf16[352,1024]{1,0:T(8,128)(2,1)S(1)}, bf16[352,1024]{1,0:T(8,128)(2,1)}, u32[]{:S(2)}, u32[]{:S(2)}) collective-permute-start(bf16[352,1024]{1,0:T(8,128)(2,1)S(1)} %pad_maximum_fusion.1.refs_2_.refs_4_), channel_id=1, source_target_pairs={{0,96},{1,33},{2,98},{3,35},{4,100},{5,37},{6,102},{7,39},{8,104},... | collective-permute-start | bytes 2162696 | tf_op jit(solution)/shard_map/ppermute | solution.py:91
  43.5 31.7 %collective-permute-start.1 = (bf16[352,1024]{1,0:T(8,128)(2,1)S(1)}, bf16[352,1024]{1,0:T(8,128)(2,1)}, u32[]{:S(2)}, u32[]{:S(2)}) collective-permute-start(bf16[352,1024]{1,0:T(8,128)(2,1)S(1)} %pad_maximum_fusion.refs_0_), channel_id=1, source_target_pairs={{0,6},{1,3},{2,4},{3,1},{4,2},{5,7},{6,0},{7,5},{8,14},{9,11},{10,... | collective-permute-start | bytes 2162696 | tf_op jit(solution)/shard_map/ppermute | solution.py:91
  48.8 26.5 %collective-permute-start.11 = (bf16[320,1024]{1,0:T(8,128)(2,1)}, bf16[320,1024]{1,0:T(8,128)(2,1)}, u32[]{:S(2)}, u32[]{:S(2)}) collective-permute-start(bf16[320,1024]{1,0:T(8,128)(2,1)} %collective-permute-done.10.refs_5_.refs_9_), channel_id=1, source_target_pairs={{0,24},{1,9},{2,26},{3,11},{4,28},{5,13},{6,30},{7,15},{8,16},{9,1... | collective-permute-start | bytes 1966088 | tf_op jit(solution)/shard_map/ppermute | solution.py:91
  51.1 15.4 %copy-start.3 = (bf16[352,1024]{1,0:T(8,128)(2,1)}, bf16[352,1024]{1,0:T(8,128)(2,1)S(1)}, u32[]{:S(2)}) copy-start(bf16[352,1024]{1,0:T(8,128)(2,1)S(1)} %collective-permute-done.6.refs_3_.refs_5_) | copy-start | bytes 2162692
  51.1 24.2 %collective-permute-start.7 = (bf16[352,1024]{1,0:T(8,128)(2,1)S(1)}, bf16[352,1024]{1,0:T(8,128)(2,1)}, u32[]{:S(2)}, u32[]{:S(2)}) collective-permute-start(bf16[352,1024]{1,0:T(8,128)(2,1)S(1)} %collective-permute-done.6.refs_3_.refs_5_), channel_id=1, source_target_pairs={{0,96},{1,33},{2,98},{3,35},{4,100},{5,37},{6,102},{7,39},{8,104},... | collective-permute-start | bytes 2162696 | tf_op jit(solution)/shard_map/ppermute | solution.py:91
  53.1 13.4 %copy-start.4 = (bf16[352,1024]{1,0:T(8,128)(2,1)}, bf16[352,1024]{1,0:T(8,128)(2,1)S(1)}, u32[]{:S(2)}) copy-start(bf16[352,1024]{1,0:T(8,128)(2,1)S(1)} %collective-permute-done.2.refs_1_) | copy-start | bytes 2162692
  53.1 22.2 %collective-permute-start.3 = (bf16[352,1024]{1,0:T(8,128)(2,1)S(1)}, bf16[352,1024]{1,0:T(8,128)(2,1)}, u32[]{:S(2)}, u32[]{:S(2)}) collective-permute-start(bf16[352,1024]{1,0:T(8,128)(2,1)S(1)} %collective-permute-done.2.refs_1_), channel_id=1, source_target_pairs={{0,6},{1,3},{2,4},{3,1},{4,2},{5,7},{6,0},{7,5},{8,14},{9,11},{10,... | collective-permute-start | bytes 2162696 | tf_op jit(solution)/shard_map/ppermute | solution.py:91
  54.5 12.0 %copy-start.8 = (s32[1024]{0:T(1024)S(1)}, s32[1024]{0:T(1024)}, u32[]{:S(2)}) copy-start(s32[1024]{0:T(1024)} %param.7) | copy-start | bytes 12292
  66.5 8.7 %copy-start.6 = (s32[1024]{0:T(1024)}, s32[1024]{0:T(1024)S(1)}, u32[]{:S(2)}) copy-start(s32[1024]{0:T(1024)S(1)} %broadcast_subtract_fusion) | copy-start | bytes 12292
  86.1 17.4 %all-to-all-start.1 = ((f32[64,16,128]{2,1,0:T(8,128)}), f32[64,16,128]{2,1,0:T(8,128)}, u32[]{:S(2)}, u32[]{:S(2)}) async-start(f32[64,16,128]{2,1,0:T(8,128)} %get-tuple-element.14), calls=%async_computation.1 | async-start | bytes 1048576 | tf_op jit(solution)/shard_map/all_to_all | solution.py:532
  114.9 20.5 %collective-permute-start.15 = (bf16[4,176,1024]{2,1,0:T(8,128)(2,1)}, bf16[4,176,1024]{2,1,0:T(8,128)(2,1)}, u32[]{:S(2)}, u32[]{:S(2)}) collective-permute-start(bf16[4,176,1024]{2,1,0:T(8,128)(2,1)} %get-tuple-element.21), channel_id=1, source_target_pairs={{0,96},{1,33},{2,98},{3,35},{4,100},{5,37},{6,102},{7,39},{8,104},... | collective-permute-start | bytes 4325384 | tf_op jit(solution)/shard_map/ppermute | solution.py:167
  116.8 22.4 %collective-permute-start.12 = (bf16[4,176,1024]{2,1,0:T(8,128)(2,1)}, bf16[4,176,1024]{2,1,0:T(8,128)(2,1)}, u32[]{:S(2)}, u32[]{:S(2)}) collective-permute-start(bf16[4,176,1024]{2,1,0:T(8,128)(2,1)} %get-tuple-element.19), channel_id=1, source_target_pairs={{0,6},{1,3},{2,4},{3,1},{4,2},{5,7},{6,0},{7,5},{8,14},{9,11},{10,... | collective-permute-start | bytes 4325384 | tf_op jit(solution)/shard_map/ppermute | solution.py:167
  119.5 31.9 %collective-permute-start.18 = (bf16[4,160,1024]{2,1,0:T(8,128)(2,1)}, bf16[4,160,1024]{2,1,0:T(8,128)(2,1)}, u32[]{:S(2)}, u32[]{:S(2)}) collective-permute-start(bf16[4,160,1024]{2,1,0:T(8,128)(2,1)} %get-tuple-element.23), channel_id=1, source_target_pairs={{0,24},{1,9},{2,26},{3,11},{4,28},{5,13},{6,30},{7,15},{8,16},{9,1... | collective-permute-start | bytes 3932168 | tf_op jit(solution)/shard_map/ppermute | solution.py:167
  122.2 59.4 %collective-permute-start.21 = (bf16[1024,1024]{1,0:T(8,128)(2,1)}, bf16[1024,1024]{1,0:T(8,128)(2,1)}, u32[]{:S(2)}, u32[]{:S(2)}) collective-permute-start(bf16[1024,1024]{1,0:T(8,128)(2,1)} %get-tuple-element.17.grad), channel_id=1, source_target_pairs={{0,1},{1,0},{2,3},{3,2},{4,5},{5,4},{6,7},{7,6},{8,9},{9,8},{10,11... | collective-permute-start | bytes 6291464 | tf_op jit(solution)/shard_map/ppermute | solution.py:545
  137.6 18.3 %collective-permute-start.16 = (bf16[2,176,1024]{2,1,0:T(8,128)(2,1)}, bf16[2,176,1024]{2,1,0:T(8,128)(2,1)}, u32[]{:S(2)}, u32[]{:S(2)}) collective-permute-start(bf16[2,176,1024]{2,1,0:T(8,128)(2,1)} %shard_map.92), channel_id=1, source_target_pairs={{0,6},{1,3},{2,4},{3,1},{4,2},{5,7},{6,0},{7,5},{8,14},{9,11},{10,... | collective-permute-start | bytes 2162696 | tf_op jit(solution)/shard_map/ppermute | solution.py:167
  141.3 16.5 %collective-permute-start.13 = (bf16[2,176,1024]{2,1,0:T(8,128)(2,1)}, bf16[2,176,1024]{2,1,0:T(8,128)(2,1)}, u32[]{:S(2)}, u32[]{:S(2)}) collective-permute-start(bf16[2,176,1024]{2,1,0:T(8,128)(2,1)} %shard_map.90), channel_id=1, source_target_pairs={{0,24},{1,9},{2,26},{3,11},{4,28},{5,13},{6,30},{7,15},{8,16},{9,1... | collective-permute-start | bytes 2162696 | tf_op jit(solution)/shard_map/ppermute | solution.py:167
  151.3 28.0 %collective-permute-start.22 = (f32[64,4096]{1,0:T(8,128)}, f32[64,4096]{1,0:T(8,128)}, u32[]{:S(2)}, u32[]{:S(2)}) collective-permute-start(f32[64,4096]{1,0:T(8,128)} %shard_map.99), channel_id=1, source_target_pairs={{0,1},{1,0},{2,3},{3,2},{4,5},{5,4},{6,7},{7,6},{8,9},{9,8},{10,11... | collective-permute-start | bytes 3145736 | tf_op jit(solution)/shard_map/ppermute | solution.py:546
  152.8 11.9 %collective-permute-start.19 = (bf16[2,160,1024]{2,1,0:T(8,128)(2,1)S(1)}, bf16[2,160,1024]{2,1,0:T(8,128)(2,1)S(1)}, u32[]{:S(2)}, u32[]{:S(2)}) collective-permute-start(bf16[2,160,1024]{2,1,0:T(8,128)(2,1)S(1)} %shard_map.94), channel_id=1, source_target_pairs={{0,96},{1,33},{2,98},{3,35},{4,100},{5,37},{6,102},{7,39},{8,104},... | collective-permute-start | bytes 1966088 | tf_op jit(solution)/shard_map/ppermute | solution.py:167
  157.2 17.0 %collective-permute-start.17 = (bf16[1,176,1024]{2,1,0:T(8,128)(2,1)S(1)}, bf16[1,176,1024]{2,1,0:T(8,128)(2,1)S(1)}, u32[]{:S(2)}, u32[]{:S(2)}) collective-permute-start(bf16[1,176,1024]{2,1,0:T(8,128)(2,1)S(1)} %shard_map.93), channel_id=1, source_target_pairs={{0,24},{1,9},{2,26},{3,11},{4,28},{5,13},{6,30},{7,15},{8,16},{9,1... | collective-permute-start | bytes 1081352 | tf_op jit(solution)/shard_map/ppermute | solution.py:167
  159.1 15.1 %collective-permute-start.14 = (bf16[1,176,1024]{2,1,0:T(8,128)(2,1)S(1)}, bf16[1,176,1024]{2,1,0:T(8,128)(2,1)S(1)}, u32[]{:S(2)}, u32[]{:S(2)}) collective-permute-start(bf16[1,176,1024]{2,1,0:T(8,128)(2,1)S(1)} %shard_map.91), channel_id=1, source_target_pairs={{0,96},{1,33},{2,98},{3,35},{4,100},{5,37},{6,102},{7,39},{8,104},... | collective-permute-start | bytes 1081352 | tf_op jit(solution)/shard_map/ppermute | solution.py:167
  165.9 8.4 %collective-permute-start.20 = (bf16[1,160,1024]{2,1,0:T(8,128)(2,1)S(1)}, bf16[1,160,1024]{2,1,0:T(8,128)(2,1)S(1)}, u32[]{:S(2)}, u32[]{:S(2)}) collective-permute-start(bf16[1,160,1024]{2,1,0:T(8,128)(2,1)S(1)} %shard_map.95), channel_id=1, source_target_pairs={{0,6},{1,3},{2,4},{3,1},{4,2},{5,7},{6,0},{7,5},{8,14},{9,11},{10,... | collective-permute-start | bytes 983048 | tf_op jit(solution)/shard_map/ppermute | solution.py:167
  175.6 3.7 %copy-start.7 = (f32[64,4096]{1,0:T(8,128)S(1)}, f32[64,4096]{1,0:T(8,128)}, u32[]{:S(2)}) copy-start(f32[64,4096]{1,0:T(8,128)} %shard_map.99) | copy-start | bytes 3145732
  175.6 14.9 %all-to-all-start.2 = ((bf16[8,64,1024]{2,1,0:T(8,128)(2,1)}), bf16[8,64,1024]{2,1,0:T(8,128)(2,1)S(1)}, u32[]{:S(2)}, u32[]{:S(2)}) async-start(bf16[8,64,1024]{2,1,0:T(8,128)(2,1)} %bitcast.6), calls=%async_computation.2 | async-start | bytes 2097152 | tf_op jit(solution)/shard_map/all_to_all | solution.py:82
  181.6 3.3 %copy-start.9 = (bf16[1024,1024]{1,0:T(8,128)(2,1)S(1)}, bf16[1024,1024]{1,0:T(8,128)(2,1)}, u32[]{:S(2)}) copy-start(bf16[1024,1024]{1,0:T(8,128)(2,1)} %get-tuple-element.17.grad) | copy-start | bytes 6291460
